TPU v7x, 512 devices: a whole 4x8x8 slice. The times are simulated.
512 devices in a mesh: scen: 64 (over y, z), fac: 8 (over x, core).
Axes of the slice: x: 4, y: 8, z: 8, core: 2. Of those that a mesh axis runs over, the one named last changes fastest.
Arguments:
- scenarios: bfloat16 [4096, 8192], P(('scen', 'fac')), may hold values from -40 to 40
Outputs:
- shrunk: float32 [8192, 8192], P('scen', 'fac')
- shrinkage: float32 [], replicated
- col_mean: float32 [8192], P('fac')
All inputs are finite; a program needn't handle non-finite values.
Results may differ from a plain program's by a relative error of at most 0.0008.
Values may be sent and summed in bfloat16 or wider, within the bound.
No kernel may reach another device: no remote copies, remote signals or barrier semaphores. Data moves between devices by JAX's collectives and lax.ppermute only.
A program may use at most 64 MiB of HBM per device.

v0:
```python
import functools

import jax
import jax.numpy as jnp
from jax import lax
from jax.sharding import Mesh
from jax.sharding import PartitionSpec as P

SCEN = ("scen_0", "scen_1")
FAC = ("fac_0", "fac_1")
SCEN_FAC = ("scen_0", "scen_1", "fac_0", "fac_1")


def by_axis(shard, axes):
    return functools.reduce(lax.psum, axes, shard)


def joined_along(parts, dim):
    parts = jnp.moveaxis(parts, 0, dim)
    shape = parts.shape
    return parts.reshape(*shape[:dim], shape[dim] * shape[dim + 1], *shape[dim + 2 :])


def copy_for_each(shard, axis):
    copies = jnp.broadcast_to(shard, (lax.axis_size(axis), *shard.shape))
    return lax.all_to_all(copies, axis, split_axis=0, concat_axis=0, tiled=True)


def gather_directly(shard, axis, dim):
    return joined_along(copy_for_each(shard, axis), dim)


def on_device(scenarios):
    row_count = scenarios.shape[0]
    factors = scenarios.shape[1]
    scen_size = lax.axis_size(SCEN)
    fac_size = lax.axis_size(FAC)
    total_rows = row_count * scen_size * fac_size
    group_width = factors // scen_size
    block_width = factors // fac_size
    owner_idx = lax.axis_index(SCEN)
    block_idx = lax.axis_index(FAC)
    col_total = by_axis(jnp.sum(scenarios.astype(jnp.float32), axis=0), SCEN_FAC)
    col_mean = col_total / total_rows
    centered = (scenarios.astype(jnp.float32) - col_mean).astype(jnp.bfloat16)
    as_float = centered.astype(jnp.float32)
    squared = jnp.sum(as_float * as_float, axis=1)
    trace_part = jnp.sum(squared)
    fourth_part = jnp.sum(squared * squared)
    trace_total, fourth_total = (by_axis(trace_part, SCEN_FAC), by_axis(fourth_part, SCEN_FAC))
    contract = (((0,), (0,)), ((), ()))
    local_rows = gather_directly(centered, FAC, 0)
    narrow_all = lax.all_to_all(local_rows, SCEN, split_axis=1, concat_axis=0, tiled=True)
    wide_cols = lax.dynamic_slice_in_dim(local_rows, block_idx * block_width, block_width, 1)
    summed = lax.dot_general(
        narrow_all,
        lax.all_gather(wide_cols, SCEN, axis=0, tiled=True),
        contract,
        preferred_element_type=jnp.float32,
    )
    covariance = summed / total_rows
    row_index = owner_idx * group_width + lax.broadcasted_iota(
        jnp.int32, (group_width, block_width), 0
    )
    col_index = block_idx * block_width + lax.broadcasted_iota(
        jnp.int32, (group_width, block_width), 1
    )
    diag_mask = (row_index == col_index).astype(jnp.float32)
    mu_scale = trace_total / (total_rows * factors)
    distance = covariance - mu_scale * diag_mask
    frob_sum = by_axis(jnp.sum(distance * distance), SCEN_FAC)
    spread = frob_sum / factors
    norm_sq = factors * (spread + mu_scale * mu_scale)
    beta_value = (fourth_total / total_rows - norm_sq) / (factors * total_rows)
    shrinkage = beta_value / spread
    shrunk = (1.0 - shrinkage) * covariance + shrinkage * mu_scale * diag_mask
    mean_block = lax.dynamic_slice_in_dim(col_mean, block_idx * block_width, block_width, 0)
    return (shrunk, shrinkage, mean_block)


def solution(mesh):
    finer = Mesh(mesh.devices.reshape(8, 8, 4, 2), ("scen_0", "scen_1", "fac_0", "fac_1"))
    return jax.shard_map(
        on_device,
        mesh=finer,
        in_specs=(P(SCEN_FAC, None),),
        out_specs=(P(SCEN, FAC), P(), P(FAC)),
        check_vma=False,
    )
```

profile of v0, /device:TPU:1, one launch (start us, length us, event | category | flops | bytes accessed | tf_op | source)
XLA Modules:
  0.0 289.3 jit_solution(17670801236604795033)
XLA Ops:
  7.2 1.0 convert_reduce_fusion
  8.2 24.2 %psum.112 = f32[8192]{0:T(1024)S(1)} all-reduce(f32[8192]{0:T(1024)S(1)} %convert_reduce_fusion), channel_id=1, replica_groups=mesh['scen_0'=8,'scen_1'=8,'fac_0'=4,'fac_1'=2] {'scen_0'}, use_global_device_ids=true, to_apply=%region_1.0 | all-reduce | flops 8192 | bytes 65536 | tf_op jit(solution)/shard_map/psum | solution.py:15
  32.3 28.7 %psum.113 = f32[8192]{0:T(1024)S(1)} all-reduce(f32[8192]{0:T(1024)S(1)} %psum.112), channel_id=1, replica_groups=mesh['scen_0'=8,'scen_1'=8,'fac_0'=4,'fac_1'=2] {'scen_1'}, use_global_device_ids=true, to_apply=%region_2.0 | all-reduce | flops 8192 | bytes 65536 | tf_op jit(solution)/shard_map/psum | solution.py:15
  61.1 13.3 %psum.114 = f32[8192]{0:T(1024)S(1)} all-reduce(f32[8192]{0:T(1024)S(1)} %psum.113), channel_id=1, replica_groups=mesh['scen_0'=8,'scen_1'=8,'fac_0'=4,'fac_1'=2] {'fac_0'}, use_global_device_ids=true, to_apply=%region_3.0 | all-reduce | flops 8192 | bytes 65536 | tf_op jit(solution)/shard_map/psum | solution.py:15
  74.4 21.9 %psum.115 = f32[8192]{0:T(1024)S(1)} all-reduce(f32[8192]{0:T(1024)S(1)} %psum.114), channel_id=1, replica_groups=mesh['scen_0'=8,'scen_1'=8,'fac_0'=4,'fac_1'=2] {'fac_1'}, use_global_device_ids=true, to_apply=%region_4.0 | all-reduce | flops 8192 | bytes 65536 | tf_op jit(solution)/shard_map/psum | solution.py:15
  96.3 1.6 fusion.5
  97.9 1.1 broadcast_in_dim.4
  99.0 3.6 %all-to-all-start = ((bf16[8,8,8192]{2,1,0:T(8,128)(2,1)}), bf16[8,8,8192]{2,1,0:T(8,128)(2,1)S(1)}, u32[]{:S(2)}, u32[]{:S(2)}) async-start(bf16[8,8,8192]{2,1,0:T(8,128)(2,1)} %broadcast_in_dim.4), calls=%async_computation | async-start | bytes 2097152 | tf_op jit(solution)/shard_map/all_to_all | solution.py:26
  102.6 0.0 all-gather.2.cloned.1.call-start
  102.6 15.0 %all-to-all-done = bf16[8,8,8192]{2,1,0:T(8,128)(2,1)S(1)} async-done(((bf16[8,8,8192]{2,1,0:T(8,128)(2,1)}), bf16[8,8,8192]{2,1,0:T(8,128)(2,1)S(1)}, u32[]{:S(2)}, u32[]{:S(2)}) %all-to-all-start) | async-done | bytes 1048608 | tf_op jit(solution)/shard_map/all_to_all | solution.py:26
  117.6 0.7 constant_dynamic-slice_fusion
  118.2 0.0 all-gather.2.cloned.1.call-update
  118.3 0.3 copy.6
  118.5 1.8 copy.5
  120.3 5.9 %all-to-all-start.1 = ((bf16[64,64,128]{2,0,1:T(8,128)(2,1)}), bf16[64,64,128]{2,0,1:T(8,128)(2,1)S(1)}, u32[]{:S(2)}, u32[]{:S(2)}) async-start(bf16[64,64,128]{2,0,1:T(8,128)(2,1)} %copy.5), calls=%async_computation.1 | async-start | bytes 2097152 | tf_op jit(solution)/shard_map/all_to_all | solution.py:53
  126.2 35.0 %psum.120 = f32[]{:T(128)} all-reduce(f32[]{:T(128)} %get-tuple-element.3), channel_id=1, replica_groups=mesh['scen_0'=8,'scen_1'=8,'fac_0'=4,'fac_1'=2] {'scen_0'}, use_global_device_ids=true, to_apply=%region_12.0 | all-reduce | flops 1 | bytes 8 | tf_op jit(solution)/shard_map/psum | solution.py:15
  161.2 13.5 %psum.121 = f32[]{:T(128)} all-reduce(f32[]{:T(128)} %psum.120), channel_id=1, replica_groups=mesh['scen_0'=8,'scen_1'=8,'fac_0'=4,'fac_1'=2] {'scen_1'}, use_global_device_ids=true, to_apply=%region_13.0 | all-reduce | flops 1 | bytes 8 | tf_op jit(solution)/shard_map/psum | solution.py:15
  174.7 7.3 %psum.122 = f32[]{:T(128)} all-reduce(f32[]{:T(128)} %psum.121), channel_id=1, replica_groups=mesh['scen_0'=8,'scen_1'=8,'fac_0'=4,'fac_1'=2] {'fac_0'}, use_global_device_ids=true, to_apply=%region_14.0 | all-reduce | flops 1 | bytes 8 | tf_op jit(solution)/shard_map/psum | solution.py:15
  182.0 12.5 %psum.123 = f32[]{:T(128)} all-reduce(f32[]{:T(128)} %psum.122), channel_id=1, replica_groups=mesh['scen_0'=8,'scen_1'=8,'fac_0'=4,'fac_1'=2] {'fac_1'}, use_global_device_ids=true, to_apply=%region_15.0 | all-reduce | flops 1 | bytes 8 | tf_op jit(solution)/shard_map/psum | solution.py:15
  194.5 0.6 dynamic_slice.7
  197.1 0.7 multiply_reduce_fusion
  197.8 0.0 all-to-all-done.1
  197.8 27.5 %all-gather.2.cloned.1.call-done = bf16[4096,1024]{1,0:T(8,128)(2,1)} async-done(((bf16[64,1024]{1,0:T(8,128)(2,1)}), bf16[4096,1024]{1,0:T(8,128)(2,1)}) %all-gather.2.cloned.1.call-update) | async-done | bytes 8388624 | tf_op jit(solution)/shard_map/all_gather | solution.py:57
  225.3 5.3 %fusion.2 = (f32[]{:T(128)}, f32[128,1024]{1,0:T(8,128)S(1)}) fusion(f32[]{:T(128)S(6)} %div.32, s32[1024]{0:T(1024)S(1)} %iota_add_fusion, s32[128]{0:T(128)S(1)} %iota_add_fusion.1, bf16[4096,128]{1,0:T(8,128)(2,1)S(1)} %bitcast.9, bf16[4096,1024]{1,0:T(8,128)(2,1)} %all-gather.2.cloned.1.call-done), kind=kOutput, calls=%fused_computation.4 | convolution fusion | flops 1074528256 | bytes 9966088 | tf_op jit(solution)/shard_map/dot_general | solution.py:55
  230.6 13.8 %all-reduce.1 = (f32[]{:T(128)}, f32[]{:T(128)}) all-reduce(f32[]{:T(128)} %multiply_reduce_fusion, f32[]{:T(128)} %get-tuple-element.14), channel_id=1, replica_groups=mesh['scen_0'=8,'scen_1'=8,'fac_0'=4,'fac_1'=2] {'scen_0'}, use_global_device_ids=true, to_apply=%region_7.0 | all-reduce | flops 2 | bytes 16 | tf_op jit(solution)/shard_map/psum | solution.py:15
  244.4 12.8 %all-reduce = (f32[]{:T(128)}, f32[]{:T(128)}) all-reduce(f32[]{:T(128)} %get-tuple-element.7, f32[]{:T(128)} %get-tuple-element.8), channel_id=1, replica_groups=mesh['scen_0'=8,'scen_1'=8,'fac_0'=4,'fac_1'=2] {'scen_1'}, use_global_device_ids=true, to_apply=%region_8.0 | all-reduce | flops 2 | bytes 16 | tf_op jit(solution)/shard_map/psum | solution.py:15
  257.2 9.0 %all-reduce.2 = (f32[]{:T(128)}, f32[]{:T(128)}) all-reduce(f32[]{:T(128)} %get-tuple-element.5, f32[]{:T(128)} %get-tuple-element.6), channel_id=1, replica_groups=mesh['scen_0'=8,'scen_1'=8,'fac_0'=4,'fac_1'=2] {'fac_0'}, use_global_device_ids=true, to_apply=%region_9.0 | all-reduce | flops 2 | bytes 16 | tf_op jit(solution)/shard_map/psum | solution.py:15
  266.2 12.8 %all-reduce.3 = (f32[]{:T(128)}, f32[]{:T(128)}) all-reduce(f32[]{:T(128)} %get-tuple-element.9, f32[]{:T(128)} %get-tuple-element.10), channel_id=1, replica_groups=mesh['scen_0'=8,'scen_1'=8,'fac_0'=4,'fac_1'=2] {'fac_1'}, use_global_device_ids=true, to_apply=%region_10.0 | all-reduce | flops 2 | bytes 16 | tf_op jit(solution)/shard_map/psum | solution.py:15
  280.4 0.9 fusion.3
  (3 shorter events, 0.0 us)
Async XLA Ops:
  99.0 18.6 %all-to-all-start = ((bf16[8,8,8192]{2,1,0:T(8,128)(2,1)}), bf16[8,8,8192]{2,1,0:T(8,128)(2,1)S(1)}, u32[]{:S(2)}, u32[]{:S(2)}) async-start(bf16[8,8,8192]{2,1,0:T(8,128)(2,1)} %broadcast_in_dim.4), calls=%async_computation | async-start | bytes 2097152 | tf_op jit(solution)/shard_map/all_to_all | solution.py:26
  102.6 122.7 %all-gather.2.cloned.1.call-start = ((), (), s32[]{:S(2)}) async-start(), calls=%async_computation.2 | async-start | bytes 8519680 | tf_op jit(solution)/shard_map/all_gather | solution.py:57
  120.3 77.5 %all-to-all-start.1 = ((bf16[64,64,128]{2,0,1:T(8,128)(2,1)}), bf16[64,64,128]{2,0,1:T(8,128)(2,1)S(1)}, u32[]{:S(2)}, u32[]{:S(2)}) async-start(bf16[64,64,128]{2,0,1:T(8,128)(2,1)} %copy.5), calls=%async_computation.1 | async-start | bytes 2097152 | tf_op jit(solution)/shard_map/all_to_all | solution.py:53
Sparse Core Ops, SparseCore 0:
  118.4 106.8 all-gather.1
where the time goes:
time: 290 us; the launch traced here: 289 us
  blocking collectives  205 us (71%)
  waiting for transfers between devices  42.5 us (15%)
  between operations  18.5 us (6%)
  starting transfers between devices  9.55 us (3%)
  matrix products  5.33 us (2%)
  local copies, waits for them, and re-layouts  4.33 us (1%)
  other arithmetic  4.18 us (1%)
    psum x12, blocking collectives, by_axis(): return functools.reduce(lax.psum, axes, shard)  205 us
    all_gather x1, waiting for transfers between devices, on_device(): lax.all_gather(wide_cols, SCEN, axis=0, tiled=True)  27.5 us
    all_to_all x1, waiting for transfers between devices, copy_for_each(): return lax.all_to_all(copies, axis, split_axis=0, concat_axis=0, tiled=True)  15 us
    all_to_all x1, starting transfers between devices, on_device(): lax.all_to_all(local_rows, SCEN, split_axis=1, concat_axis=0, tiled=True)  5.92 us
  transfers between devices with their start and end apart: 3, of which 2 were waited for; matrix products, arithmetic and copies ran while one was open for 1% of the time, Pallas kernels for 0%

commit v1 on v0

v1 whole, which is shorter than its diff:
```python
import jax
import jax.numpy as jnp
from jax import lax
from jax.sharding import Mesh
from jax.sharding import PartitionSpec as P

PLANE = ("y", "z")
LINE = ("x", "c")
SLAB = ("z", "x", "c")
F32 = jnp.float32
BF16 = jnp.bfloat16
EXTRA = 8


def gather_small(row, axes):
    copies = jnp.broadcast_to(row[None], (lax.axis_size(axes), *row.shape))
    return lax.all_to_all(copies, axes, split_axis=0, concat_axis=0, tiled=True)


def partial_rows(left, right):
    return lax.dot_general(left, right, (((0,), (0,)), ((), ())), preferred_element_type=F32)


def on_device(scenarios):
    row_count, factors = scenarios.shape
    ny, nz, nx, nc = (lax.axis_size(axis) for axis in ("y", "z", "x", "c"))
    nf = nx * nc
    total_rows = row_count * ny * nz * nf
    block = factors // ny
    width = block // nf
    y_idx, z_idx, c_idx = lax.axis_index("y"), lax.axis_index("z"), lax.axis_index("c")
    f_idx = lax.axis_index(LINE)

    blocks = scenarios.reshape(row_count, ny, block).transpose(1, 0, 2)
    to_rows = jnp.broadcast_to(blocks[:, None], (ny, nz, row_count, block))
    to_cols = jnp.broadcast_to(blocks[None, :], (ny, nz, row_count, block))
    outgoing = jnp.stack((to_rows, to_cols), axis=2).reshape(ny * nz, 2, row_count, block)
    arrived = lax.all_to_all(outgoing, PLANE, split_axis=0, concat_axis=0, tiled=True)

    part_rows = row_count * ny * nz
    local_mean = jnp.sum(arrived.astype(F32), axis=(0, 2)) / part_rows
    centered = (arrived.astype(F32) - local_mean[None, :, None, :]).astype(BF16)
    left = centered[:, 0].reshape(part_rows, nx, nc, width)
    right = centered[:, 1].reshape(part_rows, block)

    mean_cols = jnp.broadcast_to(local_mean[1], (nx, block))
    mean_rows = local_mean[0].reshape(nx, nc, width)

    def extra_rows(core):
        rows = lax.dynamic_index_in_dim(mean_rows, core, 1, keepdims=False)
        rows = jnp.pad(rows, ((0, 0), (0, block - width)))
        slot = lax.broadcasted_iota(jnp.int32, (nx, EXTRA, block), 1)
        return jnp.where(
            slot == c_idx, mean_cols[:, None], jnp.where(slot == nc + c_idx, rows[:, None], 0.0)
        )

    def half(core):
        picked = lax.dynamic_index_in_dim(left, core, 2, keepdims=False)
        return jnp.concatenate((partial_rows(picked, right), extra_rows(core)), axis=1)

    swapped = lax.ppermute(half(1 - c_idx), "c", [(0, 1), (1, 0)])
    chip_sum = half(c_idx) + swapped
    pieces = lax.all_to_all(chip_sum, "x", split_axis=0, concat_axis=0, tiled=True)

    scatter = jnp.sum(pieces[:, :width], axis=0)
    means_c = pieces[:, width : width + nc].reshape(nf, block)
    means_r = pieces[:, width + nc : width + 2 * nc, :width].reshape(nf, width)
    mean_c = jnp.sum(means_c, axis=0) / nf
    mean_r = jnp.sum(means_r, axis=0) / nf
    off_c = means_c - mean_c
    off_r = means_r - mean_r
    between = jnp.sum(off_r[:, :, None] * off_c[:, None, :], axis=0)
    covariance = (scatter + part_rows * between) / total_rows

    packed = jnp.concatenate(
        (covariance, jnp.broadcast_to(mean_c, (EXTRA, block))), axis=0
    )
    pairs = [(z * nf + f, f * nz + z) for z in range(nz) for f in range(nf)]
    owned = lax.ppermute(packed, SLAB, pairs)

    mine = lax.dynamic_slice_in_dim(arrived, y_idx * nz, nz, 0)[:, 1]
    mine = (mine.astype(F32) - mean_c).astype(BF16).astype(F32)
    norms = jnp.sum(mine * mine, axis=2).reshape(nz * row_count)

    row_at = f_idx * width + lax.broadcasted_iota(jnp.int32, (width, block), 0)
    col_at = lax.broadcasted_iota(jnp.int32, (width, block), 1)
    on_diag = row_at == col_at
    holds_diag = (y_idx == z_idx).astype(F32)
    diag_here = on_diag & (y_idx == z_idx)
    off_squares = jnp.sum(jnp.where(diag_here, 0.0, covariance * covariance))
    diagonal = jnp.sum(jnp.where(on_diag, covariance, 0.0), axis=1)
    diag_mean = jnp.sum(diagonal) / width
    diag_dev = diagonal - diag_mean
    diag_m2 = jnp.sum(diag_dev * diag_dev)
    scalars = jnp.stack(
        (off_squares, holds_diag * diag_mean, holds_diag * diag_m2, holds_diag)
    )
    message = jnp.concatenate((norms, scalars))
    message = jnp.pad(message, (0, 128 - message.shape[0]))[None]

    seen = gather_small(message, SLAB).reshape(nz, nf, 128)
    count = nz * row_count
    squared = jnp.sum(seen[:, :, :count], axis=0)
    off_part = jnp.sum(seen[:, :, count])
    means, m2s, flags = seen[:, :, count + 1], seen[:, :, count + 2], seen[:, :, count + 3]
    block_mean = jnp.sum(means) / nf
    apart = flags * (means - block_mean)
    block_m2 = jnp.sum(m2s) + width * jnp.sum(apart * apart)
    second = jnp.stack(
        (jnp.sum(squared), jnp.sum(squared * squared), off_part, block_mean, block_m2)
    )
    second = jnp.pad(second, (0, 128 - second.shape[0]))[None]
    totals = gather_small(second, "y").reshape(ny, 128)
    trace_total = jnp.sum(totals[:, 0])
    fourth_total = jnp.sum(totals[:, 1])
    off_total = jnp.sum(totals[:, 2])
    mu_scale = trace_total / (total_rows * factors)
    from_mu = totals[:, 3] - mu_scale
    diag_total = jnp.sum(totals[:, 4]) + block * jnp.sum(from_mu * from_mu)
    spread = (off_total + diag_total) / factors
    norm_sq = factors * (spread + mu_scale * mu_scale)
    beta_value = (fourth_total / total_rows - norm_sq) / (factors * total_rows)
    shrinkage = beta_value / spread

    own_row = z_idx * width + lax.broadcasted_iota(jnp.int32, (width, block), 0)
    own_diag = ((own_row == col_at) & (y_idx == f_idx)).astype(F32)
    shrunk = (1.0 - shrinkage) * owned[:width] + shrinkage * mu_scale * own_diag
    return (shrunk, shrinkage, owned[width])


def solution(mesh):
    finer = Mesh(mesh.devices.reshape(8, 8, 4, 2), ("y", "z", "x", "c"))
    return jax.shard_map(
        on_device,
        mesh=finer,
        in_specs=(P(("y", "z", "x", "c"), None),),
        out_specs=(P(("y", "z"), ("x", "c")), P(), P(("x", "c"))),
        check_vma=False,
    )
```

time: 290 us -> 194 us (0.67)
  the two profiles are of different devices: /device:TPU:1 before, /device:TPU:31 now
where the time goes in v1:
time: 194 us; the launch traced here: 193 us
  waiting for transfers between devices  100 us (52%)
  starting transfers between devices  42.1 us (22%)
  local copies, waits for them, and re-layouts  19.4 us (10%)
  other arithmetic  18 us (9%)
  between operations  9.89 us (5%)
  matrix products  4.03 us (2%)
    all_to_all x1, waiting for transfers between devices, on_device(): lax.all_to_all(outgoing, PLANE, split_axis=0, concat_axis=0, tiled=True)  54 us
    all_to_all x1, waiting for transfers between devices, on_device(): lax.all_to_all(chip_sum, 'x', split_axis=0, concat_axis=0, tiled=True)  25.9 us
    all_to_all x1, starting transfers between devices, on_device(): lax.all_to_all(outgoing, PLANE, split_axis=0, concat_axis=0, tiled=True)  15.8 us
    ppermute x1, waiting for transfers between devices, on_device(): owned = lax.ppermute(packed, SLAB, pairs)  13.8 us
    all_to_all x2, starting transfers between devices, gather_small(): return lax.all_to_all(copies, axes, split_axis=0, concat_axis=0, tiled=True)  13.6 us
    all_to_all x2, waiting for transfers between devices, gather_small(): return lax.all_to_all(copies, axes, split_axis=0, concat_axis=0, tiled=True)  6.45 us
    unnamed x8, local copies, waits for them, and re-layouts  6.2 us
    ppermute x1, starting transfers between devices, on_device(): owned = lax.ppermute(packed, SLAB, pairs)  4.84 us
  transfers between devices with their start and end apart: 6, of which 5 were waited for; matrix products, arithmetic and copies ran while one was open for 6% of the time, Pallas kernels for 0%

profile of v1, /device:TPU:31, one launch (start us, length us, event | category | flops | bytes accessed | tf_op | source)
XLA Modules:
  0.0 193.5 jit_solution(11625009205004526603)
XLA Ops:
  0.6 1.0 stack_broadcast_in_dim.5
  1.7 1.0 stack_broadcast_in_dim.4
  2.7 1.5 pad_maximum_fusion.1
  4.2 15.8 %all-to-all-start = ((bf16[64,2,8,1024]{3,2,1,0:T(8,128)(2,1)}), bf16[64,2,8,1024]{3,2,1,0:T(8,128)(2,1)S(1)}, u32[]{:S(2)}, u32[]{:S(2)}) async-start(bf16[64,2,8,1024]{3,2,1,0:T(8,128)(2,1)} %bitcast.44), calls=%async_computation | async-start | bytes 4194304 | tf_op jit(solution)/shard_map/all_to_all | solution.py:38
  20.1 54.0 %all-to-all-done = bf16[64,2,8,1024]{3,2,1,0:T(8,128)(2,1)S(1)} async-done(((bf16[64,2,8,1024]{3,2,1,0:T(8,128)(2,1)}), bf16[64,2,8,1024]{3,2,1,0:T(8,128)(2,1)S(1)}, u32[]{:S(2)}, u32[]{:S(2)}) %all-to-all-start) | async-done | bytes 2097184 | tf_op jit(solution)/shard_map/all_to_all | solution.py:38
  75.1 1.3 copy-done
  76.4 1.1 slice.80
  77.5 1.8 reshape_squeeze.9
  79.3 3.5 %constant_dynamic-slice_fusion.3 = (bf16[512,4,1,128]{3,2,1,0:T(2,128)(2,1)}, bf16[512,4,1,128]{3,2,1,0:T(2,128)(2,1)}) fusion(bf16[512,4,2,128]{3,2,1,0:T(2,128)(2,1)S(1)} %reshape_squeeze.9, s32[]{:T(128)S(6)} %select_n.36, s32[]{:T(128)S(6)} %select_n.39), kind=kLoop, calls=%fused_computation.49 | loop fusion | bytes 2097160 | tf_op jit(solution)/shard_map/jit(dynamic_index_in_dim)/dynamic_slice | solution.py:58
  82.8 2.3 %copy.61 = bf16[512,4,1,128]{0,3,1,2:T(8,128)(2,1)S(1)} copy(bf16[512,4,1,128]{3,2,1,0:T(2,128)(2,1)} %get-tuple-element.21) | data formatting | bytes 1048576
  85.2 1.9 %fusion.1 = f32[4,128,1024]{2,1,0:T(8,128)S(1)} fusion(bf16[64,2,8,1024]{3,2,1,0:T(8,128)(2,1)} %copy-done, bf16[512,4,1,128]{0,3,1,2:T(8,128)(2,1)S(1)} %copy.61), kind=kOutput, calls=%fused_computation.9 | convolution fusion | flops 536870912 | bytes 3670016 | tf_op jit(solution)/shard_map/dot_general | solution.py:21
  87.2 1.5 pad_maximum_fusion
  88.7 3.2 %collective-permute-start = (f32[4,136,1024]{2,1,0:T(8,128)}, f32[4,136,1024]{2,1,0:T(8,128)}, u32[]{:S(2)}, u32[]{:S(2)}) collective-permute-start(f32[4,136,1024]{2,1,0:T(8,128)} %pad_maximum_fusion), channel_id=1, source_target_pairs={{0,1},{1,0},{2,3},{3,2},{4,5},{5,4},{6,7},{7,6},{8,9},{9,8},{10,11... | collective-permute-start | bytes 6684680 | tf_op jit(solution)/shard_map/ppermute | solution.py:61
  91.9 2.3 %copy.59 = bf16[512,4,1,128]{0,3,1,2:T(8,128)(2,1)} copy(bf16[512,4,1,128]{3,2,1,0:T(2,128)(2,1)S(1)} %copy-done.1) | data formatting | bytes 1048576
  94.2 2.1 %fusion.2 = f32[4,128,1024]{2,1,0:T(8,128)S(1)} fusion(bf16[64,2,8,1024]{3,2,1,0:T(8,128)(2,1)} %copy-done, bf16[512,4,1,128]{0,3,1,2:T(8,128)(2,1)} %copy.59), kind=kOutput, calls=%fused_computation.10 | convolution fusion | flops 536870912 | bytes 3670016 | tf_op jit(solution)/shard_map/dot_general | solution.py:21
  96.3 3.5 %maximum_add_fusion = f32[4,136,1024]{2,1,0:T(8,128)} fusion(f32[4,136,1024]{2,1,0:T(8,128)} %collective-permute-done, f32[4,8,1024]{2,1,0:T(8,128)S(1)} %get-tuple-element.26, f32[4,128,1024]{2,1,0:T(8,128)S(1)} %fusion.2), kind=kLoop, calls=%fused_computation.4 | loop fusion | flops 1114112 | bytes 6684672 | tf_op jit(solution)/shard_map/add | solution.py:62
  99.8 4.6 %all-to-all-start.1 = ((f32[4,136,1024]{2,1,0:T(8,128)}), f32[4,136,1024]{2,1,0:T(8,128)}, u32[]{:S(2)}, u32[]{:S(2)}) async-start(f32[4,136,1024]{2,1,0:T(8,128)} %maximum_add_fusion), calls=%async_computation.1 | async-start | bytes 4456448 | tf_op jit(solution)/shard_map/all_to_all | solution.py:63
  104.4 25.9 %all-to-all-done.1 = f32[4,136,1024]{2,1,0:T(8,128)} async-done(((f32[4,136,1024]{2,1,0:T(8,128)}), f32[4,136,1024]{2,1,0:T(8,128)}, u32[]{:S(2)}, u32[]{:S(2)}) %all-to-all-start.1) | async-done | bytes 2228256 | tf_op jit(solution)/shard_map/all_to_all | solution.py:63
  130.3 0.7 slice_reduce_fusion.9
  131.0 0.9 fusion.12
  132.6 1.8 slice_reduce_fusion
  134.4 0.9 fusion.9
  137.3 0.7 concatenate.14
  138.6 8.4 %all-to-all-start.2 = ((f32[64,1,128]{2,1,0:T(1,128)}), f32[64,1,128]{2,1,0:T(1,128)S(1)}, u32[]{:S(2)}, u32[]{:S(2)}) async-start(f32[64,1,128]{2,1,0:T(1,128)} %broadcast_in_dim.61), calls=%async_computation.2 | async-start | bytes 65536 | tf_op jit(solution)/shard_map/all_to_all | solution.py:17
  147.1 4.8 %collective-permute-start.1 = (f32[136,1024]{1,0:T(8,128)S(1)}, f32[136,1024]{1,0:T(8,128)S(1)}, u32[]{:S(2)}, u32[]{:S(2)}) collective-permute-start(f32[136,1024]{1,0:T(8,128)S(1)} %pad_maximum_fusion.2), channel_id=1, source_target_pairs={{0,0},{1,8},{2,16},{3,24},{4,32},{5,40},{6,48},{7,56},{8,1},{9,9},... | collective-permute-start | bytes 1671176 | tf_op jit(solution)/shard_map/ppermute | solution.py:79
  152.0 2.7 %all-to-all-done.2 = f32[64,1,128]{2,1,0:T(1,128)S(1)} async-done(((f32[64,1,128]{2,1,0:T(1,128)}), f32[64,1,128]{2,1,0:T(1,128)S(1)}, u32[]{:S(2)}, u32[]{:S(2)}) %all-to-all-start.2) | async-done | bytes 32800 | tf_op jit(solution)/shard_map/all_to_all | solution.py:17
  159.3 2.0 %stack.47 = f32[5]{0:T(128)S(1)} concatenate(f32[1]{0:T(128)} %bitcast.20, f32[1]{0:T(128)} %bitcast.21, f32[1]{0:T(128)} %bitcast.22, f32[1]{0:T(128)} %bitcast.23, f32[1]{0:T(128)} %bitcast.24), dimensions={0} | concatenate | bytes 40 | tf_op jit(solution)/shard_map/stack | solution.py:109
  161.9 5.2 %all-to-all-start.3 = ((f32[8,1,128]{2,1,0:T(1,128)}), f32[8,1,128]{2,1,0:T(1,128)S(1)}, u32[]{:S(2)}, u32[]{:S(2)}) async-start(f32[8,1,128]{2,1,0:T(1,128)} %broadcast_in_dim.62), calls=%async_computation.3 | async-start | bytes 8192 | tf_op jit(solution)/shard_map/all_to_all | solution.py:17
  167.2 3.8 %all-to-all-done.3 = f32[8,1,128]{2,1,0:T(1,128)S(1)} async-done(((f32[8,1,128]{2,1,0:T(1,128)}), f32[8,1,128]{2,1,0:T(1,128)S(1)}, u32[]{:S(2)}, u32[]{:S(2)}) %all-to-all-start.3) | async-done | bytes 4128 | tf_op jit(solution)/shard_map/all_to_all | solution.py:17
  173.5 0.8 multiply_reduce_fusion.2
  176.9 13.8 %collective-permute-done.1 = f32[136,1024]{1,0:T(8,128)S(1)} collective-permute-done((f32[136,1024]{1,0:T(8,128)S(1)}, f32[136,1024]{1,0:T(8,128)S(1)}, u32[]{:S(2)}, u32[]{:S(2)}) %collective-permute-start.1) | collective-permute-done | bytes 557088 | tf_op jit(solution)/shard_map/ppermute | solution.py:79
  191.4 1.0 fusion.3
  (38 shorter events, 7.6 us)
Async XLA Ops:
  4.2 69.8 %all-to-all-start = ((bf16[64,2,8,1024]{3,2,1,0:T(8,128)(2,1)}), bf16[64,2,8,1024]{3,2,1,0:T(8,128)(2,1)S(1)}, u32[]{:S(2)}, u32[]{:S(2)}) async-start(bf16[64,2,8,1024]{3,2,1,0:T(8,128)(2,1)} %bitcast.44), calls=%async_computation | async-start | bytes 4194304 | tf_op jit(solution)/shard_map/all_to_all | solution.py:38
  75.1 1.3 copy-start
  87.2 4.7 %copy-start.1 = (bf16[512,4,1,128]{3,2,1,0:T(2,128)(2,1)S(1)}, bf16[512,4,1,128]{3,2,1,0:T(2,128)(2,1)}, u32[]{:S(2)}) copy-start(bf16[512,4,1,128]{3,2,1,0:T(2,128)(2,1)} %get-tuple-element.20) | copy-start | bytes 1572868
  88.7 7.6 %collective-permute-start = (f32[4,136,1024]{2,1,0:T(8,128)}, f32[4,136,1024]{2,1,0:T(8,128)}, u32[]{:S(2)}, u32[]{:S(2)}) collective-permute-start(f32[4,136,1024]{2,1,0:T(8,128)} %pad_maximum_fusion), channel_id=1, source_target_pairs={{0,1},{1,0},{2,3},{3,2},{4,5},{5,4},{6,7},{7,6},{8,9},{9,8},{10,11... | collective-permute-start | bytes 6684680 | tf_op jit(solution)/shard_map/ppermute | solution.py:61
  99.8 30.5 %all-to-all-start.1 = ((f32[4,136,1024]{2,1,0:T(8,128)}), f32[4,136,1024]{2,1,0:T(8,128)}, u32[]{:S(2)}, u32[]{:S(2)}) async-start(f32[4,136,1024]{2,1,0:T(8,128)} %maximum_add_fusion), calls=%async_computation.1 | async-start | bytes 4456448 | tf_op jit(solution)/shard_map/all_to_all | solution.py:63
  138.6 16.0 %all-to-all-start.2 = ((f32[64,1,128]{2,1,0:T(1,128)}), f32[64,1,128]{2,1,0:T(1,128)S(1)}, u32[]{:S(2)}, u32[]{:S(2)}) async-start(f32[64,1,128]{2,1,0:T(1,128)} %broadcast_in_dim.61), calls=%async_computation.2 | async-start | bytes 65536 | tf_op jit(solution)/shard_map/all_to_all | solution.py:17
  147.1 43.7 %collective-permute-start.1 = (f32[136,1024]{1,0:T(8,128)S(1)}, f32[136,1024]{1,0:T(8,128)S(1)}, u32[]{:S(2)}, u32[]{:S(2)}) collective-permute-start(f32[136,1024]{1,0:T(8,128)S(1)} %pad_maximum_fusion.2), channel_id=1, source_target_pairs={{0,0},{1,8},{2,16},{3,24},{4,32},{5,40},{6,48},{7,56},{8,1},{9,9},... | collective-permute-start | bytes 1671176 | tf_op jit(solution)/shard_map/ppermute | solution.py:79
  161.9 9.0 %all-to-all-start.3 = ((f32[8,1,128]{2,1,0:T(1,128)}), f32[8,1,128]{2,1,0:T(1,128)S(1)}, u32[]{:S(2)}, u32[]{:S(2)}) async-start(f32[8,1,128]{2,1,0:T(1,128)} %broadcast_in_dim.62), calls=%async_computation.3 | async-start | bytes 8192 | tf_op jit(solution)/shard_map/all_to_all | solution.py:17

commit v2 on v0

v2 whole, which is shorter than its diff:
```python
import functools

import jax
import jax.numpy as jnp
from jax import lax
from jax.experimental import pallas as pl
from jax.experimental.pallas import tpu as pltpu
from jax.sharding import Mesh
from jax.sharding import PartitionSpec as P

PLANE = ("y", "z")
SLAB = ("z", "x", "c")
EVERY = ("y", "z", "x", "c")
F32 = jnp.float32
BF16 = jnp.bfloat16
LANES = 128
NZ, NX, NC = 8, 4, 2
NF = NX * NC
SHIFT = (0, 4, 1, 7, 2, 6, 3, 5)
COLUMN = tuple(2 * (z % 4) + z // 4 for z in range(NZ))
HOLDER = tuple(COLUMN.index(block) for block in range(NZ))


def deal_rows_kernel(core_ref, x_ref, out_ref):
    block = out_ref.shape[2]

    def deal(core):
        order = [2 * x + core for x in range(NX)] + [2 * x + 1 - core for x in range(NX)]

        def one(y, carry):
            for z in range(NZ):
                for place, f in enumerate(order):
                    start = y * block + ((z + SHIFT[f]) % NZ) * LANES
                    out_ref[y * NZ + z, :, pl.ds(place * LANES, LANES)] = x_ref[
                        :, pl.ds(pl.multiple_of(start, LANES), LANES)
                    ]
            return carry

        lax.fori_loop(0, NZ, one, 0)

    @pl.when(core_ref[0] == 0)
    def _():
        deal(0)

    @pl.when(core_ref[0] == 1)
    def _():
        deal(1)


def block_kernel(place_ref, pieces_ref, mean_ref, norms_ref, packed_ref, message_ref, *, scale):
    width, block = pieces_ref.shape[1:]
    first = place_ref[0]
    lane = lax.broadcasted_iota(jnp.int32, (8, block), 1)
    sub = lax.broadcasted_iota(jnp.int32, (8, block), 0)

    def rows(step, carry):
        off, diagonal = carry
        at = pl.ds(pl.multiple_of(step * 8, 8), 8)
        tile = (pieces_ref[0, at, :] + pieces_ref[1, at, :]) + (
            pieces_ref[2, at, :] + pieces_ref[3, at, :]
        )
        tile = tile * scale
        packed_ref[at, :] = tile
        hit = lane == first + step * 8 + sub
        rest = jnp.where(hit, 0.0, tile)
        kept = jnp.where(hit, tile, 0.0)
        squares = rest * rest
        for k in range(block // LANES):
            cut = slice(k * LANES, (k + 1) * LANES)
            off = off + squares[:, cut]
            diagonal = diagonal + jnp.where(
                sub[:, :LANES] + step * 8 == lane[:, :LANES],
                jnp.sum(kept[:, cut], axis=1, keepdims=True),
                0.0,
            )
        return off, diagonal

    zero = jnp.zeros((8, LANES), F32)
    off, diagonal = lax.fori_loop(0, width // 8, rows, (zero, zero))
    packed_ref[pl.ds(width, 8), :] = jnp.broadcast_to(mean_ref[...], (8, block))

    def total(value):
        return jnp.sum(jnp.sum(value, axis=1, keepdims=True), axis=0, keepdims=True)

    flag = jnp.where(first >= 0, 1.0, 0.0)
    own = (lane[:, :LANES] % 8) == sub[:, :LANES]
    mean = total(diagonal) / width
    apart = jnp.where(own, diagonal - mean, 0.0)
    second = total(apart * apart) * flag
    norms = norms_ref[...]
    values = (
        total(norms) / NZ,
        total(norms * norms) / NZ,
        total(off),
        mean * flag,
        second,
    )
    slot = lax.broadcasted_iota(jnp.int32, (1, LANES), 1)
    message = jnp.zeros((1, LANES), F32)
    for k, value in enumerate(values):
        message = jnp.where(slot == k, value, message)
    message_ref[...] = message


def shrink_kernel(place_ref, all_ref, owned_ref, shrunk_ref, value_ref, mean_ref, *, rows, factors):
    width, block = shrunk_ref.shape
    first = place_ref[0]
    slot = lax.broadcasted_iota(jnp.int32, (1, LANES), 1)
    count = all_ref.shape[0]

    def add(step, acc):
        return acc + all_ref[pl.ds(step * 8, 8)]

    sums = lax.fori_loop(1, count // 8, add, all_ref[pl.ds(0, 8)], unroll=4)
    sums = jnp.sum(sums, axis=0)

    def pick(row, k):
        return jnp.sum(jnp.where(slot == k, row, 0.0), axis=1, keepdims=True)

    trace_total, fourth_total, off_total = (pick(sums, k) for k in range(3))
    mu_scale = trace_total / (rows * factors)
    spread_diag = jnp.zeros((1, LANES), F32)
    for y in range(NZ):
        at = (y * NZ + HOLDER[y]) * NF
        apart = all_ref[pl.ds(at, NF)] - mu_scale[None]
        spread_diag = spread_diag + jnp.sum(apart * apart, axis=0)
    diag_total = pick(sums, 4) + width * pick(spread_diag, 3)
    spread = (off_total + diag_total) / factors
    norm_sq = factors * (spread + mu_scale * mu_scale)
    beta_value = (fourth_total / rows - norm_sq) / (factors * rows)
    shrinkage = beta_value / spread
    value_ref[...] = shrinkage
    keep = 1.0 - shrinkage
    lift = shrinkage * mu_scale
    lane = lax.broadcasted_iota(jnp.int32, (8, block), 1)
    sub = lax.broadcasted_iota(jnp.int32, (8, block), 0)

    def scale_rows(step, carry):
        at = pl.ds(pl.multiple_of(step * 8, 8), 8)
        hit = lane == first + step * 8 + sub
        shrunk_ref[at, :] = keep * owned_ref[at, :] + jnp.where(hit, lift, 0.0)
        return carry

    lax.fori_loop(0, width // 8, scale_rows, 0)
    for k in range(block // LANES):
        mean_ref[pl.ds(k, 1), :] = owned_ref[pl.ds(width, 1), pl.ds(k * LANES, LANES)]


IN_VMEM = pl.BlockSpec(memory_space=pltpu.VMEM)
IN_SMEM = pl.BlockSpec(memory_space=pltpu.SMEM)


def flip(size, bit):
    return [(k, k ^ bit) for k in range(size)]


def product(left, right):
    return lax.dot_general(left, right, (((0,), (0,)), ((), ())), preferred_element_type=F32)


def on_device(scenarios):
    row_count, factors = scenarios.shape
    ny, nz = lax.axis_size("y"), lax.axis_size("z")
    plane = ny * nz
    total_rows = row_count * plane * NF
    block = factors // ny
    width = block // NF
    y_idx, z_idx, c_idx = lax.axis_index("y"), lax.axis_index("z"), lax.axis_index("c")
    f_idx = lax.axis_index(("x", "c"))
    exchange = functools.partial(lax.all_to_all, split_axis=0, concat_axis=0, tiled=True)

    dealt = pl.pallas_call(
        deal_rows_kernel,
        out_shape=jax.ShapeDtypeStruct((plane, row_count, block), BF16),
        in_specs=[IN_SMEM, IN_VMEM],
        out_specs=IN_VMEM,
        name="deal_rows",
    )(c_idx.reshape(1), scenarios)
    rows_in = exchange(dealt, PLANE)

    blocks = scenarios.reshape(row_count, 4, 2, block).transpose(2, 1, 0, 3)
    blocks = blocks.reshape(1, nz, row_count, block)
    blocks = jnp.broadcast_to(blocks, (ny, nz, row_count, block))
    cols_in = exchange(blocks.reshape(plane, row_count, block), PLANE)

    sums = jnp.sum(rows_in.astype(F32), axis=(0, 1)).reshape(8, width)
    sums = sums + jnp.roll(lax.ppermute(sums, "c", flip(NC, 1)), NX, axis=0)
    sums = sums + lax.ppermute(sums, "x", flip(NX, 1))
    sums = sums + lax.ppermute(sums, "x", flip(NX, 2))
    mean_dealt = sums / total_rows
    own = jnp.arange(8)
    to_shift = jnp.array([SHIFT[2 * x + c] for c in range(2) for x in range(NX)], jnp.int32)
    shift_here = to_shift[(c_idx * NX + own) % 8]
    slice_of = (z_idx + shift_here) % nz
    place_of = jnp.argmax(slice_of[None, :] == own[:, None], axis=1)
    mean_plain = mean_dealt[place_of]
    pairs = [(b * nz + z, z * nz + HOLDER[b]) for b in range(ny) for z in range(nz)]
    mean_c = lax.ppermute(mean_plain, PLANE, pairs).reshape(block)

    left = (rows_in.astype(F32) - mean_dealt.reshape(block)).astype(BF16)
    left = left.reshape(plane * row_count, block)
    right = (cols_in.astype(F32) - mean_c).astype(BF16)

    mine = lax.dynamic_slice_in_dim(right, y_idx * nz, nz, 0).astype(F32)
    norms = jnp.sum(mine * mine, axis=2)
    right = right.reshape(plane * row_count, block)

    half = block // 2
    swapped = lax.ppermute(product(left[:, half:], right), "c", flip(NC, 1))
    chip_sum = product(left[:, :half], right) + swapped
    pieces = exchange(chip_sum.reshape(NX, width, block), "x")

    for bit in (1, 2, 4):
        norms = norms + lax.ppermute(norms, "z", flip(NZ, bit))

    shift = jnp.array(SHIFT, jnp.int32)[f_idx]
    column = 2 * (z_idx % 4) + z_idx // 4
    slice_here = (z_idx + shift) % nz
    first = jnp.where(y_idx == column, slice_here * width, -2 * block)
    packed, message = pl.pallas_call(
        functools.partial(block_kernel, scale=1.0 / total_rows),
        out_shape=(
            jax.ShapeDtypeStruct((width + 8, block), F32),
            jax.ShapeDtypeStruct((1, LANES), F32),
        ),
        in_specs=[IN_SMEM, IN_VMEM, IN_VMEM, IN_VMEM],
        out_specs=(IN_VMEM, IN_VMEM),
        name="block_stats",
    )(first.reshape(1), pieces, mean_c.reshape(1, block), norms)

    moves = [
        (z * NF + f, ((z + SHIFT[f]) % NZ) * NF + COLUMN[z]) for z in range(NZ) for f in range(NF)
    ]
    owned = lax.ppermute(packed, SLAB, moves)
    everyone = lax.axis_size(EVERY)
    seen = exchange(jnp.broadcast_to(message[None], (everyone, 1, LANES)), EVERY)

    first_own = jnp.where(y_idx == f_idx, z_idx * width, -2 * block)
    shrunk, shrinkage, col_mean = pl.pallas_call(
        functools.partial(shrink_kernel, rows=total_rows, factors=factors),
        out_shape=(
            jax.ShapeDtypeStruct((width, block), F32),
            jax.ShapeDtypeStruct((1, 1), F32),
            jax.ShapeDtypeStruct((block // LANES, LANES), F32),
        ),
        in_specs=[IN_SMEM, IN_VMEM, IN_VMEM],
        out_specs=(IN_VMEM, IN_VMEM, IN_VMEM),
        name="shrink",
    )(first_own.reshape(1), seen, owned)
    return (shrunk, shrinkage.reshape(()), col_mean.reshape(block))


def solution(mesh):
    finer = Mesh(mesh.devices.reshape(8, NZ, NX, NC), EVERY)
    return jax.shard_map(
        on_device,
        mesh=finer,
        in_specs=(P(EVERY, None),),
        out_specs=(P(PLANE, ("x", "c")), P(), P(("x", "c"))),
        check_vma=False,
    )
```

time: 290 us -> 175 us (0.60)
  blocking collectives: 205 us -> 0 us
  starting transfers between devices: 9.55 us -> 77 us
  waiting for transfers between devices: 42.5 us -> 72.8 us
  between operations: 18.5 us -> 1.6 us
  Pallas kernels: 0 us -> 8.36 us
  local copies, waits for them, and re-layouts: 4.33 us -> 7.76 us
    psum x12 -> x0, blocking collectives: 205 us -> none  [by_axis(): return functools.reduce(lax.psum, axes, shard)]
    all_to_all x2 -> x4, waiting for transfers between devices: 15 us -> 57.8 us  [the longest x1 26.6 us: on_device(): rows_in = exchange(dealt, PLANE)]
    ppermute x0 -> x9, starting transfers between devices: none -> 34.4 us  [the longest x3 10.3 us: on_device(): norms = norms + lax.ppermute(norms, 'z', flip(NZ, bit))]
    all_to_all x2 -> x4, starting transfers between devices: 9.55 us -> 42.6 us  [the longest x1 17.1 us: on_device(): rows_in = exchange(dealt, PLANE)]
    all_gather x1 -> x0, waiting for transfers between devices: 27.5 us -> none  [on_device(): lax.all_gather(wide_cols, SCEN, axis=0, tiled=True)]
    ppermute x0 -> x9, waiting for transfers between devices: none -> 15 us  [the longest x3 8.05 us: on_device(): norms = norms + lax.ppermute(norms, 'z', flip(NZ, bit))]
    pallas_call x0 -> x3, Pallas kernels: none -> 8.36 us  [the longest x1 3.82 us: on_device(): pl.pallas_call(functools.partial(block_kernel, scale=1.0 / total_rows), o...]
    unnamed x1 -> x18, local copies, waits for them, and re-layouts: 0.27 us -> 3.25 us
  transfers between devices with their start and end apart: 3 -> 13, of which waited for: 2 -> 11; matrix products, arithmetic and copies ran while one was open for 1% -> 4% of each run, Pallas kernels for 0% -> 0%
where the time goes in v2:
time: 175 us
  starting transfers between devices  77 us (44%)
  waiting for transfers between devices  72.8 us (42%)
  Pallas kernels  8.36 us (5%)
  local copies, waits for them, and re-layouts  7.76 us (4%)
  other arithmetic  4.28 us (2%)
  matrix products  2.8 us (2%)
    all_to_all x1, waiting for transfers between devices, on_device(): rows_in = exchange(dealt, PLANE)  26.6 us
    all_to_all x1, waiting for transfers between devices, on_device(): exchange(jnp.broadcast_to(message[None], (everyone, 1, LANES)), EVERY)  17.4 us
    all_to_all x1, starting transfers between devices, on_device(): rows_in = exchange(dealt, PLANE)  17.1 us
    all_to_all x1, starting transfers between devices, on_device(): exchange(jnp.broadcast_to(message[None], (everyone, 1, LANES)), EVERY)  12.5 us
    ppermute x3, starting transfers between devices, on_device(): norms = norms + lax.ppermute(norms, 'z', flip(NZ, bit))  10.3 us
    all_to_all x1, starting transfers between devices, on_device(): cols_in = exchange(blocks.reshape(plane, row_count, block), PLANE)  8.84 us
    all_to_all x1, waiting for transfers between devices, on_device(): cols_in = exchange(blocks.reshape(plane, row_count, block), PLANE)  8.43 us
    ppermute x3, waiting for transfers between devices, on_device(): norms = norms + lax.ppermute(norms, 'z', flip(NZ, bit))  8.05 us
  transfers between devices with their start and end apart: 13, of which 11 were waited for; matrix products, arithmetic and copies ran while one was open for 4% of the time, Pallas kernels for 0%

profile of v2, /device:TPU:1, one launch (start us, length us, event | category | flops | bytes accessed | tf_op | source)
XLA Modules:
  0.0 174.6 jit_solution(17239050066213249116)
XLA Ops:
  0.6 2.1 %deal_rows.1 = bf16[64,8,1024]{2,1,0:T(8,128)(2,1)} custom-call(s32[1]{0:T(128)} %bitcast.3.core_ref, bf16[8,8192]{1,0:T(8,128)(2,1)} %x_ref.1), custom_call_target="tpu_custom_call" | custom-call | tf_op jit(solution)/shard_map/deal_rows/pallas_call | solution.py:172
  2.7 17.1 %all-to-all-start = ((bf16[64,8,1024]{2,1,0:T(8,128)(2,1)}), bf16[64,8,1024]{2,1,0:T(8,128)(2,1)S(1)}, u32[]{:S(2)}, u32[]{:S(2)}) async-start(bf16[64,8,1024]{2,1,0:T(8,128)(2,1)} %deal_rows.1), calls=%async_computation | async-start | bytes 2097152 | tf_op jit(solution)/shard_map/all_to_all | solution.py:179
  20.1 26.6 %all-to-all-done = bf16[64,8,1024]{2,1,0:T(8,128)(2,1)S(1)} async-done(((bf16[64,8,1024]{2,1,0:T(8,128)(2,1)}), bf16[64,8,1024]{2,1,0:T(8,128)(2,1)S(1)}, u32[]{:S(2)}, u32[]{:S(2)}) %all-to-all-start) | async-done | bytes 1048608 | tf_op jit(solution)/shard_map/all_to_all | solution.py:179
  46.7 1.1 broadcast_in_dim.22
  47.8 8.8 %all-to-all-start.1 = ((bf16[64,8,1024]{2,1,0:T(8,128)(2,1)}), bf16[64,8,1024]{2,1,0:T(8,128)(2,1)S(1)}, u32[]{:S(2)}, u32[]{:S(2)}) async-start(bf16[64,8,1024]{2,1,0:T(8,128)(2,1)} %bitcast.9), calls=%async_computation.1 | async-start | bytes 2097152 | tf_op jit(solution)/shard_map/all_to_all | solution.py:184
  57.6 3.2 %collective-permute-start = (f32[8,128]{1,0:T(8,128)S(1)}, f32[8,128]{1,0:T(8,128)S(1)}, u32[]{:S(2)}, u32[]{:S(2)}) collective-permute-start(f32[8,128]{1,0:T(8,128)S(1)} %bitcast.31), channel_id=1, source_target_pairs={{0,1},{1,0},{2,3},{3,2},{4,5},{5,4},{6,7},{7,6},{8,9},{9,8},{10,11... | collective-permute-start | bytes 12296 | tf_op jit(solution)/shard_map/ppermute | solution.py:187
  61.6 3.1 %collective-permute-start.1 = (f32[8,128]{1,0:T(8,128)S(1)}, f32[8,128]{1,0:T(8,128)S(1)}, u32[]{:S(2)}, u32[]{:S(2)}) collective-permute-start(f32[8,128]{1,0:T(8,128)S(1)} %maximum_add_fusion), channel_id=1, source_target_pairs={{0,2},{2,0},{4,6},{6,4},{1,3},{3,1},{5,7},{7,5},{8,10},{10,8},{12,... | collective-permute-start | bytes 12296 | tf_op jit(solution)/shard_map/ppermute | solution.py:188
  64.8 1.5 collective-permute-done.1
  66.3 4.6 %collective-permute-start.2 = (f32[8,128]{1,0:T(8,128)S(1)}, f32[8,128]{1,0:T(8,128)S(1)}, u32[]{:S(2)}, u32[]{:S(2)}) collective-permute-start(f32[8,128]{1,0:T(8,128)S(1)} %add.108), channel_id=1, source_target_pairs={{0,4},{2,6},{4,0},{6,2},{1,5},{3,7},{5,1},{7,3},{8,12},{10,14},{12... | collective-permute-start | bytes 12296 | tf_op jit(solution)/shard_map/ppermute | solution.py:189
  70.9 1.5 collective-permute-done.2
  73.6 1.2 fusion.1
  74.9 8.4 %all-to-all-done.1 = bf16[64,8,1024]{2,1,0:T(8,128)(2,1)S(1)} async-done(((bf16[64,8,1024]{2,1,0:T(8,128)(2,1)}), bf16[64,8,1024]{2,1,0:T(8,128)(2,1)S(1)}, u32[]{:S(2)}, u32[]{:S(2)}) %all-to-all-start.1) | async-done | bytes 1048608 | tf_op jit(solution)/shard_map/all_to_all | solution.py:184
  83.3 1.0 copy-done.2
  84.3 1.5 subtract_convert_fusion
  86.5 6.0 %collective-permute-start.4 = (f32[512,1024]{1,0:T(8,128)S(1)}, f32[512,1024]{1,0:T(8,128)S(1)}, u32[]{:S(2)}, u32[]{:S(2)}) collective-permute-start(f32[512,1024]{1,0:T(8,128)S(1)} %fusion.2), channel_id=1, source_target_pairs={{0,1},{1,0},{2,3},{3,2},{4,5},{5,4},{6,7},{7,6},{8,9},{9,8},{10,11... | collective-permute-start | bytes 6291464 | tf_op jit(solution)/shard_map/ppermute | solution.py:209
  92.5 3.8 %collective-permute-done.4 = f32[512,1024]{1,0:T(8,128)S(1)} collective-permute-done((f32[512,1024]{1,0:T(8,128)S(1)}, f32[512,1024]{1,0:T(8,128)S(1)}, u32[]{:S(2)}, u32[]{:S(2)}) %collective-permute-start.4) | collective-permute-done | bytes 2097184 | tf_op jit(solution)/shard_map/ppermute | solution.py:209
  96.3 2.1 %convolution_add_fusion = f32[512,1024]{1,0:T(8,128)} fusion(f32[512,1024]{1,0:T(8,128)S(1)} %collective-permute-done.4, bf16[64,8,1024]{2,1,0:T(8,128)(2,1)S(1)} %subtract_convert_fusion, bf16[512,1024]{1,0:T(8,128)(2,1)S(1)} %copy-done.3), kind=kOutput, calls=%fused_computation.6 | convolution fusion | flops 537395200 | bytes 5767168 | tf_op jit(solution)/shard_map/dot_general | solution.py:158
  98.4 4.1 %all-to-all-start.2 = ((f32[4,128,1024]{2,1,0:T(8,128)}), f32[4,128,1024]{2,1,0:T(8,128)S(1)}, u32[]{:S(2)}, u32[]{:S(2)}) async-start(f32[4,128,1024]{2,1,0:T(8,128)} %bitcast.25), calls=%async_computation.2 | async-start | bytes 4194304 | tf_op jit(solution)/shard_map/all_to_all | solution.py:211
  103.9 1.9 %collective-permute-start.5 = (f32[8,8]{1,0:T(8,128)S(1)}, f32[8,8]{1,0:T(8,128)S(1)}, u32[]{:S(2)}, u32[]{:S(2)}) collective-permute-start(f32[8,8]{1,0:T(8,128)S(1)} %multiply_reduce_fusion), channel_id=1, source_target_pairs={{0,8},{8,0},{16,24},{24,16},{32,40},{40,32},{48,56},{56,48},{1,9},... | collective-permute-start | bytes 776 | tf_op jit(solution)/shard_map/ppermute | solution.py:214
  105.8 2.7 %collective-permute-done.5 = f32[8,8]{1,0:T(8,128)S(1)} collective-permute-done((f32[8,8]{1,0:T(8,128)S(1)}, f32[8,8]{1,0:T(8,128)S(1)}, u32[]{:S(2)}, u32[]{:S(2)}) %collective-permute-start.5) | collective-permute-done | bytes 288 | tf_op jit(solution)/shard_map/ppermute | solution.py:214
  108.5 3.4 %collective-permute-start.6 = (f32[8,8]{1,0:T(8,128)S(1)}, f32[8,8]{1,0:T(8,128)S(1)}, u32[]{:S(2)}, u32[]{:S(2)}) collective-permute-start(f32[8,8]{1,0:T(8,128)S(1)} %add.120), channel_id=1, source_target_pairs={{0,16},{8,24},{16,0},{24,8},{32,48},{40,56},{48,32},{56,40},{1,17}... | collective-permute-start | bytes 776 | tf_op jit(solution)/shard_map/ppermute | solution.py:214
  111.9 2.1 %collective-permute-done.6 = f32[8,8]{1,0:T(8,128)S(1)} collective-permute-done((f32[8,8]{1,0:T(8,128)S(1)}, f32[8,8]{1,0:T(8,128)S(1)}, u32[]{:S(2)}, u32[]{:S(2)}) %collective-permute-start.6) | collective-permute-done | bytes 288 | tf_op jit(solution)/shard_map/ppermute | solution.py:214
  114.1 5.0 %collective-permute-start.7 = (f32[8,8]{1,0:T(8,128)S(1)}, f32[8,8]{1,0:T(8,128)S(1)}, u32[]{:S(2)}, u32[]{:S(2)}) collective-permute-start(f32[8,8]{1,0:T(8,128)S(1)} %add.121), channel_id=1, source_target_pairs={{0,32},{8,40},{16,48},{24,56},{32,0},{40,8},{48,16},{56,24},{1,33}... | collective-permute-start | bytes 776 | tf_op jit(solution)/shard_map/ppermute | solution.py:214
  119.1 3.2 %collective-permute-done.7 = f32[8,8]{1,0:T(8,128)S(1)} collective-permute-done((f32[8,8]{1,0:T(8,128)S(1)}, f32[8,8]{1,0:T(8,128)S(1)}, u32[]{:S(2)}, u32[]{:S(2)}) %collective-permute-start.7) | collective-permute-done | bytes 288 | tf_op jit(solution)/shard_map/ppermute | solution.py:214
  122.9 5.4 %all-to-all-done.2.pieces_ref = f32[4,128,1024]{2,1,0:T(8,128)S(1)} async-done(((f32[4,128,1024]{2,1,0:T(8,128)}), f32[4,128,1024]{2,1,0:T(8,128)S(1)}, u32[]{:S(2)}, u32[]{:S(2)}) %all-to-all-start.2) | async-done | bytes 2097184 | tf_op jit(solution)/shard_map/all_to_all | solution.py:211
  128.3 1.3 copy-done.1
  129.6 3.8 %block_stats.1 = (f32[136,1024]{1,0:T(8,128)}, f32[1,128]{1,0:T(1,128)}) custom-call(s32[1]{0:T(128)} %bitcast.2.place_ref, f32[4,128,1024]{2,1,0:T(8,128)} %copy-done.1, f32[1,1024]{1,0:T(1,128)} %bitcast.30, f32[8,8]{1,0:T(8,128)} %add.122.norms_ref), custom_call_target="tpu_custom_call" | custom-call | tf_op jit(solution)/shard_map/block_stats/pallas_call | solution.py:220
  133.4 6.4 %collective-permute-start.8 = (f32[136,1024]{1,0:T(8,128)}, f32[136,1024]{1,0:T(8,128)S(1)}, u32[]{:S(2)}, u32[]{:S(2)}) collective-permute-start(f32[136,1024]{1,0:T(8,128)} %get-tuple-element.11), channel_id=1, source_target_pairs={{0,0},{1,32},{2,8},{3,56},{4,16},{5,48},{6,24},{7,40},{8,10},{9,42... | collective-permute-start | bytes 1671176 | tf_op jit(solution)/shard_map/ppermute | solution.py:234
  139.9 1.4 broadcast_in_dim.25
  141.3 12.5 %all-to-all-start.3 = ((f32[512,1,128]{2,1,0:T(1,128)}), f32[512,1,128]{2,1,0:T(1,128)S(1)}, u32[]{:S(2)}, u32[]{:S(2)}) async-start(f32[512,1,128]{2,1,0:T(1,128)} %broadcast_in_dim.25), calls=%async_computation.3 | async-start | bytes 524288 | tf_op jit(solution)/shard_map/all_to_all | solution.py:236
  153.8 17.4 %all-to-all-done.3.all_ref = f32[512,1,128]{2,1,0:T(1,128)S(1)} async-done(((f32[512,1,128]{2,1,0:T(1,128)}), f32[512,1,128]{2,1,0:T(1,128)S(1)}, u32[]{:S(2)}, u32[]{:S(2)}) %all-to-all-start.3) | async-done | bytes 262176 | tf_op jit(solution)/shard_map/all_to_all | solution.py:236
  172.1 2.4 %shrink.1 = (f32[128,1024]{1,0:T(8,128)}, f32[1,1]{1,0:T(1,128)}, f32[8,128]{1,0:T(8,128)}) custom-call(s32[1]{0:T(128)} %bitcast.place_ref, f32[512,1,128]{2,1,0:T(1,128)} %copy-done.4, f32[136,1024]{1,0:T(8,128)} %copy-done.5), custom_call_target="tpu_custom_call" | custom-call | tf_op jit(solution)/shard_map/shrink/pallas_call | solution.py:239
  (41 shorter events, 6.0 us)
Async XLA Ops:
  0.6 19.2 %copy-start.6 = (bf16[8,8192]{1,0:T(8,128)(2,1)S(1)}, bf16[8,8192]{1,0:T(8,128)(2,1)}, u32[]{:S(2)}) copy-start(bf16[8,8192]{1,0:T(8,128)(2,1)} %x_ref.1) | copy-start | bytes 393220
  2.7 44.0 %all-to-all-start = ((bf16[64,8,1024]{2,1,0:T(8,128)(2,1)}), bf16[64,8,1024]{2,1,0:T(8,128)(2,1)S(1)}, u32[]{:S(2)}, u32[]{:S(2)}) async-start(bf16[64,8,1024]{2,1,0:T(8,128)(2,1)} %deal_rows.1), calls=%async_computation | async-start | bytes 2097152 | tf_op jit(solution)/shard_map/all_to_all | solution.py:179
  19.9 36.8 %copy-start = (s32[8]{0:T(128)S(1)}, s32[8]{0:T(128)}, u32[]{:S(2)}) copy-start(s32[8]{0:T(128)} %constant.89.clone) | copy-start | bytes 100
  47.8 35.5 %all-to-all-start.1 = ((bf16[64,8,1024]{2,1,0:T(8,128)(2,1)}), bf16[64,8,1024]{2,1,0:T(8,128)(2,1)S(1)}, u32[]{:S(2)}, u32[]{:S(2)}) async-start(bf16[64,8,1024]{2,1,0:T(8,128)(2,1)} %bitcast.9), calls=%async_computation.1 | async-start | bytes 2097152 | tf_op jit(solution)/shard_map/all_to_all | solution.py:184
  57.6 4.0 %collective-permute-start = (f32[8,128]{1,0:T(8,128)S(1)}, f32[8,128]{1,0:T(8,128)S(1)}, u32[]{:S(2)}, u32[]{:S(2)}) collective-permute-start(f32[8,128]{1,0:T(8,128)S(1)} %bitcast.31), channel_id=1, source_target_pairs={{0,1},{1,0},{2,3},{3,2},{4,5},{5,4},{6,7},{7,6},{8,9},{9,8},{10,11... | collective-permute-start | bytes 12296 | tf_op jit(solution)/shard_map/ppermute | solution.py:187
  61.6 4.6 %collective-permute-start.1 = (f32[8,128]{1,0:T(8,128)S(1)}, f32[8,128]{1,0:T(8,128)S(1)}, u32[]{:S(2)}, u32[]{:S(2)}) collective-permute-start(f32[8,128]{1,0:T(8,128)S(1)} %maximum_add_fusion), channel_id=1, source_target_pairs={{0,2},{2,0},{4,6},{6,4},{1,3},{3,1},{5,7},{7,5},{8,10},{10,8},{12,... | collective-permute-start | bytes 12296 | tf_op jit(solution)/shard_map/ppermute | solution.py:188
  66.3 6.1 %collective-permute-start.2 = (f32[8,128]{1,0:T(8,128)S(1)}, f32[8,128]{1,0:T(8,128)S(1)}, u32[]{:S(2)}, u32[]{:S(2)}) collective-permute-start(f32[8,128]{1,0:T(8,128)S(1)} %add.108), channel_id=1, source_target_pairs={{0,4},{2,6},{4,0},{6,2},{1,5},{3,7},{5,1},{7,3},{8,12},{10,14},{12... | collective-permute-start | bytes 12296 | tf_op jit(solution)/shard_map/ppermute | solution.py:189
  73.0 10.3 %collective-permute-start.3 = (f32[8,128]{1,0:T(8,128)S(1)}, f32[8,128]{1,0:T(8,128)S(1)}, u32[]{:S(2)}, u32[]{:S(2)}) collective-permute-start(f32[8,128]{1,0:T(8,128)S(1)} %gather_fusion.1), channel_id=1, source_target_pairs={{0,0},{8,64},{16,128},{24,192},{32,256},{40,320},{48,384},{56,448}... | collective-permute-start | bytes 12296 | tf_op jit(solution)/shard_map/ppermute | solution.py:198
  74.9 10.9 %copy-start.3 = (bf16[512,1024]{1,0:T(8,128)(2,1)S(1)}, bf16[512,1024]{1,0:T(8,128)(2,1)}, u32[]{:S(2)}) copy-start(bf16[512,1024]{1,0:T(8,128)(2,1)} %fusion.1) | copy-start | bytes 3145732
  83.3 1.0 copy-start.2
  84.3 2.2 %copy-start.7 = (f32[8,128]{1,0:T(8,128)}, f32[8,128]{1,0:T(8,128)S(1)}, u32[]{:S(2)}) copy-start(f32[8,128]{1,0:T(8,128)S(1)} %collective-permute-done.3) | copy-start | bytes 12292
  86.5 9.8 %collective-permute-start.4 = (f32[512,1024]{1,0:T(8,128)S(1)}, f32[512,1024]{1,0:T(8,128)S(1)}, u32[]{:S(2)}, u32[]{:S(2)}) collective-permute-start(f32[512,1024]{1,0:T(8,128)S(1)} %fusion.2), channel_id=1, source_target_pairs={{0,1},{1,0},{2,3},{3,2},{4,5},{5,4},{6,7},{7,6},{8,9},{9,8},{10,11... | collective-permute-start | bytes 6291464 | tf_op jit(solution)/shard_map/ppermute | solution.py:209
  98.4 4.1 %copy-start.8 = (s32[8]{0:T(128)S(1)}, s32[8]{0:T(128)}, u32[]{:S(2)}) copy-start(s32[8]{0:T(128)} %constant.90.clone) | copy-start | bytes 100
  98.4 29.9 %all-to-all-start.2 = ((f32[4,128,1024]{2,1,0:T(8,128)}), f32[4,128,1024]{2,1,0:T(8,128)S(1)}, u32[]{:S(2)}, u32[]{:S(2)}) async-start(f32[4,128,1024]{2,1,0:T(8,128)} %bitcast.25), calls=%async_computation.2 | async-start | bytes 4194304 | tf_op jit(solution)/shard_map/all_to_all | solution.py:211
  103.9 4.6 %collective-permute-start.5 = (f32[8,8]{1,0:T(8,128)S(1)}, f32[8,8]{1,0:T(8,128)S(1)}, u32[]{:S(2)}, u32[]{:S(2)}) collective-permute-start(f32[8,8]{1,0:T(8,128)S(1)} %multiply_reduce_fusion), channel_id=1, source_target_pairs={{0,8},{8,0},{16,24},{24,16},{32,40},{40,32},{48,56},{56,48},{1,9},... | collective-permute-start | bytes 776 | tf_op jit(solution)/shard_map/ppermute | solution.py:214
  108.5 5.5 %collective-permute-start.6 = (f32[8,8]{1,0:T(8,128)S(1)}, f32[8,8]{1,0:T(8,128)S(1)}, u32[]{:S(2)}, u32[]{:S(2)}) collective-permute-start(f32[8,8]{1,0:T(8,128)S(1)} %add.120), channel_id=1, source_target_pairs={{0,16},{8,24},{16,0},{24,8},{32,48},{40,56},{48,32},{56,40},{1,17}... | collective-permute-start | bytes 776 | tf_op jit(solution)/shard_map/ppermute | solution.py:214
  114.1 8.2 %collective-permute-start.7 = (f32[8,8]{1,0:T(8,128)S(1)}, f32[8,8]{1,0:T(8,128)S(1)}, u32[]{:S(2)}, u32[]{:S(2)}) collective-permute-start(f32[8,8]{1,0:T(8,128)S(1)} %add.121), channel_id=1, source_target_pairs={{0,32},{8,40},{16,48},{24,56},{32,0},{40,8},{48,16},{56,24},{1,33}... | collective-permute-start | bytes 776 | tf_op jit(solution)/shard_map/ppermute | solution.py:214
  128.3 1.3 copy-start.1
  133.4 37.8 %collective-permute-start.8 = (f32[136,1024]{1,0:T(8,128)}, f32[136,1024]{1,0:T(8,128)S(1)}, u32[]{:S(2)}, u32[]{:S(2)}) collective-permute-start(f32[136,1024]{1,0:T(8,128)} %get-tuple-element.11), channel_id=1, source_target_pairs={{0,0},{1,32},{2,8},{3,56},{4,16},{5,48},{6,24},{7,40},{8,10},{9,42... | collective-permute-start | bytes 1671176 | tf_op jit(solution)/shard_map/ppermute | solution.py:234
  141.3 29.9 %all-to-all-start.3 = ((f32[512,1,128]{2,1,0:T(1,128)}), f32[512,1,128]{2,1,0:T(1,128)S(1)}, u32[]{:S(2)}, u32[]{:S(2)}) async-start(f32[512,1,128]{2,1,0:T(1,128)} %broadcast_in_dim.25), calls=%async_computation.3 | async-start | bytes 524288 | tf_op jit(solution)/shard_map/all_to_all | solution.py:236
  171.2 0.7 copy-start.4
  171.2 0.9 copy-start.5

commit v3 on v0

v3 whole, which is shorter than its diff:
```python
import functools

import jax
import jax.numpy as jnp
from jax import lax
from jax.experimental import pallas as pl
from jax.experimental.pallas import tpu as pltpu
from jax.sharding import Mesh
from jax.sharding import PartitionSpec as P

PLANE = ("y", "z")
LINE = ("x", "c")
SLAB = ("z", "x", "c")
EVERY = ("y", "z", "x", "c")
F32 = jnp.float32
BF16 = jnp.bfloat16
LANES = 128
NY, NZ, NX, NC = 8, 8, 4, 2
NF = NX * NC
SHIFT = (0, 4, 1, 7, 2, 6, 3, 5)
COLUMN = tuple(2 * (z % 4) + z // 4 for z in range(NZ))
HOLDER = tuple(COLUMN.index(block) for block in range(NZ))
OFF, SECOND, MEANS = 64, 65, 66
IN_VMEM = pl.BlockSpec(memory_space=pltpu.VMEM)
IN_SMEM = pl.BlockSpec(memory_space=pltpu.SMEM)


def deal_kernel(core_ref, x_ref, out_ref):
    block = out_ref.shape[3]
    half = block // 2
    core = core_ref[0]

    def take(start, size):
        return x_ref[:, pl.ds(pl.multiple_of(start, LANES), size)]

    def one(y, carry):
        for z in range(NZ):
            to = y * NZ + z
            for f in range(NF):
                at = pl.ds(f * LANES, LANES)
                out_ref[to, 0, :, at] = take(y * block + ((z + SHIFT[f]) % NZ) * LANES, LANES)
            start = COLUMN[z] * block
            out_ref[to, 1, :, pl.ds(0, half)] = take(start + core * half, half)
            out_ref[to, 1, :, pl.ds(half, half)] = take(start + (1 - core) * half, half)
        return carry

    lax.fori_loop(0, NY, one, 0)


def add_all(value):
    return jnp.sum(jnp.sum(value, axis=1, keepdims=True), axis=0, keepdims=True)


def in_lane(k, value, row):
    slot = lax.broadcasted_iota(jnp.int32, (1, LANES), 1)
    return jnp.where(slot == k, value, row)


def block_kernel(
    place_ref, pieces_ref, mean_ref, norms_ref, same_ref, other_ref, message_ref, off_ref, diag_ref, *, scale
):
    step, steps = pl.program_id(0), pl.num_programs(0)
    rows, half = pieces_ref.shape[1:]
    width = rows * steps // 2
    which = step // (steps // 2)
    base = (step % (steps // 2)) * rows
    first = place_ref[which]
    same = place_ref[2] == which
    lane = lax.broadcasted_iota(jnp.int32, (8, half), 1)
    sub = lax.broadcasted_iota(jnp.int32, (8, half), 0)

    @pl.when(step == 0)
    def _():
        off_ref[...] = jnp.zeros_like(off_ref)
        diag_ref[...] = jnp.zeros_like(diag_ref)

    off = off_ref[...]
    diagonal = diag_ref[which]
    tiles = []
    for k in range(rows // 8):
        at = pl.ds(k * 8, 8)
        tile = (pieces_ref[0, at, :] + pieces_ref[1, at, :]) + (
            pieces_ref[2, at, :] + pieces_ref[3, at, :]
        )
        tile = tile * scale
        tiles.append(tile)
        hit = lane == first + base + k * 8 + sub
        rest = jnp.where(hit, 0.0, tile)
        kept = jnp.where(hit, tile, 0.0)
        squares = rest * rest
        for j in range(half // LANES):
            cut = slice(j * LANES, (j + 1) * LANES)
            off = off + squares[:, cut]
            diagonal = diagonal + kept[:, cut]
    off_ref[...] = off
    diag_ref[which] = diagonal
    whole = jnp.concatenate(tiles, axis=0)
    to = pl.ds(pl.multiple_of(base, 8), rows)

    @pl.when(same)
    def _():
        same_ref[to, :] = whole

    @pl.when(jnp.logical_not(same))
    def _():
        other_ref[to, :] = whole

    @pl.when(step == steps - 1)
    def _():
        same_ref[pl.ds(width, 8), :] = mean_ref[...]
        own = lax.broadcasted_iota(jnp.int32, (8, LANES), 1) % 8 == lax.broadcasted_iota(
            jnp.int32, (8, LANES), 0
        )
        row = in_lane(OFF, add_all(off_ref[...]), norms_ref[...])
        flags = jnp.zeros((1, LANES), F32)
        second = jnp.zeros((1, 1), F32)
        for j in range(2):
            flag = jnp.where(place_ref[j] >= 0, 1.0, 0.0)
            mean = add_all(diag_ref[j]) / width
            apart = jnp.where(own, diag_ref[j] - mean, 0.0)
            second = second + add_all(apart * apart) * flag
            row = in_lane(MEANS + j, mean * flag, row)
            flags = in_lane(MEANS + j, flag, flags)
        row = in_lane(SECOND, second, row)
        message_ref[...] = jnp.broadcast_to(
            jnp.concatenate((row, flags), axis=0)[None], message_ref.shape
        )


def middle_kernel(seen_ref, message_ref, *, width):
    seen = seen_ref[...]
    slot = lax.broadcasted_iota(jnp.int32, (1, 1, LANES), 2)
    values, flags = seen[:, 0:1, :], seen[:, 1:2, :]
    norms = jnp.sum(values.reshape(NZ, NF, 1, LANES), axis=0)
    norms = jnp.where(slot < OFF, norms, 0.0)
    total = jnp.sum(values, axis=0)
    is_mean = (slot >= MEANS) & (slot < MEANS + 2)

    def lanes(row):
        return jnp.sum(row, axis=1, keepdims=True)

    mean = lanes(jnp.where(is_mean[0], total, 0.0)) / NF
    apart = jnp.where(is_mean, (values - mean[None]) * flags, 0.0)
    between = lanes(jnp.sum(apart * apart, axis=0))
    second = lanes(jnp.where(slot[0] == SECOND, total, 0.0)) + width * between
    row = jnp.zeros((1, LANES), F32)
    row = in_lane(0, lanes(jnp.sum(norms, axis=0)), row)
    row = in_lane(1, lanes(jnp.sum(norms * norms, axis=0)), row)
    row = in_lane(2, lanes(jnp.where(slot[0] == OFF, total, 0.0)), row)
    row = in_lane(3, mean, row)
    row = in_lane(4, second, row)
    message_ref[...] = jnp.broadcast_to(row[None], message_ref.shape)


def shrink_kernel(
    place_ref, totals_ref, same_ref, other_ref, shrunk_ref, value_ref, mean_ref, *, rows, factors
):
    width, block = shrunk_ref.shape
    half = block // 2
    first, which = place_ref[0], place_ref[1]
    slot = lax.broadcasted_iota(jnp.int32, (1, LANES), 1)
    totals = totals_ref[...]
    sums = jnp.sum(totals, axis=0)

    def pick(row, k):
        return jnp.sum(jnp.where(slot == k, row, 0.0), axis=1, keepdims=True)

    mu_scale = pick(sums, 0) / (rows * factors)
    apart = totals - mu_scale[None]
    from_mu = pick(jnp.sum(apart * apart, axis=0), 3)
    spread = (pick(sums, 2) + pick(sums, 4) + block * from_mu) / factors
    norm_sq = factors * (spread + mu_scale * mu_scale)
    beta_value = (pick(sums, 1) / rows - norm_sq) / (factors * rows)
    shrinkage = beta_value / spread
    value_ref[...] = shrinkage
    keep = 1.0 - shrinkage
    lift = shrinkage * mu_scale
    lane = lax.broadcasted_iota(jnp.int32, (8, half), 1)
    sub = lax.broadcasted_iota(jnp.int32, (8, half), 0)

    def write(source_ref, side):
        for k in range(width // 8):
            at = pl.ds(k * 8, 8)
            hit = lane + side * half == first + k * 8 + sub
            shrunk_ref[at, pl.ds(side * half, half)] = keep * source_ref[at, :] + jnp.where(
                hit, lift, 0.0
            )

    @pl.when(which == 0)
    def _():
        write(same_ref, 0)
        write(other_ref, 1)

    @pl.when(which == 1)
    def _():
        write(other_ref, 0)
        write(same_ref, 1)

    for k in range(block // LANES):
        mean_ref[pl.ds(k, 1), :] = same_ref[
            pl.ds(width + k * LANES // half, 1), pl.ds(k * LANES % half, LANES)
        ]


def flip(size):
    return [(k, k ^ 1) for k in range(size)]


def product(left, right):
    return lax.dot_general(left, right, (((0,), (0,)), ((), ())), preferred_element_type=F32)


def on_device(scenarios):
    row_count, factors = scenarios.shape
    plane = NY * NZ
    total_rows = row_count * plane * NF
    part_rows = row_count * plane
    block = factors // NY
    half, width = block // 2, block // NF
    y_idx, z_idx = lax.axis_index("y"), lax.axis_index("z")
    x_idx, c_idx = lax.axis_index("x"), lax.axis_index("c")
    f_idx = x_idx * NC + c_idx
    exchange = functools.partial(lax.all_to_all, split_axis=0, concat_axis=0, tiled=True)
    shapes = jax.ShapeDtypeStruct

    dealt = pl.pallas_call(
        deal_kernel,
        out_shape=shapes((plane, 2, row_count, block), BF16),
        in_specs=[IN_SMEM, IN_VMEM],
        out_specs=IN_VMEM,
        name="deal",
    )(c_idx.reshape(1), scenarios)
    arrived = exchange(dealt, PLANE)

    swapped = lax.ppermute(arrived, "c", flip(NC))
    sums = jnp.sum(arrived.astype(F32), axis=(0, 2))
    sums_c = jnp.where(c_idx == 0, sums[1], jnp.roll(sums[1], half))
    sums = jnp.stack((sums[0], sums_c)).reshape(2 * NF, width)
    sums = exchange(jnp.broadcast_to(sums[None], (NF, 2 * NF, width)), LINE)
    means = (jnp.sum(sums, axis=0) / total_rows).reshape(2, block)
    mean_r, mean_c = means[0], means[1]
    mean_own = jnp.where(c_idx == 0, mean_c, jnp.roll(mean_c, half))

    def centred(rows, mean):
        out = (rows.astype(F32) - mean).astype(BF16)
        return out.reshape(part_rows, out.shape[-1])

    mean_half = mean_own[:half]
    partial = product(centred(arrived[:, 0], mean_r), centred(arrived[:, 1, :, :half], mean_half))
    partial = partial + product(
        centred(swapped[:, 0], mean_r), centred(swapped[:, 1, :, half:], mean_half)
    )
    pieces = exchange(partial.reshape(NX, 2 * width, half), "x")

    mine = lax.dynamic_slice_in_dim(arrived, y_idx * NZ, NZ, 0)[:, 1]
    mine = (mine.astype(F32) - mean_own).astype(BF16).astype(F32)
    norms = jnp.sum(mine * mine, axis=2).reshape(1, NZ * row_count)
    norms = jnp.pad(norms, ((0, 0), (0, LANES - NZ * row_count)))

    shift = jnp.array(SHIFT, jnp.int32)
    column = 2 * (z_idx % 4) + z_idx // 4
    never = -2 * block
    places = []
    for j in range(2):
        piece = (z_idx + shift[x_idx * NC + j]) % NZ
        held = (y_idx == column) & (piece // 4 == c_idx)
        places.append(jnp.where(held, (piece % 4) * width, never))
    places.append(c_idx)
    steps = 4
    mean_rows = jnp.pad(mean_c.reshape(2, half), ((0, 6), (0, 0)))
    whole = lambda *dims: pl.BlockSpec(dims, lambda i: (0,) * len(dims))
    same, other, message = pl.pallas_call(
        functools.partial(block_kernel, scale=1.0 / total_rows),
        grid=(steps,),
        out_shape=(
            shapes((width + 8, half), F32),
            shapes((width, half), F32),
            shapes((NZ * NF, 2, LANES), F32),
        ),
        in_specs=[
            IN_SMEM,
            pl.BlockSpec((NX, 2 * width // steps, half), lambda i: (0, i, 0)),
            whole(8, half),
            whole(1, LANES),
        ],
        out_specs=(whole(width + 8, half), whole(width, half), whole(NZ * NF, 2, LANES)),
        scratch_shapes=[pltpu.VMEM((8, LANES), F32), pltpu.VMEM((2, 8, LANES), F32)],
        name="block_stats",
    )(jnp.stack(places), pieces, mean_rows, norms)

    seen = exchange(message, SLAB)

    def owner(z, f):
        return ((z + SHIFT[f]) % NZ) * NF + COLUMN[z]

    own_same = lax.ppermute(
        same, SLAB, [(z * NF + f, owner(z, f)) for z in range(NZ) for f in range(NF)]
    )
    own_other = lax.ppermute(
        other, SLAB, [(z * NF + f, owner(z, f ^ 1)) for z in range(NZ) for f in range(NF)]
    )
    second = pl.pallas_call(
        functools.partial(middle_kernel, width=width),
        out_shape=shapes((NY, 1, LANES), F32),
        in_specs=[IN_VMEM],
        out_specs=IN_VMEM,
        name="middle_stats",
    )(seen)
    totals = exchange(second, "y")

    first_own = jnp.where(y_idx == f_idx, z_idx * width, never)
    core_of = jnp.array([SHIFT.index(s) % 2 for s in range(NZ)], jnp.int32)
    from_z = f_idx // 2 + 4 * (f_idx % 2)
    which_own = core_of[(z_idx - from_z) % NZ]
    shrunk, shrinkage, col_mean = pl.pallas_call(
        functools.partial(shrink_kernel, rows=total_rows, factors=factors),
        out_shape=(
            shapes((width, block), F32),
            shapes((1, 1), F32),
            shapes((block // LANES, LANES), F32),
        ),
        in_specs=[IN_SMEM, IN_VMEM, IN_VMEM, IN_VMEM],
        out_specs=(IN_VMEM, IN_VMEM, IN_VMEM),
        name="shrink",
    )(jnp.stack((first_own, which_own)), totals, own_same, own_other)
    return (shrunk, shrinkage.reshape(()), col_mean.reshape(block))


def solution(mesh):
    finer = Mesh(mesh.devices.reshape(NY, NZ, NX, NC), EVERY)
    return jax.shard_map(
        on_device,
        mesh=finer,
        in_specs=(P(EVERY, None),),
        out_specs=(P(PLANE, LINE), P(), P(LINE)),
        check_vma=False,
    )
```

time: 290 us -> 171 us (0.59)
  blocking collectives: 205 us -> 0 us
  starting transfers between devices: 9.55 us -> 57.4 us
  waiting for transfers between devices: 42.5 us -> 89.3 us
  between operations: 18.5 us -> 2.28 us
  Pallas kernels: 0 us -> 9.91 us
    psum x12 -> x0, blocking collectives: 205 us -> none  [by_axis(): return functools.reduce(lax.psum, axes, shard)]
    all_to_all x2 -> x5, waiting for transfers between devices: 15 us -> 88.8 us  [the longest x1 48.5 us: on_device(): arrived = exchange(dealt, PLANE)]
    all_to_all x2 -> x5, starting transfers between devices: 9.55 us -> 46.1 us  [the longest x1 17.1 us: on_device(): arrived = exchange(dealt, PLANE)]
    all_gather x1 -> x0, waiting for transfers between devices: 27.5 us -> none  [on_device(): lax.all_gather(wide_cols, SCEN, axis=0, tiled=True)]
    ppermute x0 -> x3, starting transfers between devices: none -> 11.3 us  [the longest x1 7.42 us: on_device(): lax.ppermute(same, SLAB, [(z * NF + f, owner(z, f)) for z in range(NZ) fo...]
    pallas_call x0 -> x4, Pallas kernels: none -> 9.91 us  [the longest x1 3.53 us: on_device(): pl.pallas_call(functools.partial(block_kernel, scale=1.0 / total_rows), g...]
  transfers between devices with their start and end apart: 3 -> 8, of which waited for: 2 -> 6; matrix products, arithmetic and copies ran while one was open for 1% -> 3% of each run, Pallas kernels for 0% -> 1%
where the time goes in v3:
time: 171 us
  waiting for transfers between devices  89.3 us (52%)
  starting transfers between devices  57.4 us (34%)
  Pallas kernels  9.91 us (6%)
  local copies, waits for them, and re-layouts  5.09 us (3%)
  matrix products  4.22 us (2%)
  other arithmetic  2.43 us (1%)
  between operations  2.28 us (1%)
    all_to_all x1, waiting for transfers between devices, on_device(): arrived = exchange(dealt, PLANE)  48.5 us
    all_to_all x1, waiting for transfers between devices, on_device(): pieces = exchange(partial.reshape(NX, 2 * width, half), 'x')  22.1 us
    all_to_all x1, starting transfers between devices, on_device(): arrived = exchange(dealt, PLANE)  17.1 us
    all_to_all x1, waiting for transfers between devices, on_device(): seen = exchange(message, SLAB)  10.1 us
    all_to_all x1, starting transfers between devices, on_device(): sums = exchange(jnp.broadcast_to(sums[None], (NF, 2 * NF, width)), LINE)  8.61 us
    all_to_all x1, starting transfers between devices, on_device(): seen = exchange(message, SLAB)  8.5 us
    ppermute x1, starting transfers between devices, on_device(): lax.ppermute(same, SLAB, [(z * NF + f, owner(z, f)) for z in range(NZ) fo...  7.42 us
    all_to_all x1, starting transfers between devices, on_device(): totals = exchange(second, 'y')  7.33 us
  transfers between devices with their start and end apart: 8, of which 6 were waited for; matrix products, arithmetic and copies ran while one was open for 3% of the time, Pallas kernels for 1%

profile of v3, /device:TPU:1, one launch (start us, length us, event | category | flops | bytes accessed | tf_op | source)
XLA Modules:
  0.0 170.6 jit_solution(7195395382104940477)
XLA Ops:
  0.6 2.5 %deal.1 = bf16[64,2,8,1024]{3,2,1,0:T(8,128)(2,1)} custom-call(s32[1]{0:T(128)} %bitcast.5.core_ref, bf16[8,8192]{1,0:T(8,128)(2,1)} %x_ref.1), custom_call_target="tpu_custom_call" | custom-call | tf_op jit(solution)/shard_map/deal/pallas_call | solution.py:226
  3.2 17.1 %all-to-all-start = ((bf16[64,2,8,1024]{3,2,1,0:T(8,128)(2,1)}), bf16[64,2,8,1024]{3,2,1,0:T(8,128)(2,1)S(1)}, u32[]{:S(2)}, u32[]{:S(2)}) async-start(bf16[64,2,8,1024]{3,2,1,0:T(8,128)(2,1)} %deal.1), calls=%async_computation | async-start | bytes 4194304 | tf_op jit(solution)/shard_map/all_to_all | solution.py:233
  20.3 48.5 %all-to-all-done = bf16[64,2,8,1024]{3,2,1,0:T(8,128)(2,1)S(1)} async-done(((bf16[64,2,8,1024]{3,2,1,0:T(8,128)(2,1)}), bf16[64,2,8,1024]{3,2,1,0:T(8,128)(2,1)S(1)}, u32[]{:S(2)}, u32[]{:S(2)}) %all-to-all-start) | async-done | bytes 2097184 | tf_op jit(solution)/shard_map/all_to_all | solution.py:233
  68.8 0.4 convert_reduce_fusion
  69.2 0.6 broadcast_in_dim.5
  69.9 8.6 %all-to-all-start.1 = ((f32[8,16,128]{2,1,0:T(8,128)}), f32[8,16,128]{2,1,0:T(8,128)S(1)}, u32[]{:S(2)}, u32[]{:S(2)}) async-start(f32[8,16,128]{2,1,0:T(8,128)} %broadcast_in_dim.5), calls=%async_computation.1 | async-start | bytes 131072 | tf_op jit(solution)/shard_map/all_to_all | solution.py:239
  78.5 1.9 %collective-permute-start = (bf16[64,2,8,1024]{3,2,1,0:T(8,128)(2,1)S(1)}, bf16[64,2,8,1024]{3,2,1,0:T(8,128)(2,1)}, u32[]{:S(2)}, u32[]{:S(2)}) collective-permute-start(bf16[64,2,8,1024]{3,2,1,0:T(8,128)(2,1)S(1)} %all-to-all-done), channel_id=1, source_target_pairs={{0,1},{1,0},{2,3},{3,2},{4,5},{5,4},{6,7},{7,6},{8,9},{9,8},{10,11... | collective-permute-start | bytes 6291464 | tf_op jit(solution)/shard_map/ppermute | solution.py:235
  80.4 2.9 %all-to-all-done.1 = f32[8,16,128]{2,1,0:T(8,128)S(1)} async-done(((f32[8,16,128]{2,1,0:T(8,128)}), f32[8,16,128]{2,1,0:T(8,128)S(1)}, u32[]{:S(2)}, u32[]{:S(2)}) %all-to-all-start.1) | async-done | bytes 65568 | tf_op jit(solution)/shard_map/all_to_all | solution.py:239
  83.4 0.8 fusion.1
  84.2 0.5 collective-permute-done
  84.7 3.5 %bitcast_add_fusion = f32[1024,512]{1,0:T(8,128)} fusion(f32[1024,512,1]{1,0,2:T(8,128)S(1)} %fusion.1, bf16[64,2,8,1024]{3,2,1,0:T(8,128)(2,1)} %collective-permute-done, f32[1024]{0:T(1024)S(1)} %get-tuple-element.16, f32[512]{0:T(512)S(1)} %slice.71), kind=kOutput, calls=%fused_computation.1 | convolution fusion | flops 539754496 | bytes 5773312 | tf_op jit(solution)/shard_map/dot_general | solution.py:210
  88.1 4.6 %all-to-all-start.2 = ((f32[4,256,512]{2,1,0:T(8,128)}), f32[4,256,512]{2,1,0:T(8,128)}, u32[]{:S(2)}, u32[]{:S(2)}) async-start(f32[4,256,512]{2,1,0:T(8,128)} %bitcast.38), calls=%async_computation.2 | async-start | bytes 4194304 | tf_op jit(solution)/shard_map/all_to_all | solution.py:253
  92.7 0.6 fusion.21
  94.7 0.6 pad_add_fusion.1.place_ref
  95.3 0.1 multiply_reduce_fusion
  95.5 0.5 pad.9.norms_ref
  96.1 0.6 pad.8.mean_ref
  96.7 22.1 %all-to-all-done.2.pieces_ref = f32[4,256,512]{2,1,0:T(8,128)} async-done(((f32[4,256,512]{2,1,0:T(8,128)}), f32[4,256,512]{2,1,0:T(8,128)}, u32[]{:S(2)}, u32[]{:S(2)}) %all-to-all-start.2) | async-done | bytes 2097184 | tf_op jit(solution)/shard_map/all_to_all | solution.py:253
  118.8 3.5 %block_stats.1 = (f32[136,512]{1,0:T(8,128)}, f32[128,512]{1,0:T(8,128)}, f32[64,2,128]{2,1,0:T(2,128)}) custom-call(s32[3]{0:T(128)} %pad_add_fusion.1.place_ref, f32[4,256,512]{2,1,0:T(8,128)} %all-to-all-done.2.pieces_ref, f32[8,512]{1,0:T(8,128)} %pad.8.mean_ref, f32[1,128]{1,0:T(1,128)} %pad.9.norms_ref), custom_call_target="tpu_custom_call" | custom-call | tf_op jit(solution)/shard_map/block_stats/pallas_call | solution.py:272
  122.3 7.4 %collective-permute-start.1 = (f32[136,512]{1,0:T(8,128)}, f32[136,512]{1,0:T(8,128)S(1)}, u32[]{:S(2)}, u32[]{:S(2)}) collective-permute-start(f32[136,512]{1,0:T(8,128)} %get-tuple-element.10), channel_id=1, source_target_pairs={{0,0},{1,32},{2,8},{3,56},{4,16},{5,48},{6,24},{7,40},{8,10},{9,42... | collective-permute-start | bytes 835592 | tf_op jit(solution)/shard_map/ppermute | solution.py:296
  129.7 1.9 %collective-permute-start.2 = (f32[128,512]{1,0:T(8,128)}, f32[128,512]{1,0:T(8,128)S(1)}, u32[]{:S(2)}, u32[]{:S(2)}) collective-permute-start(f32[128,512]{1,0:T(8,128)} %get-tuple-element.11), channel_id=1, source_target_pairs={{0,32},{1,0},{2,56},{3,8},{4,48},{5,16},{6,40},{7,24},{8,42},{9,10... | collective-permute-start | bytes 786440 | tf_op jit(solution)/shard_map/ppermute | solution.py:299
  131.7 8.5 %all-to-all-start.3 = ((f32[64,2,128]{2,1,0:T(2,128)}), f32[64,2,128]{2,1,0:T(2,128)S(1)}, u32[]{:S(2)}, u32[]{:S(2)}) async-start(f32[64,2,128]{2,1,0:T(2,128)} %get-tuple-element.9), calls=%async_computation.3 | async-start | bytes 131072 | tf_op jit(solution)/shard_map/all_to_all | solution.py:291
  140.2 0.6 dynamic_slice.12
  140.8 10.1 %all-to-all-done.3.seen_ref = f32[64,2,128]{2,1,0:T(2,128)S(1)} async-done(((f32[64,2,128]{2,1,0:T(2,128)}), f32[64,2,128]{2,1,0:T(2,128)S(1)}, u32[]{:S(2)}, u32[]{:S(2)}) %all-to-all-start.3) | async-done | bytes 65568 | tf_op jit(solution)/shard_map/all_to_all | solution.py:291
  150.9 0.6 copy-done.2
  151.5 1.7 %middle_stats.1 = f32[8,1,128]{2,1,0:T(1,128)} custom-call(f32[64,2,128]{2,1,0:T(2,128)} %copy-done.2), custom_call_target="tpu_custom_call" | custom-call | tf_op jit(solution)/shard_map/middle_stats/pallas_call | solution.py:302
  153.3 7.3 %all-to-all-start.4 = ((f32[8,1,128]{2,1,0:T(1,128)}), f32[8,1,128]{2,1,0:T(1,128)S(1)}, u32[]{:S(2)}, u32[]{:S(2)}) async-start(f32[8,1,128]{2,1,0:T(1,128)} %middle_stats.1), calls=%async_computation.4 | async-start | bytes 8192 | tf_op jit(solution)/shard_map/all_to_all | solution.py:309
  160.6 1.3 pad_add_fusion.place_ref
  161.8 5.2 %all-to-all-done.4.totals_ref = f32[8,1,128]{2,1,0:T(1,128)S(1)} async-done(((f32[8,1,128]{2,1,0:T(1,128)}), f32[8,1,128]{2,1,0:T(1,128)S(1)}, u32[]{:S(2)}, u32[]{:S(2)}) %all-to-all-start.4) | async-done | bytes 4128 | tf_op jit(solution)/shard_map/all_to_all | solution.py:309
  167.1 0.6 copy-done.3
  167.8 0.7 copy-done
  168.5 2.1 %shrink.1 = (f32[128,1024]{1,0:T(8,128)}, f32[1,1]{1,0:T(1,128)}, f32[8,128]{1,0:T(8,128)}) custom-call(s32[2]{0:T(128)} %pad_add_fusion.place_ref, f32[8,1,128]{2,1,0:T(1,128)} %copy-done.3, f32[136,512]{1,0:T(8,128)} %copy-done, f32[128,512]{1,0:T(8,128)} %copy-done.1), custom_call_target="tpu_custom_call" | custom-call | tf_op jit(solution)/shard_map/shrink/pallas_call | solution.py:315
  (23 shorter events, 0.3 us)
Async XLA Ops:
  3.2 65.6 %all-to-all-start = ((bf16[64,2,8,1024]{3,2,1,0:T(8,128)(2,1)}), bf16[64,2,8,1024]{3,2,1,0:T(8,128)(2,1)S(1)}, u32[]{:S(2)}, u32[]{:S(2)}) async-start(bf16[64,2,8,1024]{3,2,1,0:T(8,128)(2,1)} %deal.1), calls=%async_computation | async-start | bytes 4194304 | tf_op jit(solution)/shard_map/all_to_all | solution.py:233
  69.9 13.5 %all-to-all-start.1 = ((f32[8,16,128]{2,1,0:T(8,128)}), f32[8,16,128]{2,1,0:T(8,128)S(1)}, u32[]{:S(2)}, u32[]{:S(2)}) async-start(f32[8,16,128]{2,1,0:T(8,128)} %broadcast_in_dim.5), calls=%async_computation.1 | async-start | bytes 131072 | tf_op jit(solution)/shard_map/all_to_all | solution.py:239
  78.5 6.2 %collective-permute-start = (bf16[64,2,8,1024]{3,2,1,0:T(8,128)(2,1)S(1)}, bf16[64,2,8,1024]{3,2,1,0:T(8,128)(2,1)}, u32[]{:S(2)}, u32[]{:S(2)}) collective-permute-start(bf16[64,2,8,1024]{3,2,1,0:T(8,128)(2,1)S(1)} %all-to-all-done), channel_id=1, source_target_pairs={{0,1},{1,0},{2,3},{3,2},{4,5},{5,4},{6,7},{7,6},{8,9},{9,8},{10,11... | collective-permute-start | bytes 6291464 | tf_op jit(solution)/shard_map/ppermute | solution.py:235
  88.1 4.6 %copy-start.4 = (s32[8]{0:T(128)S(1)}, s32[8]{0:T(128)}, u32[]{:S(2)}) copy-start(s32[8]{0:T(128)} %constant.118.clone) | copy-start | bytes 100
  88.1 30.7 %all-to-all-start.2 = ((f32[4,256,512]{2,1,0:T(8,128)}), f32[4,256,512]{2,1,0:T(8,128)}, u32[]{:S(2)}, u32[]{:S(2)}) async-start(f32[4,256,512]{2,1,0:T(8,128)} %bitcast.38), calls=%async_computation.2 | async-start | bytes 4194304 | tf_op jit(solution)/shard_map/all_to_all | solution.py:253
  92.7 47.5 %copy-start.5 = (s32[8]{0:T(128)S(1)}, s32[8]{0:T(128)}, u32[]{:S(2)}) copy-start(s32[8]{0:T(128)} %constant.119.clone) | copy-start | bytes 100
  122.3 44.8 %collective-permute-start.1 = (f32[136,512]{1,0:T(8,128)}, f32[136,512]{1,0:T(8,128)S(1)}, u32[]{:S(2)}, u32[]{:S(2)}) collective-permute-start(f32[136,512]{1,0:T(8,128)} %get-tuple-element.10), channel_id=1, source_target_pairs={{0,0},{1,32},{2,8},{3,56},{4,16},{5,48},{6,24},{7,40},{8,10},{9,42... | collective-permute-start | bytes 835592 | tf_op jit(solution)/shard_map/ppermute | solution.py:296
  129.7 37.3 %collective-permute-start.2 = (f32[128,512]{1,0:T(8,128)}, f32[128,512]{1,0:T(8,128)S(1)}, u32[]{:S(2)}, u32[]{:S(2)}) collective-permute-start(f32[128,512]{1,0:T(8,128)} %get-tuple-element.11), channel_id=1, source_target_pairs={{0,32},{1,0},{2,56},{3,8},{4,48},{5,16},{6,40},{7,24},{8,42},{9,10... | collective-permute-start | bytes 786440 | tf_op jit(solution)/shard_map/ppermute | solution.py:299
  131.7 19.2 %all-to-all-start.3 = ((f32[64,2,128]{2,1,0:T(2,128)}), f32[64,2,128]{2,1,0:T(2,128)S(1)}, u32[]{:S(2)}, u32[]{:S(2)}) async-start(f32[64,2,128]{2,1,0:T(2,128)} %get-tuple-element.9), calls=%async_computation.3 | async-start | bytes 131072 | tf_op jit(solution)/shard_map/all_to_all | solution.py:291
  150.9 0.6 copy-start.2
  153.3 13.8 %all-to-all-start.4 = ((f32[8,1,128]{2,1,0:T(1,128)}), f32[8,1,128]{2,1,0:T(1,128)S(1)}, u32[]{:S(2)}, u32[]{:S(2)}) async-start(f32[8,1,128]{2,1,0:T(1,128)} %middle_stats.1), calls=%async_computation.4 | async-start | bytes 8192 | tf_op jit(solution)/shard_map/all_to_all | solution.py:309
  167.1 0.6 copy-start.3
  167.1 0.7 copy-start.1
  167.8 0.7 copy-start

commit v4 on v3

--- a/solution.py
+++ b/solution.py
@@ -7,6 +7,7 @@
 from jax.experimental.pallas import tpu as pltpu
 from jax.sharding import Mesh
 from jax.sharding import PartitionSpec as P
+
 
 PLANE = ("y", "z")
 LINE = ("x", "c")
@@ -19,7 +20,6 @@
 NF = NX * NC
 SHIFT = (0, 4, 1, 7, 2, 6, 3, 5)
 COLUMN = tuple(2 * (z % 4) + z // 4 for z in range(NZ))
-HOLDER = tuple(COLUMN.index(block) for block in range(NZ))
 OFF, SECOND, MEANS = 64, 65, 66
 IN_VMEM = pl.BlockSpec(memory_space=pltpu.VMEM)
 IN_SMEM = pl.BlockSpec(memory_space=pltpu.SMEM)
@@ -210,7 +210,7 @@
     return lax.dot_general(left, right, (((0,), (0,)), ((), ())), preferred_element_type=F32)
 
 
-def on_device(scenarios):
+def shrinkage_step(scenarios):
     row_count, factors = scenarios.shape
     plane = NY * NZ
     total_rows = row_count * plane * NF
@@ -329,7 +329,7 @@
 def solution(mesh):
     finer = Mesh(mesh.devices.reshape(NY, NZ, NX, NC), EVERY)
     return jax.shard_map(
-        on_device,
+        shrinkage_step,
         mesh=finer,
         in_specs=(P(EVERY, None),),
         out_specs=(P(PLANE, LINE), P(), P(LINE)),

time: 171 us -> 171 us (level)
  no operation moved by 1% of the time
where the time goes in v4:
time: 171 us
  waiting for transfers between devices  89.3 us (52%)
  starting transfers between devices  57.4 us (34%)
  Pallas kernels  9.91 us (6%)
  local copies, waits for them, and re-layouts  5.09 us (3%)
  matrix products  4.22 us (2%)
  other arithmetic  2.43 us (1%)
  between operations  2.28 us (1%)
    all_to_all x1, waiting for transfers between devices, shrinkage_step(): arrived = exchange(dealt, PLANE)  48.5 us
    all_to_all x1, waiting for transfers between devices, shrinkage_step(): pieces = exchange(partial.reshape(NX, 2 * width, half), 'x')  22.1 us
    all_to_all x1, starting transfers between devices, shrinkage_step(): arrived = exchange(dealt, PLANE)  17.1 us
    all_to_all x1, waiting for transfers between devices, shrinkage_step(): seen = exchange(message, SLAB)  10.1 us
    all_to_all x1, starting transfers between devices, shrinkage_step(): sums = exchange(jnp.broadcast_to(sums[None], (NF, 2 * NF, width)), LINE)  8.61 us
    all_to_all x1, starting transfers between devices, shrinkage_step(): seen = exchange(message, SLAB)  8.5 us
    ppermute x1, starting transfers between devices, shrinkage_step(): lax.ppermute(same, SLAB, [(z * NF + f, owner(z, f)) for z in range(NZ) fo...  7.42 us
    all_to_all x1, starting transfers between devices, shrinkage_step(): totals = exchange(second, 'y')  7.33 us
  transfers between devices with their start and end apart: 8, of which 6 were waited for; matrix products, arithmetic and copies ran while one was open for 3% of the time, Pallas kernels for 1%

profile of v4, /device:TPU:1, one launch (start us, length us, event | category | flops | bytes accessed | tf_op | source)
XLA Modules:
  0.0 170.6 jit_solution(7195395382104940477)
XLA Ops:
  0.6 2.5 %deal.1 = bf16[64,2,8,1024]{3,2,1,0:T(8,128)(2,1)} custom-call(s32[1]{0:T(128)} %bitcast.5.core_ref, bf16[8,8192]{1,0:T(8,128)(2,1)} %x_ref.1), custom_call_target="tpu_custom_call" | custom-call | tf_op jit(solution)/shard_map/deal/pallas_call | solution.py:226
  3.2 17.1 %all-to-all-start = ((bf16[64,2,8,1024]{3,2,1,0:T(8,128)(2,1)}), bf16[64,2,8,1024]{3,2,1,0:T(8,128)(2,1)S(1)}, u32[]{:S(2)}, u32[]{:S(2)}) async-start(bf16[64,2,8,1024]{3,2,1,0:T(8,128)(2,1)} %deal.1), calls=%async_computation | async-start | bytes 4194304 | tf_op jit(solution)/shard_map/all_to_all | solution.py:233
  20.3 48.5 %all-to-all-done = bf16[64,2,8,1024]{3,2,1,0:T(8,128)(2,1)S(1)} async-done(((bf16[64,2,8,1024]{3,2,1,0:T(8,128)(2,1)}), bf16[64,2,8,1024]{3,2,1,0:T(8,128)(2,1)S(1)}, u32[]{:S(2)}, u32[]{:S(2)}) %all-to-all-start) | async-done | bytes 2097184 | tf_op jit(solution)/shard_map/all_to_all | solution.py:233
  68.8 0.4 convert_reduce_fusion
  69.2 0.6 broadcast_in_dim.5
  69.9 8.6 %all-to-all-start.1 = ((f32[8,16,128]{2,1,0:T(8,128)}), f32[8,16,128]{2,1,0:T(8,128)S(1)}, u32[]{:S(2)}, u32[]{:S(2)}) async-start(f32[8,16,128]{2,1,0:T(8,128)} %broadcast_in_dim.5), calls=%async_computation.1 | async-start | bytes 131072 | tf_op jit(solution)/shard_map/all_to_all | solution.py:239
  78.5 1.9 %collective-permute-start = (bf16[64,2,8,1024]{3,2,1,0:T(8,128)(2,1)S(1)}, bf16[64,2,8,1024]{3,2,1,0:T(8,128)(2,1)}, u32[]{:S(2)}, u32[]{:S(2)}) collective-permute-start(bf16[64,2,8,1024]{3,2,1,0:T(8,128)(2,1)S(1)} %all-to-all-done), channel_id=1, source_target_pairs={{0,1},{1,0},{2,3},{3,2},{4,5},{5,4},{6,7},{7,6},{8,9},{9,8},{10,11... | collective-permute-start | bytes 6291464 | tf_op jit(solution)/shard_map/ppermute | solution.py:235
  80.4 2.9 %all-to-all-done.1 = f32[8,16,128]{2,1,0:T(8,128)S(1)} async-done(((f32[8,16,128]{2,1,0:T(8,128)}), f32[8,16,128]{2,1,0:T(8,128)S(1)}, u32[]{:S(2)}, u32[]{:S(2)}) %all-to-all-start.1) | async-done | bytes 65568 | tf_op jit(solution)/shard_map/all_to_all | solution.py:239
  83.4 0.8 fusion.1
  84.2 0.5 collective-permute-done
  84.7 3.5 %bitcast_add_fusion = f32[1024,512]{1,0:T(8,128)} fusion(f32[1024,512,1]{1,0,2:T(8,128)S(1)} %fusion.1, bf16[64,2,8,1024]{3,2,1,0:T(8,128)(2,1)} %collective-permute-done, f32[1024]{0:T(1024)S(1)} %get-tuple-element.16, f32[512]{0:T(512)S(1)} %slice.71), kind=kOutput, calls=%fused_computation.1 | convolution fusion | flops 539754496 | bytes 5773312 | tf_op jit(solution)/shard_map/dot_general | solution.py:210
  88.1 4.6 %all-to-all-start.2 = ((f32[4,256,512]{2,1,0:T(8,128)}), f32[4,256,512]{2,1,0:T(8,128)}, u32[]{:S(2)}, u32[]{:S(2)}) async-start(f32[4,256,512]{2,1,0:T(8,128)} %bitcast.38), calls=%async_computation.2 | async-start | bytes 4194304 | tf_op jit(solution)/shard_map/all_to_all | solution.py:253
  92.7 0.6 fusion.21
  94.7 0.6 pad_add_fusion.1.place_ref
  95.3 0.1 multiply_reduce_fusion
  95.5 0.5 pad.9.norms_ref
  96.1 0.6 pad.8.mean_ref
  96.7 22.1 %all-to-all-done.2.pieces_ref = f32[4,256,512]{2,1,0:T(8,128)} async-done(((f32[4,256,512]{2,1,0:T(8,128)}), f32[4,256,512]{2,1,0:T(8,128)}, u32[]{:S(2)}, u32[]{:S(2)}) %all-to-all-start.2) | async-done | bytes 2097184 | tf_op jit(solution)/shard_map/all_to_all | solution.py:253
  118.8 3.5 %block_stats.1 = (f32[136,512]{1,0:T(8,128)}, f32[128,512]{1,0:T(8,128)}, f32[64,2,128]{2,1,0:T(2,128)}) custom-call(s32[3]{0:T(128)} %pad_add_fusion.1.place_ref, f32[4,256,512]{2,1,0:T(8,128)} %all-to-all-done.2.pieces_ref, f32[8,512]{1,0:T(8,128)} %pad.8.mean_ref, f32[1,128]{1,0:T(1,128)} %pad.9.norms_ref), custom_call_target="tpu_custom_call" | custom-call | tf_op jit(solution)/shard_map/block_stats/pallas_call | solution.py:272
  122.3 7.4 %collective-permute-start.1 = (f32[136,512]{1,0:T(8,128)}, f32[136,512]{1,0:T(8,128)S(1)}, u32[]{:S(2)}, u32[]{:S(2)}) collective-permute-start(f32[136,512]{1,0:T(8,128)} %get-tuple-element.10), channel_id=1, source_target_pairs={{0,0},{1,32},{2,8},{3,56},{4,16},{5,48},{6,24},{7,40},{8,10},{9,42... | collective-permute-start | bytes 835592 | tf_op jit(solution)/shard_map/ppermute | solution.py:296
  129.7 1.9 %collective-permute-start.2 = (f32[128,512]{1,0:T(8,128)}, f32[128,512]{1,0:T(8,128)S(1)}, u32[]{:S(2)}, u32[]{:S(2)}) collective-permute-start(f32[128,512]{1,0:T(8,128)} %get-tuple-element.11), channel_id=1, source_target_pairs={{0,32},{1,0},{2,56},{3,8},{4,48},{5,16},{6,40},{7,24},{8,42},{9,10... | collective-permute-start | bytes 786440 | tf_op jit(solution)/shard_map/ppermute | solution.py:299
  131.7 8.5 %all-to-all-start.3 = ((f32[64,2,128]{2,1,0:T(2,128)}), f32[64,2,128]{2,1,0:T(2,128)S(1)}, u32[]{:S(2)}, u32[]{:S(2)}) async-start(f32[64,2,128]{2,1,0:T(2,128)} %get-tuple-element.9), calls=%async_computation.3 | async-start | bytes 131072 | tf_op jit(solution)/shard_map/all_to_all | solution.py:291
  140.2 0.6 dynamic_slice.12
  140.8 10.1 %all-to-all-done.3.seen_ref = f32[64,2,128]{2,1,0:T(2,128)S(1)} async-done(((f32[64,2,128]{2,1,0:T(2,128)}), f32[64,2,128]{2,1,0:T(2,128)S(1)}, u32[]{:S(2)}, u32[]{:S(2)}) %all-to-all-start.3) | async-done | bytes 65568 | tf_op jit(solution)/shard_map/all_to_all | solution.py:291
  150.9 0.6 copy-done.2
  151.5 1.7 %middle_stats.1 = f32[8,1,128]{2,1,0:T(1,128)} custom-call(f32[64,2,128]{2,1,0:T(2,128)} %copy-done.2), custom_call_target="tpu_custom_call" | custom-call | tf_op jit(solution)/shard_map/middle_stats/pallas_call | solution.py:302
  153.3 7.3 %all-to-all-start.4 = ((f32[8,1,128]{2,1,0:T(1,128)}), f32[8,1,128]{2,1,0:T(1,128)S(1)}, u32[]{:S(2)}, u32[]{:S(2)}) async-start(f32[8,1,128]{2,1,0:T(1,128)} %middle_stats.1), calls=%async_computation.4 | async-start | bytes 8192 | tf_op jit(solution)/shard_map/all_to_all | solution.py:309
  160.6 1.3 pad_add_fusion.place_ref
  161.8 5.2 %all-to-all-done.4.totals_ref = f32[8,1,128]{2,1,0:T(1,128)S(1)} async-done(((f32[8,1,128]{2,1,0:T(1,128)}), f32[8,1,128]{2,1,0:T(1,128)S(1)}, u32[]{:S(2)}, u32[]{:S(2)}) %all-to-all-start.4) | async-done | bytes 4128 | tf_op jit(solution)/shard_map/all_to_all | solution.py:309
  167.1 0.6 copy-done.3
  167.8 0.7 copy-done
  168.5 2.1 %shrink.1 = (f32[128,1024]{1,0:T(8,128)}, f32[1,1]{1,0:T(1,128)}, f32[8,128]{1,0:T(8,128)}) custom-call(s32[2]{0:T(128)} %pad_add_fusion.place_ref, f32[8,1,128]{2,1,0:T(1,128)} %copy-done.3, f32[136,512]{1,0:T(8,128)} %copy-done, f32[128,512]{1,0:T(8,128)} %copy-done.1), custom_call_target="tpu_custom_call" | custom-call | tf_op jit(solution)/shard_map/shrink/pallas_call | solution.py:315
  (23 shorter events, 0.3 us)
Async XLA Ops:
  3.2 65.6 %all-to-all-start = ((bf16[64,2,8,1024]{3,2,1,0:T(8,128)(2,1)}), bf16[64,2,8,1024]{3,2,1,0:T(8,128)(2,1)S(1)}, u32[]{:S(2)}, u32[]{:S(2)}) async-start(bf16[64,2,8,1024]{3,2,1,0:T(8,128)(2,1)} %deal.1), calls=%async_computation | async-start | bytes 4194304 | tf_op jit(solution)/shard_map/all_to_all | solution.py:233
  69.9 13.5 %all-to-all-start.1 = ((f32[8,16,128]{2,1,0:T(8,128)}), f32[8,16,128]{2,1,0:T(8,128)S(1)}, u32[]{:S(2)}, u32[]{:S(2)}) async-start(f32[8,16,128]{2,1,0:T(8,128)} %broadcast_in_dim.5), calls=%async_computation.1 | async-start | bytes 131072 | tf_op jit(solution)/shard_map/all_to_all | solution.py:239
  78.5 6.2 %collective-permute-start = (bf16[64,2,8,1024]{3,2,1,0:T(8,128)(2,1)S(1)}, bf16[64,2,8,1024]{3,2,1,0:T(8,128)(2,1)}, u32[]{:S(2)}, u32[]{:S(2)}) collective-permute-start(bf16[64,2,8,1024]{3,2,1,0:T(8,128)(2,1)S(1)} %all-to-all-done), channel_id=1, source_target_pairs={{0,1},{1,0},{2,3},{3,2},{4,5},{5,4},{6,7},{7,6},{8,9},{9,8},{10,11... | collective-permute-start | bytes 6291464 | tf_op jit(solution)/shard_map/ppermute | solution.py:235
  88.1 4.6 %copy-start.4 = (s32[8]{0:T(128)S(1)}, s32[8]{0:T(128)}, u32[]{:S(2)}) copy-start(s32[8]{0:T(128)} %constant.118.clone) | copy-start | bytes 100
  88.1 30.7 %all-to-all-start.2 = ((f32[4,256,512]{2,1,0:T(8,128)}), f32[4,256,512]{2,1,0:T(8,128)}, u32[]{:S(2)}, u32[]{:S(2)}) async-start(f32[4,256,512]{2,1,0:T(8,128)} %bitcast.38), calls=%async_computation.2 | async-start | bytes 4194304 | tf_op jit(solution)/shard_map/all_to_all | solution.py:253
  92.7 47.5 %copy-start.5 = (s32[8]{0:T(128)S(1)}, s32[8]{0:T(128)}, u32[]{:S(2)}) copy-start(s32[8]{0:T(128)} %constant.119.clone) | copy-start | bytes 100
  122.3 44.8 %collective-permute-start.1 = (f32[136,512]{1,0:T(8,128)}, f32[136,512]{1,0:T(8,128)S(1)}, u32[]{:S(2)}, u32[]{:S(2)}) collective-permute-start(f32[136,512]{1,0:T(8,128)} %get-tuple-element.10), channel_id=1, source_target_pairs={{0,0},{1,32},{2,8},{3,56},{4,16},{5,48},{6,24},{7,40},{8,10},{9,42... | collective-permute-start | bytes 835592 | tf_op jit(solution)/shard_map/ppermute | solution.py:296
  129.7 37.3 %collective-permute-start.2 = (f32[128,512]{1,0:T(8,128)}, f32[128,512]{1,0:T(8,128)S(1)}, u32[]{:S(2)}, u32[]{:S(2)}) collective-permute-start(f32[128,512]{1,0:T(8,128)} %get-tuple-element.11), channel_id=1, source_target_pairs={{0,32},{1,0},{2,56},{3,8},{4,48},{5,16},{6,40},{7,24},{8,42},{9,10... | collective-permute-start | bytes 786440 | tf_op jit(solution)/shard_map/ppermute | solution.py:299
  131.7 19.2 %all-to-all-start.3 = ((f32[64,2,128]{2,1,0:T(2,128)}), f32[64,2,128]{2,1,0:T(2,128)S(1)}, u32[]{:S(2)}, u32[]{:S(2)}) async-start(f32[64,2,128]{2,1,0:T(2,128)} %get-tuple-element.9), calls=%async_computation.3 | async-start | bytes 131072 | tf_op jit(solution)/shard_map/all_to_all | solution.py:291
  150.9 0.6 copy-start.2
  153.3 13.8 %all-to-all-start.4 = ((f32[8,1,128]{2,1,0:T(1,128)}), f32[8,1,128]{2,1,0:T(1,128)S(1)}, u32[]{:S(2)}, u32[]{:S(2)}) async-start(f32[8,1,128]{2,1,0:T(1,128)} %middle_stats.1), calls=%async_computation.4 | async-start | bytes 8192 | tf_op jit(solution)/shard_map/all_to_all | solution.py:309
  167.1 0.6 copy-start.3
  167.1 0.7 copy-start.1
  167.8 0.7 copy-start

commit v5 on v4

--- a/solution.py
+++ b/solution.py
@@ -21,6 +21,8 @@
 SHIFT = (0, 4, 1, 7, 2, 6, 3, 5)
 COLUMN = tuple(2 * (z % 4) + z // 4 for z in range(NZ))
 OFF, SECOND, MEANS = 64, 65, 66
+HEADER = 8
+F16 = jnp.float16
 IN_VMEM = pl.BlockSpec(memory_space=pltpu.VMEM)
 IN_SMEM = pl.BlockSpec(memory_space=pltpu.SMEM)
 
@@ -51,80 +53,69 @@
     return jnp.sum(jnp.sum(value, axis=1, keepdims=True), axis=0, keepdims=True)
 
 
+def half_power(top):
+    return jnp.clip(jnp.floor(jnp.log2(jnp.maximum(top, 1e-30))), -90.0, 90.0) - 13.0
+
+
 def in_lane(k, value, row):
     slot = lax.broadcasted_iota(jnp.int32, (1, LANES), 1)
     return jnp.where(slot == k, value, row)
 
 
-def block_kernel(
-    place_ref, pieces_ref, mean_ref, norms_ref, same_ref, other_ref, message_ref, off_ref, diag_ref, *, scale
-):
-    step, steps = pl.program_id(0), pl.num_programs(0)
-    rows, half = pieces_ref.shape[1:]
-    width = rows * steps // 2
-    which = step // (steps // 2)
-    base = (step % (steps // 2)) * rows
-    first = place_ref[which]
-    same = place_ref[2] == which
+def block_kernel(place_ref, sum_ref, norms_ref, same_ref, other_ref, message_ref):
+    width, half = same_ref.shape[0] - HEADER, same_ref.shape[1]
     lane = lax.broadcasted_iota(jnp.int32, (8, half), 1)
     sub = lax.broadcasted_iota(jnp.int32, (8, half), 0)
-
-    @pl.when(step == 0)
+    cuts = [slice(j * LANES, (j + 1) * LANES) for j in range(half // LANES)]
+    zero = jnp.zeros((8, LANES), F32)
+    off, top, diagonals = zero, zero, []
+    for j in range(2):
+        diagonal = zero
+        for k in range(width // 8):
+            tile = sum_ref[pl.ds(j * width + k * 8, 8), :]
+            hit = lane == place_ref[j] + k * 8 + sub
+            rest = jnp.where(hit, 0.0, tile)
+            kept = jnp.where(hit, tile, 0.0)
+            squares, size = rest * rest, jnp.abs(tile)
+            for cut in cuts:
+                off = off + squares[:, cut]
+                diagonal = diagonal + kept[:, cut]
+                top = jnp.maximum(top, size[:, cut])
+        diagonals.append(diagonal)
+    top = jnp.max(jnp.max(top, axis=1, keepdims=True), axis=0, keepdims=True)
+    power = half_power(top)
+    factor = jnp.exp2(-power)
+
+    def write(out_ref, j):
+        for k in range(width // 8):
+            out_ref[pl.ds(k * 8, 8), :] = sum_ref[pl.ds(j * width + k * 8, 8), :] * factor
+        out_ref[pl.ds(width, HEADER), :] = jnp.broadcast_to(power, (HEADER, half))
+
+    @pl.when(place_ref[2] == 0)
     def _():
-        off_ref[...] = jnp.zeros_like(off_ref)
-        diag_ref[...] = jnp.zeros_like(diag_ref)
-
-    off = off_ref[...]
-    diagonal = diag_ref[which]
-    tiles = []
-    for k in range(rows // 8):
-        at = pl.ds(k * 8, 8)
-        tile = (pieces_ref[0, at, :] + pieces_ref[1, at, :]) + (
-            pieces_ref[2, at, :] + pieces_ref[3, at, :]
-        )
-        tile = tile * scale
-        tiles.append(tile)
-        hit = lane == first + base + k * 8 + sub
-        rest = jnp.where(hit, 0.0, tile)
-        kept = jnp.where(hit, tile, 0.0)
-        squares = rest * rest
-        for j in range(half // LANES):
-            cut = slice(j * LANES, (j + 1) * LANES)
-            off = off + squares[:, cut]
-            diagonal = diagonal + kept[:, cut]
-    off_ref[...] = off
-    diag_ref[which] = diagonal
-    whole = jnp.concatenate(tiles, axis=0)
-    to = pl.ds(pl.multiple_of(base, 8), rows)
-
-    @pl.when(same)
+        write(same_ref, 0)
+        write(other_ref, 1)
+
+    @pl.when(place_ref[2] == 1)
     def _():
-        same_ref[to, :] = whole
-
-    @pl.when(jnp.logical_not(same))
-    def _():
-        other_ref[to, :] = whole
-
-    @pl.when(step == steps - 1)
-    def _():
-        same_ref[pl.ds(width, 8), :] = mean_ref[...]
-        own = lax.broadcasted_iota(jnp.int32, (8, LANES), 1) % 8 == lax.broadcasted_iota(
-            jnp.int32, (8, LANES), 0
-        )
-        row = in_lane(OFF, add_all(off_ref[...]), norms_ref[...])
-        flags = jnp.zeros((1, LANES), F32)
-        second = jnp.zeros((1, 1), F32)
-        for j in range(2):
-            flag = jnp.where(place_ref[j] >= 0, 1.0, 0.0)
-            mean = add_all(diag_ref[j]) / width
-            apart = jnp.where(own, diag_ref[j] - mean, 0.0)
-            second = second + add_all(apart * apart) * flag
-            row = in_lane(MEANS + j, mean * flag, row)
-            flags = in_lane(MEANS + j, flag, flags)
-        row = in_lane(SECOND, second, row)
-        message_ref[...] = jnp.broadcast_to(
-            jnp.concatenate((row, flags), axis=0)[None], message_ref.shape
-        )
+        write(same_ref, 1)
+        write(other_ref, 0)
+
+    own = lane[:, :LANES] % 8 == sub[:, :LANES]
+    row = in_lane(OFF, add_all(off), norms_ref[...])
+    flags = jnp.zeros((1, LANES), F32)
+    second = jnp.zeros((1, 1), F32)
+    for j in range(2):
+        flag = jnp.where(place_ref[j] >= 0, 1.0, 0.0)
+        mean = add_all(diagonals[j]) / width
+        apart = jnp.where(own, diagonals[j] - mean, 0.0)
+        second = second + add_all(apart * apart) * flag
+        row = in_lane(MEANS + j, mean * flag, row)
+        flags = in_lane(MEANS + j, flag, flags)
+    row = in_lane(SECOND, second, row)
+    message_ref[...] = jnp.broadcast_to(
+        jnp.concatenate((row, flags), axis=0)[None], message_ref.shape
+    )
 
 
 def middle_kernel(seen_ref, message_ref, *, width):
@@ -153,7 +144,7 @@
 
 
 def shrink_kernel(
-    place_ref, totals_ref, same_ref, other_ref, shrunk_ref, value_ref, mean_ref, *, rows, factors
+    place_ref, totals_ref, same_ref, other_ref, shrunk_ref, value_ref, *, rows, factors
 ):
     width, block = shrunk_ref.shape
     half = block // 2
@@ -196,11 +187,6 @@
         write(other_ref, 0)
         write(same_ref, 1)
 
-    for k in range(block // LANES):
-        mean_ref[pl.ds(k, 1), :] = same_ref[
-            pl.ds(width + k * LANES // half, 1), pl.ds(k * LANES % half, LANES)
-        ]
-
 
 def flip(size):
     return [(k, k ^ 1) for k in range(size)]
@@ -250,7 +236,14 @@
     partial = partial + product(
         centred(swapped[:, 0], mean_r), centred(swapped[:, 1, :, half:], mean_half)
     )
-    pieces = exchange(partial.reshape(NX, 2 * width, half), "x")
+    partial = partial * (1.0 / total_rows)
+    power = half_power(jnp.max(jnp.abs(partial)))
+    parcel = jnp.pad(partial.reshape(NX, 2 * width, half), ((0, 0), (0, HEADER), (0, 0)))
+    at_row = lax.broadcasted_iota(jnp.int32, parcel.shape, 1)
+    parcel = jnp.where(at_row < 2 * width, parcel * jnp.exp2(-power), power).astype(F16)
+    pieces = exchange(parcel, "x")
+    powers = jnp.exp2(pieces[:, 2 * width, 0].astype(F32))
+    summed = jnp.sum(pieces[:, : 2 * width].astype(F32) * powers[:, None, None], axis=0)
 
     mine = lax.dynamic_slice_in_dim(arrived, y_idx * NZ, NZ, 0)[:, 1]
     mine = (mine.astype(F32) - mean_own).astype(BF16).astype(F32)
@@ -266,39 +259,32 @@
         held = (y_idx == column) & (piece // 4 == c_idx)
         places.append(jnp.where(held, (piece % 4) * width, never))
     places.append(c_idx)
-    steps = 4
-    mean_rows = jnp.pad(mean_c.reshape(2, half), ((0, 6), (0, 0)))
-    whole = lambda *dims: pl.BlockSpec(dims, lambda i: (0,) * len(dims))
     same, other, message = pl.pallas_call(
-        functools.partial(block_kernel, scale=1.0 / total_rows),
-        grid=(steps,),
+        block_kernel,
         out_shape=(
-            shapes((width + 8, half), F32),
-            shapes((width, half), F32),
+            shapes((width + HEADER, half), F32),
+            shapes((width + HEADER, half), F32),
             shapes((NZ * NF, 2, LANES), F32),
         ),
-        in_specs=[
-            IN_SMEM,
-            pl.BlockSpec((NX, 2 * width // steps, half), lambda i: (0, i, 0)),
-            whole(8, half),
-            whole(1, LANES),
-        ],
-        out_specs=(whole(width + 8, half), whole(width, half), whole(NZ * NF, 2, LANES)),
-        scratch_shapes=[pltpu.VMEM((8, LANES), F32), pltpu.VMEM((2, 8, LANES), F32)],
+        in_specs=[IN_SMEM, IN_VMEM, IN_VMEM],
+        out_specs=(IN_VMEM, IN_VMEM, IN_VMEM),
         name="block_stats",
-    )(jnp.stack(places), pieces, mean_rows, norms)
+    )(jnp.stack(places), summed, norms)
 
     seen = exchange(message, SLAB)
 
     def owner(z, f):
         return ((z + SHIFT[f]) % NZ) * NF + COLUMN[z]
 
-    own_same = lax.ppermute(
-        same, SLAB, [(z * NF + f, owner(z, f)) for z in range(NZ) for f in range(NF)]
-    )
-    own_other = lax.ppermute(
-        other, SLAB, [(z * NF + f, owner(z, f ^ 1)) for z in range(NZ) for f in range(NF)]
-    )
+    to_same = [(z * NF + f, owner(z, f)) for z in range(NZ) for f in range(NF)]
+    to_other = [(z * NF + f, owner(z, f ^ 1)) for z in range(NZ) for f in range(NF)]
+
+    def unpack(block):
+        return block[:width].astype(F32) * jnp.exp2(block[width, 0].astype(F32))
+
+    own_same = unpack(lax.ppermute(same.astype(F16), SLAB, to_same))
+    own_other = unpack(lax.ppermute(other.astype(F16), SLAB, to_other))
+    col_mean = lax.ppermute(mean_c.reshape(NF, width), SLAB, to_same).reshape(block)
     second = pl.pallas_call(
         functools.partial(middle_kernel, width=width),
         out_shape=shapes((NY, 1, LANES), F32),
@@ -312,18 +298,17 @@
     core_of = jnp.array([SHIFT.index(s) % 2 for s in range(NZ)], jnp.int32)
     from_z = f_idx // 2 + 4 * (f_idx % 2)
     which_own = core_of[(z_idx - from_z) % NZ]
-    shrunk, shrinkage, col_mean = pl.pallas_call(
+    shrunk, shrinkage = pl.pallas_call(
         functools.partial(shrink_kernel, rows=total_rows, factors=factors),
         out_shape=(
             shapes((width, block), F32),
             shapes((1, 1), F32),
-            shapes((block // LANES, LANES), F32),
         ),
         in_specs=[IN_SMEM, IN_VMEM, IN_VMEM, IN_VMEM],
-        out_specs=(IN_VMEM, IN_VMEM, IN_VMEM),
+        out_specs=(IN_VMEM, IN_VMEM),
         name="shrink",
     )(jnp.stack((first_own, which_own)), totals, own_same, own_other)
-    return (shrunk, shrinkage.reshape(()), col_mean.reshape(block))
+    return (shrunk, shrinkage.reshape(()), col_mean)
 
 
 def solution(mesh):

time: 171 us -> 165 us (0.965)
  waiting for transfers between devices: 89.3 us -> 66.6 us
  other arithmetic: 2.43 us -> 9.99 us
  starting transfers between devices: 57.4 us -> 64.7 us
  between operations: 2.28 us -> 4.41 us
    all_to_all x1, waiting for transfers between devices: 22.1 us -> 11.6 us  [shrinkage_step(): pieces = exchange(parcel, 'x')]
    all_to_all x1, waiting for transfers between devices: 10.1 us -> 0.6 us  [shrinkage_step(): seen = exchange(message, SLAB)]
    ppermute x2 -> x3, starting transfers between devices: 9.34 us -> 17.1 us  [the longest x1 7.69 us: shrinkage_step(): own_same = unpack(lax.ppermute(same.astype(F16), SLAB, to_same))]
    convert_element_type x0 -> x3, other arithmetic: none -> 4.84 us  [the longest x1 2.88 us: shrinkage_step(): jnp.where(at_row < 2 * width, parcel * jnp.exp2(-power), power).astype(F16)]
    all_to_all x1, waiting for transfers between devices: 5.23 us -> 2.57 us  [shrinkage_step(): totals = exchange(second, 'y')]
  transfers between devices with their start and end apart: 8 -> 9, of which waited for: 6 -> 6; matrix products, arithmetic and copies ran while one was open for 3% -> 5% of each run, Pallas kernels for 1% -> 1%
where the time goes in v5:
time: 165 us; the launch traced here: 164 us
  waiting for transfers between devices  66.6 us (40%)
  starting transfers between devices  64.7 us (39%)
  other arithmetic  9.99 us (6%)
  Pallas kernels  8.55 us (5%)
  local copies, waits for them, and re-layouts  5.3 us (3%)
  matrix products  4.84 us (3%)
  between operations  4.41 us (3%)
    all_to_all x1, waiting for transfers between devices, shrinkage_step(): arrived = exchange(dealt, PLANE)  48.5 us
    all_to_all x1, starting transfers between devices, shrinkage_step(): arrived = exchange(dealt, PLANE)  17.1 us
    all_to_all x1, waiting for transfers between devices, shrinkage_step(): pieces = exchange(parcel, 'x')  11.6 us
    all_to_all x1, starting transfers between devices, shrinkage_step(): sums = exchange(jnp.broadcast_to(sums[None], (NF, 2 * NF, width)), LINE)  8.61 us
    all_to_all x1, starting transfers between devices, shrinkage_step(): seen = exchange(message, SLAB)  8.5 us
    ppermute x1, starting transfers between devices, shrinkage_step(): own_same = unpack(lax.ppermute(same.astype(F16), SLAB, to_same))  7.69 us
    ppermute x1, starting transfers between devices, shrinkage_step(): lax.ppermute(mean_c.reshape(NF, width), SLAB, to_same).reshape(block)  7.53 us
    all_to_all x1, starting transfers between devices, shrinkage_step(): totals = exchange(second, 'y')  7.26 us
  transfers between devices with their start and end apart: 9, of which 6 were waited for; matrix products, arithmetic and copies ran while one was open for 5% of the time, Pallas kernels for 1%

profile of v5, /device:TPU:1, one launch (start us, length us, event | category | flops | bytes accessed | tf_op | source)
XLA Modules:
  0.0 164.4 jit_solution(18400353982974951398)
XLA Ops:
  0.6 2.5 %deal.1 = bf16[64,2,8,1024]{3,2,1,0:T(8,128)(2,1)} custom-call(s32[1]{0:T(128)} %bitcast.5.core_ref, bf16[8,8192]{1,0:T(8,128)(2,1)} %x_ref.1), custom_call_target="tpu_custom_call" | custom-call | tf_op jit(solution)/shard_map/deal/pallas_call | solution.py:212
  3.2 17.1 %all-to-all-start = ((bf16[64,2,8,1024]{3,2,1,0:T(8,128)(2,1)}), bf16[64,2,8,1024]{3,2,1,0:T(8,128)(2,1)S(1)}, u32[]{:S(2)}, u32[]{:S(2)}) async-start(bf16[64,2,8,1024]{3,2,1,0:T(8,128)(2,1)} %deal.1), calls=%async_computation | async-start | bytes 4194304 | tf_op jit(solution)/shard_map/all_to_all | solution.py:219
  20.3 48.5 %all-to-all-done = bf16[64,2,8,1024]{3,2,1,0:T(8,128)(2,1)S(1)} async-done(((bf16[64,2,8,1024]{3,2,1,0:T(8,128)(2,1)}), bf16[64,2,8,1024]{3,2,1,0:T(8,128)(2,1)S(1)}, u32[]{:S(2)}, u32[]{:S(2)}) %all-to-all-start) | async-done | bytes 2097184 | tf_op jit(solution)/shard_map/all_to_all | solution.py:219
  69.2 0.6 broadcast_in_dim.16
  69.9 8.6 %all-to-all-start.1 = ((f32[8,16,128]{2,1,0:T(8,128)}), f32[8,16,128]{2,1,0:T(8,128)S(1)}, u32[]{:S(2)}, u32[]{:S(2)}) async-start(f32[8,16,128]{2,1,0:T(8,128)} %broadcast_in_dim.16), calls=%async_computation.1 | async-start | bytes 131072 | tf_op jit(solution)/shard_map/all_to_all | solution.py:225
  78.5 1.9 %collective-permute-start = (bf16[64,2,8,1024]{3,2,1,0:T(8,128)(2,1)S(1)}, bf16[64,2,8,1024]{3,2,1,0:T(8,128)(2,1)}, u32[]{:S(2)}, u32[]{:S(2)}) collective-permute-start(bf16[64,2,8,1024]{3,2,1,0:T(8,128)(2,1)S(1)} %all-to-all-done), channel_id=1, source_target_pairs={{0,1},{1,0},{2,3},{3,2},{4,5},{5,4},{6,7},{7,6},{8,9},{9,8},{10,11... | collective-permute-start | bytes 6291464 | tf_op jit(solution)/shard_map/ppermute | solution.py:221
  80.4 2.9 %all-to-all-done.1 = f32[8,16,128]{2,1,0:T(8,128)S(1)} async-done(((f32[8,16,128]{2,1,0:T(8,128)}), f32[8,16,128]{2,1,0:T(8,128)S(1)}, u32[]{:S(2)}, u32[]{:S(2)}) %all-to-all-start.1) | async-done | bytes 65568 | tf_op jit(solution)/shard_map/all_to_all | solution.py:225
  83.4 0.8 fusion.2
  84.7 4.1 %abs_reduce_fusion = (f32[]{:T(128)}, f32[1024,512]{1,0:T(8,128)}) fusion(bf16[64,2,8,1024]{3,2,1,0:T(8,128)(2,1)} %collective-permute-done, f32[512]{0:T(512)S(1)} %slice.89, f32[1024]{0:T(1024)S(1)} %get-tuple-element.14, f32[1024,512,1]{1,0,2:T(8,128)S(1)} %fusion.2), kind=kOutput, calls=%fused_computation.5 | convolution fusion | flops 541327360 | bytes 5773316 | tf_op jit(solution)/shard_map/dot_general | solution.py:196
  89.5 2.9 %select_convert_fusion = f16[4,264,512]{2,1,0:T(8,128)(2,1)} fusion(f32[4,256,512]{2,1,0:T(8,128)} %bitcast.46, f32[]{:T(128)S(6)} %sub.73, f32[]{:T(128)S(6)} %exp2.35, pred[264]{0:T(512)(128)(4,1)S(1)} %iota_compare_fusion), kind=kLoop, calls=%fused_computation.1 | loop fusion | flops 1622016 | bytes 3178768 | tf_op jit(solution)/shard_map/convert_element_type | solution.py:243
  92.4 4.1 %all-to-all-start.2 = ((f16[4,264,512]{2,1,0:T(8,128)(2,1)}), f16[4,264,512]{2,1,0:T(8,128)(2,1)S(1)}, u32[]{:S(2)}, u32[]{:S(2)}) async-start(f16[4,264,512]{2,1,0:T(8,128)(2,1)} %select_convert_fusion), calls=%async_computation.2 | async-start | bytes 2162688 | tf_op jit(solution)/shard_map/all_to_all | solution.py:244
  96.5 0.6 fusion.25
  99.8 11.6 %all-to-all-done.2 = f16[4,264,512]{2,1,0:T(8,128)(2,1)S(1)} async-done(((f16[4,264,512]{2,1,0:T(8,128)(2,1)}), f16[4,264,512]{2,1,0:T(8,128)(2,1)S(1)}, u32[]{:S(2)}, u32[]{:S(2)}) %all-to-all-start.2) | async-done | bytes 1081376 | tf_op jit(solution)/shard_map/all_to_all | solution.py:244
  111.5 1.1 multiply_reduce_fusion.sum_ref
  112.7 2.2 %block_stats.1 = (f32[136,512]{1,0:T(8,128)}, f32[136,512]{1,0:T(8,128)}, f32[64,2,128]{2,1,0:T(2,128)}) custom-call(s32[3]{0:T(128)} %pad_add_fusion.1.place_ref, f32[256,512]{1,0:T(8,128)} %multiply_reduce_fusion.sum_ref, f32[1,128]{1,0:T(1,128)} %pad.9.norms_ref), custom_call_target="tpu_custom_call" | custom-call | tf_op jit(solution)/shard_map/block_stats/pallas_call | solution.py:262
  114.8 1.0 convert_element_type.109
  115.8 7.7 %collective-permute-start.1 = (f16[136,512]{1,0:T(8,128)(2,1)S(1)}, f16[136,512]{1,0:T(8,128)(2,1)S(1)}, u32[]{:S(2)}, u32[]{:S(2)}) collective-permute-start(f16[136,512]{1,0:T(8,128)(2,1)S(1)} %convert_element_type.109), channel_id=1, source_target_pairs={{0,0},{1,32},{2,8},{3,56},{4,16},{5,48},{6,24},{7,40},{8,10},{9,42... | collective-permute-start | bytes 417800 | tf_op jit(solution)/shard_map/ppermute | solution.py:285
  123.5 1.0 convert_element_type.112
  124.5 1.9 %collective-permute-start.2 = (f16[136,512]{1,0:T(8,128)(2,1)S(1)}, f16[136,512]{1,0:T(8,128)(2,1)S(1)}, u32[]{:S(2)}, u32[]{:S(2)}) collective-permute-start(f16[136,512]{1,0:T(8,128)(2,1)S(1)} %convert_element_type.112), channel_id=1, source_target_pairs={{0,32},{1,0},{2,56},{3,8},{4,48},{5,16},{6,40},{7,24},{8,42},{9,10... | collective-permute-start | bytes 417800 | tf_op jit(solution)/shard_map/ppermute | solution.py:286
  126.4 8.5 %all-to-all-start.3 = ((f32[64,2,128]{2,1,0:T(2,128)}), f32[64,2,128]{2,1,0:T(2,128)S(1)}, u32[]{:S(2)}, u32[]{:S(2)}) async-start(f32[64,2,128]{2,1,0:T(2,128)} %get-tuple-element.8), calls=%async_computation.3 | async-start | bytes 131072 | tf_op jit(solution)/shard_map/all_to_all | solution.py:274
  135.6 7.5 %collective-permute-start.3 = (f32[8,128]{1,0:T(8,128)S(1)}, f32[8,128]{1,0:T(8,128)S(1)}, u32[]{:S(2)}, u32[]{:S(2)}) collective-permute-start(f32[8,128]{1,0:T(8,128)S(1)} %get-tuple-element.13), channel_id=1, source_target_pairs={{0,0},{1,32},{2,8},{3,56},{4,16},{5,48},{6,24},{7,40},{8,10},{9,42... | collective-permute-start | bytes 12296 | tf_op jit(solution)/shard_map/ppermute | solution.py:287
  143.1 1.3 pad_add_fusion.place_ref
  144.4 0.6 all-to-all-done.3.seen_ref
  145.0 0.6 copy-done
  145.6 1.7 %middle_stats.1 = f32[8,1,128]{2,1,0:T(1,128)} custom-call(f32[64,2,128]{2,1,0:T(2,128)} %copy-done), custom_call_target="tpu_custom_call" | custom-call | tf_op jit(solution)/shard_map/middle_stats/pallas_call | solution.py:288
  147.4 7.3 %all-to-all-start.4 = ((f32[8,1,128]{2,1,0:T(1,128)}), f32[8,1,128]{2,1,0:T(1,128)S(1)}, u32[]{:S(2)}, u32[]{:S(2)}) async-start(f32[8,1,128]{2,1,0:T(1,128)} %middle_stats.1), calls=%async_computation.4 | async-start | bytes 8192 | tf_op jit(solution)/shard_map/all_to_all | solution.py:295
  157.1 0.7 convert_multiply_fusion.1.same_ref
  157.8 0.7 convert_multiply_fusion.other_ref
  158.6 2.6 %all-to-all-done.4.totals_ref = f32[8,1,128]{2,1,0:T(1,128)S(1)} async-done(((f32[8,1,128]{2,1,0:T(1,128)}), f32[8,1,128]{2,1,0:T(1,128)S(1)}, u32[]{:S(2)}, u32[]{:S(2)}) %all-to-all-start.4) | async-done | bytes 4128 | tf_op jit(solution)/shard_map/all_to_all | solution.py:295
  161.1 0.6 copy-done.1
  161.7 2.1 %shrink.1 = (f32[128,1024]{1,0:T(8,128)}, f32[1,1]{1,0:T(1,128)}) custom-call(s32[2]{0:T(128)} %pad_add_fusion.place_ref, f32[8,1,128]{2,1,0:T(1,128)} %copy-done.1, f32[128,512]{1,0:T(8,128)} %convert_multiply_fusion.1.same_ref, f32[128,512]{1,0:T(8,128)} %convert_multiply_fusion.other_ref), custom_call_target="tpu_custom_call" | custom-call | tf_op jit(solution)/shard_map/shrink/pallas_call | solution.py:301
  163.8 0.6 copy.16
  (30 shorter events, 4.0 us)
Async XLA Ops:
  3.2 65.6 %all-to-all-start = ((bf16[64,2,8,1024]{3,2,1,0:T(8,128)(2,1)}), bf16[64,2,8,1024]{3,2,1,0:T(8,128)(2,1)S(1)}, u32[]{:S(2)}, u32[]{:S(2)}) async-start(bf16[64,2,8,1024]{3,2,1,0:T(8,128)(2,1)} %deal.1), calls=%async_computation | async-start | bytes 4194304 | tf_op jit(solution)/shard_map/all_to_all | solution.py:219
  69.9 13.5 %all-to-all-start.1 = ((f32[8,16,128]{2,1,0:T(8,128)}), f32[8,16,128]{2,1,0:T(8,128)S(1)}, u32[]{:S(2)}, u32[]{:S(2)}) async-start(f32[8,16,128]{2,1,0:T(8,128)} %broadcast_in_dim.16), calls=%async_computation.1 | async-start | bytes 131072 | tf_op jit(solution)/shard_map/all_to_all | solution.py:225
  78.5 6.2 %collective-permute-start = (bf16[64,2,8,1024]{3,2,1,0:T(8,128)(2,1)S(1)}, bf16[64,2,8,1024]{3,2,1,0:T(8,128)(2,1)}, u32[]{:S(2)}, u32[]{:S(2)}) collective-permute-start(bf16[64,2,8,1024]{3,2,1,0:T(8,128)(2,1)S(1)} %all-to-all-done), channel_id=1, source_target_pairs={{0,1},{1,0},{2,3},{3,2},{4,5},{5,4},{6,7},{7,6},{8,9},{9,8},{10,11... | collective-permute-start | bytes 6291464 | tf_op jit(solution)/shard_map/ppermute | solution.py:221
  89.5 7.0 %copy-start.2 = (s32[8]{0:T(128)S(1)}, s32[8]{0:T(128)}, u32[]{:S(2)}) copy-start(s32[8]{0:T(128)} %constant.140.clone) | copy-start | bytes 100
  92.4 19.0 %all-to-all-start.2 = ((f16[4,264,512]{2,1,0:T(8,128)(2,1)}), f16[4,264,512]{2,1,0:T(8,128)(2,1)S(1)}, u32[]{:S(2)}, u32[]{:S(2)}) async-start(f16[4,264,512]{2,1,0:T(8,128)(2,1)} %select_convert_fusion), calls=%async_computation.2 | async-start | bytes 2162688 | tf_op jit(solution)/shard_map/all_to_all | solution.py:244
  96.5 38.5 %copy-start.3 = (s32[8]{0:T(128)S(1)}, s32[8]{0:T(128)}, u32[]{:S(2)}) copy-start(s32[8]{0:T(128)} %constant.141.clone) | copy-start | bytes 100
  115.8 38.8 %collective-permute-start.1 = (f16[136,512]{1,0:T(8,128)(2,1)S(1)}, f16[136,512]{1,0:T(8,128)(2,1)S(1)}, u32[]{:S(2)}, u32[]{:S(2)}) collective-permute-start(f16[136,512]{1,0:T(8,128)(2,1)S(1)} %convert_element_type.109), channel_id=1, source_target_pairs={{0,0},{1,32},{2,8},{3,56},{4,16},{5,48},{6,24},{7,40},{8,10},{9,42... | collective-permute-start | bytes 417800 | tf_op jit(solution)/shard_map/ppermute | solution.py:285
  124.5 31.4 %collective-permute-start.2 = (f16[136,512]{1,0:T(8,128)(2,1)S(1)}, f16[136,512]{1,0:T(8,128)(2,1)S(1)}, u32[]{:S(2)}, u32[]{:S(2)}) collective-permute-start(f16[136,512]{1,0:T(8,128)(2,1)S(1)} %convert_element_type.112), channel_id=1, source_target_pairs={{0,32},{1,0},{2,56},{3,8},{4,48},{5,16},{6,40},{7,24},{8,42},{9,10... | collective-permute-start | bytes 417800 | tf_op jit(solution)/shard_map/ppermute | solution.py:286
  126.4 18.6 %all-to-all-start.3 = ((f32[64,2,128]{2,1,0:T(2,128)}), f32[64,2,128]{2,1,0:T(2,128)S(1)}, u32[]{:S(2)}, u32[]{:S(2)}) async-start(f32[64,2,128]{2,1,0:T(2,128)} %get-tuple-element.8), calls=%async_computation.3 | async-start | bytes 131072 | tf_op jit(solution)/shard_map/all_to_all | solution.py:274
  135.6 8.8 %collective-permute-start.3 = (f32[8,128]{1,0:T(8,128)S(1)}, f32[8,128]{1,0:T(8,128)S(1)}, u32[]{:S(2)}, u32[]{:S(2)}) collective-permute-start(f32[8,128]{1,0:T(8,128)S(1)} %get-tuple-element.13), channel_id=1, source_target_pairs={{0,0},{1,32},{2,8},{3,56},{4,16},{5,48},{6,24},{7,40},{8,10},{9,42... | collective-permute-start | bytes 12296 | tf_op jit(solution)/shard_map/ppermute | solution.py:287
  145.0 0.6 copy-start
  147.4 13.7 %all-to-all-start.4 = ((f32[8,1,128]{2,1,0:T(1,128)}), f32[8,1,128]{2,1,0:T(1,128)S(1)}, u32[]{:S(2)}, u32[]{:S(2)}) async-start(f32[8,1,128]{2,1,0:T(1,128)} %middle_stats.1), calls=%async_computation.4 | async-start | bytes 8192 | tf_op jit(solution)/shard_map/all_to_all | solution.py:295
  161.1 0.6 copy-start.1

commit v6 on v5

v6 whole, which is shorter than its diff:
```python
import functools

import jax
import jax.numpy as jnp
from jax import lax
from jax.experimental import pallas as pl
from jax.experimental.pallas import tpu as pltpu
from jax.sharding import Mesh
from jax.sharding import PartitionSpec as P


PLANE = ("y", "z")
LINE = ("x", "c")
SLAB = ("z", "x", "c")
EVERY = ("y", "z", "x", "c")
F32 = jnp.float32
BF16 = jnp.bfloat16
LANES = 128
NY, NZ, NX, NC = 8, 8, 4, 2
NF = NX * NC
SHIFT = (0, 4, 1, 7, 2, 6, 3, 5)
COLUMN = tuple(2 * (z % 4) + z // 4 for z in range(NZ))
OFF, SECOND, MEANS = 64, 65, 66
F16 = jnp.float16
IN_VMEM = pl.BlockSpec(memory_space=pltpu.VMEM)
IN_SMEM = pl.BlockSpec(memory_space=pltpu.SMEM)


def deal_kernel(core_ref, x_ref, out_ref):
    block = out_ref.shape[3]

    def take(start, size):
        return x_ref[:, pl.ds(pl.multiple_of(start, LANES), size)]

    def deal(core):
        order = [2 * x + core for x in range(NX)] + [2 * x + 1 - core for x in range(NX)]

        def one(y, carry):
            for z in range(NZ):
                to = y * NZ + z
                for place, f in enumerate(order):
                    start = y * block + ((z + SHIFT[f]) % NZ) * LANES
                    out_ref[to, 0, :, pl.ds(place * LANES, LANES)] = take(start, LANES)
                out_ref[to, 1] = take(COLUMN[z] * block, block)
            return carry

        lax.fori_loop(0, NY, one, 0)

    for core in range(NC):
        pl.when(core_ref[0] == core)(functools.partial(deal, core))


def add_all(value):
    return jnp.sum(jnp.sum(value, axis=1, keepdims=True), axis=0, keepdims=True)


def half_power(top):
    return jnp.clip(jnp.floor(jnp.log2(jnp.maximum(top, 1e-30))), -90.0, 90.0) - 13.0


def in_lane(k, value, row):
    slot = lax.broadcasted_iota(jnp.int32, (1, LANES), 1)
    return jnp.where(slot == k, value, row)


def block_kernel(place_ref, sum_ref, norms_ref, factor_ref, message_ref):
    width, block = sum_ref.shape
    lane = lax.broadcasted_iota(jnp.int32, (8, block), 1)
    sub = lax.broadcasted_iota(jnp.int32, (8, block), 0)
    first, factor = place_ref[0], factor_ref[0]
    zero = jnp.zeros((8, LANES), F32)
    off, diagonal = zero, zero
    for k in range(width // 8):
        tile = sum_ref[pl.ds(k * 8, 8), :] * factor
        hit = lane == first + k * 8 + sub
        rest = jnp.where(hit, 0.0, tile)
        kept = jnp.where(hit, tile, 0.0)
        squares = rest * rest
        for j in range(block // LANES):
            cut = slice(j * LANES, (j + 1) * LANES)
            off = off + squares[:, cut]
            diagonal = diagonal + kept[:, cut]
    own = lane[:, :LANES] % 8 == sub[:, :LANES]
    flag = jnp.where(first >= 0, 1.0, 0.0)
    mean = add_all(diagonal) / width
    apart = jnp.where(own, diagonal - mean, 0.0)
    row = in_lane(OFF, add_all(off), norms_ref[...])
    row = in_lane(SECOND, add_all(apart * apart) * flag, row)
    row = in_lane(MEANS, mean * flag, row)
    flags = in_lane(MEANS, flag, jnp.zeros((1, LANES), F32))
    message_ref[...] = jnp.broadcast_to(
        jnp.concatenate((row, flags), axis=0)[None], message_ref.shape
    )


def middle_kernel(seen_ref, message_ref, *, width):
    seen = seen_ref[...]
    slot = lax.broadcasted_iota(jnp.int32, (1, 1, LANES), 2)
    values, flags = seen[:, 0:1, :], seen[:, 1:2, :]
    norms = jnp.sum(values.reshape(NZ, NF, 1, LANES), axis=0)
    norms = jnp.where(slot < OFF, norms, 0.0)
    total = jnp.sum(values, axis=0)
    is_mean = slot == MEANS

    def lanes(row):
        return jnp.sum(row, axis=1, keepdims=True)

    mean = lanes(jnp.where(is_mean[0], total, 0.0)) / NF
    apart = jnp.where(is_mean, (values - mean[None]) * flags, 0.0)
    between = lanes(jnp.sum(apart * apart, axis=0))
    second = lanes(jnp.where(slot[0] == SECOND, total, 0.0)) + width * between
    row = jnp.zeros((1, LANES), F32)
    row = in_lane(0, lanes(jnp.sum(norms, axis=0)), row)
    row = in_lane(1, lanes(jnp.sum(norms * norms, axis=0)), row)
    row = in_lane(2, lanes(jnp.where(slot[0] == OFF, total, 0.0)), row)
    row = in_lane(3, mean, row)
    row = in_lane(4, second, row)
    message_ref[...] = jnp.broadcast_to(row[None], message_ref.shape)


def shrink_kernel(place_ref, factor_ref, totals_ref, owned_ref, shrunk_ref, value_ref, *, rows, factors):
    width, block = shrunk_ref.shape
    first = place_ref[0]
    slot = lax.broadcasted_iota(jnp.int32, (1, LANES), 1)
    totals = totals_ref[...]
    sums = jnp.sum(totals, axis=0)

    def pick(row, k):
        return jnp.sum(jnp.where(slot == k, row, 0.0), axis=1, keepdims=True)

    mu_scale = pick(sums, 0) / (rows * factors)
    apart = totals - mu_scale[None]
    from_mu = pick(jnp.sum(apart * apart, axis=0), 3)
    spread = (pick(sums, 2) + pick(sums, 4) + block * from_mu) / factors
    norm_sq = factors * (spread + mu_scale * mu_scale)
    beta_value = (pick(sums, 1) / rows - norm_sq) / (factors * rows)
    shrinkage = beta_value / spread
    value_ref[...] = shrinkage
    keep = (1.0 - shrinkage) * factor_ref[0]
    lift = shrinkage * mu_scale
    lane = lax.broadcasted_iota(jnp.int32, (8, block), 1)
    sub = lax.broadcasted_iota(jnp.int32, (8, block), 0)
    for k in range(width // 8):
        at = pl.ds(k * 8, 8)
        hit = lane == first + k * 8 + sub
        shrunk_ref[at, :] = keep * owned_ref[at, :] + jnp.where(hit, lift, 0.0)


def flip(size):
    return [(k, k ^ 1) for k in range(size)]


def product(left, right):
    return lax.dot_general(left, right, (((0,), (0,)), ((), ())), preferred_element_type=F32)


def shrinkage_step(scenarios):
    row_count, factors = scenarios.shape
    plane = NY * NZ
    total_rows = row_count * plane * NF
    part_rows = row_count * plane
    block = factors // NY
    half, width = block // 2, block // NF
    y_idx, z_idx = lax.axis_index("y"), lax.axis_index("z")
    x_idx, c_idx = lax.axis_index("x"), lax.axis_index("c")
    f_idx = x_idx * NC + c_idx
    exchange = functools.partial(lax.all_to_all, split_axis=0, concat_axis=0, tiled=True)
    shapes = jax.ShapeDtypeStruct

    dealt = pl.pallas_call(
        deal_kernel,
        out_shape=shapes((plane, 2, row_count, block), BF16),
        in_specs=[IN_SMEM, IN_VMEM],
        out_specs=IN_VMEM,
        name="deal",
    )(c_idx.reshape(1), scenarios)
    arrived = exchange(dealt, PLANE)

    swapped = lax.ppermute(arrived, "c", flip(NC))
    values = arrived.astype(F32)
    sums = jnp.sum(values, axis=(0, 2))
    wide = jnp.max(jnp.abs(values - values[:1, :, :1]), axis=(0, 2))
    sums_r = jnp.where(c_idx == 0, sums[0], jnp.roll(sums[0], half))
    told = jnp.concatenate((sums_r.reshape(NF, width), sums[1].reshape(NF, width)))
    told = jnp.concatenate((told, jnp.broadcast_to(jnp.max(wide), (8, width))))
    told = exchange(jnp.broadcast_to(told[None], (NF, *told.shape)), LINE)
    part = told[:, : 2 * NF] / part_rows
    means = jnp.sum(told[:, : 2 * NF], axis=0) / total_rows
    reach = 2.0 * jnp.max(told[:, 2 * NF]) + jnp.max(jnp.abs(part - means))
    power = half_power(reach * reach)
    mean_c = means[NF:].reshape(block)
    mean_r = means[:NF].reshape(2, half)
    mean_half = jnp.where(c_idx == 0, mean_r[0], mean_r[1])

    def centred(rows, mean):
        out = (rows.astype(F32) - mean).astype(BF16)
        return out.reshape(part_rows, out.shape[-1])

    partial = product(centred(arrived[:, 0, :, :half], mean_half), centred(arrived[:, 1], mean_c))
    partial = partial + product(
        centred(swapped[:, 0, :, half:], mean_half), centred(swapped[:, 1], mean_c)
    )
    parcel = (partial * (jnp.exp2(-power) / total_rows)).astype(F16)
    pieces = exchange(parcel.reshape(NX, width, block), "x")
    summed = jnp.sum(pieces.astype(F32), axis=0)

    mine = lax.dynamic_slice_in_dim(arrived, y_idx * NZ, NZ, 0)[:, 1]
    mine = (mine.astype(F32) - mean_c).astype(BF16).astype(F32)
    norms = jnp.sum(mine * mine, axis=2).reshape(1, NZ * row_count)
    norms = jnp.pad(norms, ((0, 0), (0, LANES - NZ * row_count)))

    shift = jnp.array(SHIFT, jnp.int32)[f_idx]
    column = 2 * (z_idx % 4) + z_idx // 4
    never = -2 * block
    first = jnp.where(y_idx == column, (z_idx + shift) % NZ * width, never)
    message = pl.pallas_call(
        block_kernel,
        out_shape=shapes((NZ * NF, 2, LANES), F32),
        in_specs=[IN_SMEM, IN_VMEM, IN_VMEM, IN_SMEM],
        out_specs=IN_VMEM,
        name="block_stats",
    )(first.reshape(1), summed, norms, jnp.exp2(power).reshape(1))

    seen = exchange(message, SLAB)

    def owner(z, f):
        return ((z + SHIFT[f]) % NZ) * NF + COLUMN[z]

    moves = [(z * NF + f, owner(z, f)) for z in range(NZ) for f in range(NF)]
    owned = lax.ppermute(summed.astype(F16), SLAB, moves).astype(F32)
    carried = jnp.concatenate(
        (mean_c.reshape(NF, width), jnp.broadcast_to(power, (8, width)))
    )
    carried = lax.ppermute(carried, SLAB, moves)
    second = pl.pallas_call(
        functools.partial(middle_kernel, width=width),
        out_shape=shapes((NY, 1, LANES), F32),
        in_specs=[IN_VMEM],
        out_specs=IN_VMEM,
        name="middle_stats",
    )(seen)
    totals = exchange(second, "y")

    first_own = jnp.where(y_idx == f_idx, z_idx * width, never)
    shrunk, shrinkage = pl.pallas_call(
        functools.partial(shrink_kernel, rows=total_rows, factors=factors),
        out_shape=(shapes((width, block), F32), shapes((1, 1), F32)),
        in_specs=[IN_SMEM, IN_SMEM, IN_VMEM, IN_VMEM],
        out_specs=(IN_VMEM, IN_VMEM),
        name="shrink",
    )(first_own.reshape(1), jnp.exp2(carried[NF, :1]), totals, owned)
    return (shrunk, shrinkage.reshape(()), carried[:NF].reshape(block))


def solution(mesh):
    finer = Mesh(mesh.devices.reshape(NY, NZ, NX, NC), EVERY)
    return jax.shard_map(
        shrinkage_step,
        mesh=finer,
        in_specs=(P(EVERY, None),),
        out_specs=(P(PLANE, LINE), P(), P(LINE)),
        check_vma=False,
    )
```

time: 165 us -> 151 us (0.915)
  starting transfers between devices: 64.7 us -> 55.4 us
  other arithmetic: 9.99 us -> 5.57 us
    ppermute x3 -> x2, starting transfers between devices: 17.1 us -> 9.58 us  [the longest x1 7.55 us: shrinkage_step(): owned = lax.ppermute(summed.astype(F16), SLAB, moves).astype(F32)]
    convert_element_type x3 -> x2, other arithmetic: 4.84 us -> 1.9 us  [shrinkage_step(): owned = lax.ppermute(summed.astype(F16), SLAB, moves).astype(F32)]
    reduce_max x0 -> x3, other arithmetic: none -> 2.4 us  [the longest x2 1.21 us: shrinkage_step(): reach = 2.0 * jnp.max(told[:, 2 * NF]) + jnp.max(jnp.abs(part - means))]
    another operation x3 -> x0, other arithmetic: 1.86 us -> none  [the longest x1 1.29 us: shrinkage_step(): jnp.stack((first_own, which_own))]
  transfers between devices with their start and end apart: 9 -> 8, of which waited for: 6 -> 4; matrix products, arithmetic and copies ran while one was open for 5% -> 4% of each run, Pallas kernels for 1% -> 1%
where the time goes in v6:
time: 151 us; the launch traced here: 149 us
  waiting for transfers between devices  67.5 us (45%)
  starting transfers between devices  55.4 us (37%)
  Pallas kernels  8.3 us (5%)
  other arithmetic  5.57 us (4%)
  local copies, waits for them, and re-layouts  4.92 us (3%)
  matrix products  3.96 us (3%)
  between operations  3.65 us (2%)
    all_to_all x1, waiting for transfers between devices, shrinkage_step(): arrived = exchange(dealt, PLANE)  48.5 us
    all_to_all x1, starting transfers between devices, shrinkage_step(): arrived = exchange(dealt, PLANE)  17.1 us
    all_to_all x1, waiting for transfers between devices, shrinkage_step(): pieces = exchange(parcel.reshape(NX, width, block), 'x')  12.2 us
    all_to_all x1, starting transfers between devices, shrinkage_step(): seen = exchange(message, SLAB)  8.75 us
    all_to_all x1, starting transfers between devices, shrinkage_step(): told = exchange(jnp.broadcast_to(told[None], (NF, *told.shape)), LINE)  8.63 us
    ppermute x1, starting transfers between devices, shrinkage_step(): owned = lax.ppermute(summed.astype(F16), SLAB, moves).astype(F32)  7.55 us
    all_to_all x1, starting transfers between devices, shrinkage_step(): totals = exchange(second, 'y')  5.76 us
    dot_general x2, matrix products, product(): lax.dot_general(left, right, (((0,), (0,)), ((), ())), preferred_element_...  3.96 us
  transfers between devices with their start and end apart: 8, of which 4 were waited for; matrix products, arithmetic and copies ran while one was open for 4% of the time, Pallas kernels for 1%

profile of v6, /device:TPU:1, one launch (start us, length us, event | category | flops | bytes accessed | tf_op | source)
XLA Modules:
  0.0 149.3 jit_solution(17307856654443926905)
XLA Ops:
  0.6 2.5 %deal.1 = bf16[64,2,8,1024]{3,2,1,0:T(8,128)(2,1)} custom-call(s32[1]{0:T(128)} %bitcast.1.core_ref, bf16[8,8192]{1,0:T(8,128)(2,1)} %x_ref.1), custom_call_target="tpu_custom_call" | custom-call | tf_op jit(solution)/shard_map/deal/pallas_call | solution.py:170
  3.1 17.1 %all-to-all-start = ((bf16[64,2,8,1024]{3,2,1,0:T(8,128)(2,1)}), bf16[64,2,8,1024]{3,2,1,0:T(8,128)(2,1)S(1)}, u32[]{:S(2)}, u32[]{:S(2)}) async-start(bf16[64,2,8,1024]{3,2,1,0:T(8,128)(2,1)} %deal.1), calls=%async_computation | async-start | bytes 4194304 | tf_op jit(solution)/shard_map/all_to_all | solution.py:177
  20.3 48.5 %all-to-all-done = bf16[64,2,8,1024]{3,2,1,0:T(8,128)(2,1)S(1)} async-done(((bf16[64,2,8,1024]{3,2,1,0:T(8,128)(2,1)}), bf16[64,2,8,1024]{3,2,1,0:T(8,128)(2,1)S(1)}, u32[]{:S(2)}, u32[]{:S(2)}) %all-to-all-start) | async-done | bytes 2097184 | tf_op jit(solution)/shard_map/all_to_all | solution.py:177
  68.7 1.2 abs_reduce_fusion
  69.9 0.6 broadcast_in_dim.4
  70.7 0.7 broadcast_in_dim.5
  71.4 8.6 %all-to-all-start.1 = ((f32[8,24,128]{2,1,0:T(8,128)}), f32[8,24,128]{2,1,0:T(8,128)S(1)}, u32[]{:S(2)}, u32[]{:S(2)}) async-start(f32[8,24,128]{2,1,0:T(8,128)} %broadcast_in_dim.5), calls=%async_computation.1 | async-start | bytes 196608 | tf_op jit(solution)/shard_map/all_to_all | solution.py:186
  80.0 1.9 %collective-permute-start.1 = (bf16[64,2,8,1024]{3,2,1,0:T(8,128)(2,1)S(1)}, bf16[64,2,8,1024]{3,2,1,0:T(8,128)(2,1)}, u32[]{:S(2)}, u32[]{:S(2)}) collective-permute-start(bf16[64,2,8,1024]{3,2,1,0:T(8,128)(2,1)S(1)} %all-to-all-done), channel_id=1, source_target_pairs={{0,1},{1,0},{2,3},{3,2},{4,5},{5,4},{6,7},{7,6},{8,9},{9,8},{10,11... | collective-permute-start | bytes 6291464 | tf_op jit(solution)/shard_map/ppermute | solution.py:179
  81.9 3.1 %all-to-all-done.1 = f32[8,24,128]{2,1,0:T(8,128)S(1)} async-done(((f32[8,24,128]{2,1,0:T(8,128)}), f32[8,24,128]{2,1,0:T(8,128)S(1)}, u32[]{:S(2)}, u32[]{:S(2)}) %all-to-all-start.1) | async-done | bytes 98336 | tf_op jit(solution)/shard_map/all_to_all | solution.py:186
  85.0 0.6 reduce_max.32
  86.3 0.6 abs_reduce_fusion.1
  87.6 0.8 fusion.3
  88.4 3.2 %fusion.1 = f16[512,1024]{1,0:T(8,128)(2,1)} fusion(f32[512,1024,1]{1,0,2:T(8,128)S(1)} %fusion.3, bf16[64,2,8,1024]{3,2,1,0:T(8,128)(2,1)} %collective-permute-done.1, f32[]{:T(128)S(6)} %div.30, f32[1024]{0:T(1024)S(1)} %get-tuple-element.9, f32[512]{0:T(512)S(1)} %fusion.20), kind=kOutput, calls=%fused_computation.3 | convolution fusion | flops 540803072 | bytes 4724740 | tf_op jit(solution)/shard_map/dot_general | solution.py:154
  91.6 3.6 %all-to-all-start.2 = ((f16[4,128,1024]{2,1,0:T(8,128)(2,1)}), f16[4,128,1024]{2,1,0:T(8,128)(2,1)S(1)}, u32[]{:S(2)}, u32[]{:S(2)}) async-start(f16[4,128,1024]{2,1,0:T(8,128)(2,1)} %bitcast.47), calls=%async_computation.2 | async-start | bytes 2097152 | tf_op jit(solution)/shard_map/all_to_all | solution.py:204
  95.3 0.6 dynamic_slice.6
  96.8 0.5 pad.5.norms_ref
  97.4 12.2 %all-to-all-done.2 = f16[4,128,1024]{2,1,0:T(8,128)(2,1)S(1)} async-done(((f16[4,128,1024]{2,1,0:T(8,128)(2,1)}), f16[4,128,1024]{2,1,0:T(8,128)(2,1)S(1)}, u32[]{:S(2)}, u32[]{:S(2)}) %all-to-all-start.2) | async-done | bytes 1048608 | tf_op jit(solution)/shard_map/all_to_all | solution.py:204
  109.6 1.0 convert_reduce_fusion.sum_ref
  110.7 2.0 %block_stats.1 = f32[64,2,128]{2,1,0:T(2,128)} custom-call(s32[1]{0:T(128)} %bitcast.9.place_ref, f32[128,1024]{1,0:T(8,128)} %convert_reduce_fusion.sum_ref, f32[1,128]{1,0:T(1,128)} %pad.5.norms_ref, f32[1]{0:T(128)} %bitcast.20.factor_ref), custom_call_target="tpu_custom_call" | custom-call | tf_op jit(solution)/shard_map/block_stats/pallas_call | solution.py:216
  112.7 8.7 %all-to-all-start.3 = ((f32[64,2,128]{2,1,0:T(2,128)}), f32[64,2,128]{2,1,0:T(2,128)S(1)}, u32[]{:S(2)}, u32[]{:S(2)}) async-start(f32[64,2,128]{2,1,0:T(2,128)} %block_stats.1), calls=%async_computation.3 | async-start | bytes 131072 | tf_op jit(solution)/shard_map/all_to_all | solution.py:224
  121.4 1.1 convert_element_type.88
  122.5 7.5 %collective-permute-start.2 = (f16[128,1024]{1,0:T(8,128)(2,1)S(1)}, f16[128,1024]{1,0:T(8,128)(2,1)S(1)}, u32[]{:S(2)}, u32[]{:S(2)}) collective-permute-start(f16[128,1024]{1,0:T(8,128)(2,1)S(1)} %convert_element_type.88), channel_id=1, source_target_pairs={{0,0},{1,32},{2,8},{3,56},{4,16},{5,48},{6,24},{7,40},{8,10},{9,42... | collective-permute-start | bytes 786440 | tf_op jit(solution)/shard_map/ppermute | solution.py:230
  130.1 2.0 %collective-permute-start = (f32[16,128]{1,0:T(8,128)S(1)}, f32[16,128]{1,0:T(8,128)S(1)}, u32[]{:S(2)}, u32[]{:S(2)}) collective-permute-start(f32[16,128]{1,0:T(8,128)S(1)} %concatenate.19), channel_id=1, source_target_pairs={{0,0},{1,32},{2,8},{3,56},{4,16},{5,48},{6,24},{7,40},{8,10},{9,42... | collective-permute-start | bytes 24584 | tf_op jit(solution)/shard_map/ppermute | solution.py:234
  132.1 0.6 copy-done
  132.7 1.7 %middle_stats.1 = f32[8,1,128]{2,1,0:T(1,128)} custom-call(f32[64,2,128]{2,1,0:T(2,128)} %copy-done), custom_call_target="tpu_custom_call" | custom-call | tf_op jit(solution)/shard_map/middle_stats/pallas_call | solution.py:235
  134.5 5.8 %all-to-all-start.4 = ((f32[8,1,128]{2,1,0:T(1,128)}), f32[8,1,128]{2,1,0:T(1,128)S(1)}, u32[]{:S(2)}, u32[]{:S(2)}) async-start(f32[8,1,128]{2,1,0:T(1,128)} %middle_stats.1), calls=%async_computation.4 | async-start | bytes 8192 | tf_op jit(solution)/shard_map/all_to_all | solution.py:242
  140.2 0.6 slice_bitcast_fusion
  140.8 0.5 slice.89
  142.1 0.8 convert_element_type.89.owned_ref
  142.9 3.8 %all-to-all-done.4.totals_ref = f32[8,1,128]{2,1,0:T(1,128)S(1)} async-done(((f32[8,1,128]{2,1,0:T(1,128)}), f32[8,1,128]{2,1,0:T(1,128)S(1)}, u32[]{:S(2)}, u32[]{:S(2)}) %all-to-all-start.4) | async-done | bytes 4128 | tf_op jit(solution)/shard_map/all_to_all | solution.py:242
  146.6 0.6 copy-done.1
  147.2 2.1 %shrink.1 = (f32[128,1024]{1,0:T(8,128)}, f32[1,1]{1,0:T(1,128)}) custom-call(s32[1]{0:T(128)} %bitcast.place_ref, f32[1]{0:T(128)} %bitcast.7.factor_ref, f32[8,1,128]{2,1,0:T(1,128)} %copy-done.1, f32[128,1024]{1,0:T(8,128)} %convert_element_type.89.owned_ref), custom_call_target="tpu_custom_call" | custom-call | tf_op jit(solution)/shard_map/shrink/pallas_call | solution.py:245
  (23 shorter events, 0.4 us)
Async XLA Ops:
  3.1 65.6 %all-to-all-start = ((bf16[64,2,8,1024]{3,2,1,0:T(8,128)(2,1)}), bf16[64,2,8,1024]{3,2,1,0:T(8,128)(2,1)S(1)}, u32[]{:S(2)}, u32[]{:S(2)}) async-start(bf16[64,2,8,1024]{3,2,1,0:T(8,128)(2,1)} %deal.1), calls=%async_computation | async-start | bytes 4194304 | tf_op jit(solution)/shard_map/all_to_all | solution.py:177
  71.4 13.6 %all-to-all-start.1 = ((f32[8,24,128]{2,1,0:T(8,128)}), f32[8,24,128]{2,1,0:T(8,128)S(1)}, u32[]{:S(2)}, u32[]{:S(2)}) async-start(f32[8,24,128]{2,1,0:T(8,128)} %broadcast_in_dim.5), calls=%async_computation.1 | async-start | bytes 196608 | tf_op jit(solution)/shard_map/all_to_all | solution.py:186
  80.0 8.4 %collective-permute-start.1 = (bf16[64,2,8,1024]{3,2,1,0:T(8,128)(2,1)S(1)}, bf16[64,2,8,1024]{3,2,1,0:T(8,128)(2,1)}, u32[]{:S(2)}, u32[]{:S(2)}) collective-permute-start(bf16[64,2,8,1024]{3,2,1,0:T(8,128)(2,1)S(1)} %all-to-all-done), channel_id=1, source_target_pairs={{0,1},{1,0},{2,3},{3,2},{4,5},{5,4},{6,7},{7,6},{8,9},{9,8},{10,11... | collective-permute-start | bytes 6291464 | tf_op jit(solution)/shard_map/ppermute | solution.py:179
  91.6 3.7 %copy-start.2 = (s32[8]{0:T(128)S(1)}, s32[8]{0:T(128)}, u32[]{:S(2)}) copy-start(s32[8]{0:T(128)} %constant.93.clone) | copy-start | bytes 100
  91.6 18.0 %all-to-all-start.2 = ((f16[4,128,1024]{2,1,0:T(8,128)(2,1)}), f16[4,128,1024]{2,1,0:T(8,128)(2,1)S(1)}, u32[]{:S(2)}, u32[]{:S(2)}) async-start(f16[4,128,1024]{2,1,0:T(8,128)(2,1)} %bitcast.47), calls=%async_computation.2 | async-start | bytes 2097152 | tf_op jit(solution)/shard_map/all_to_all | solution.py:204
  112.7 19.5 %all-to-all-start.3 = ((f32[64,2,128]{2,1,0:T(2,128)}), f32[64,2,128]{2,1,0:T(2,128)S(1)}, u32[]{:S(2)}, u32[]{:S(2)}) async-start(f32[64,2,128]{2,1,0:T(2,128)} %block_stats.1), calls=%async_computation.3 | async-start | bytes 131072 | tf_op jit(solution)/shard_map/all_to_all | solution.py:224
  122.5 19.6 %collective-permute-start.2 = (f16[128,1024]{1,0:T(8,128)(2,1)S(1)}, f16[128,1024]{1,0:T(8,128)(2,1)S(1)}, u32[]{:S(2)}, u32[]{:S(2)}) collective-permute-start(f16[128,1024]{1,0:T(8,128)(2,1)S(1)} %convert_element_type.88), channel_id=1, source_target_pairs={{0,0},{1,32},{2,8},{3,56},{4,16},{5,48},{6,24},{7,40},{8,10},{9,42... | collective-permute-start | bytes 786440 | tf_op jit(solution)/shard_map/ppermute | solution.py:230
  130.1 10.2 %collective-permute-start = (f32[16,128]{1,0:T(8,128)S(1)}, f32[16,128]{1,0:T(8,128)S(1)}, u32[]{:S(2)}, u32[]{:S(2)}) collective-permute-start(f32[16,128]{1,0:T(8,128)S(1)} %concatenate.19), channel_id=1, source_target_pairs={{0,0},{1,32},{2,8},{3,56},{4,16},{5,48},{6,24},{7,40},{8,10},{9,42... | collective-permute-start | bytes 24584 | tf_op jit(solution)/shard_map/ppermute | solution.py:234
  132.1 0.6 copy-start
  134.5 12.2 %all-to-all-start.4 = ((f32[8,1,128]{2,1,0:T(1,128)}), f32[8,1,128]{2,1,0:T(1,128)S(1)}, u32[]{:S(2)}, u32[]{:S(2)}) async-start(f32[8,1,128]{2,1,0:T(1,128)} %middle_stats.1), calls=%async_computation.4 | async-start | bytes 8192 | tf_op jit(solution)/shard_map/all_to_all | solution.py:242
  146.6 0.6 copy-start.1

commit v7 on v6

--- a/solution.py
+++ b/solution.py
@@ -20,6 +20,7 @@
 NF = NX * NC
 SHIFT = (0, 4, 1, 7, 2, 6, 3, 5)
 COLUMN = tuple(2 * (z % 4) + z // 4 for z in range(NZ))
+HOLDER = tuple(COLUMN.index(block) for block in range(NZ))
 OFF, SECOND, MEANS = 64, 65, 66
 F16 = jnp.float16
 IN_VMEM = pl.BlockSpec(memory_space=pltpu.VMEM)
@@ -29,25 +30,75 @@
 def deal_kernel(core_ref, x_ref, out_ref):
     block = out_ref.shape[3]
 
-    def take(start, size):
-        return x_ref[:, pl.ds(pl.multiple_of(start, LANES), size)]
-
     def deal(core):
         order = [2 * x + core for x in range(NX)] + [2 * x + 1 - core for x in range(NX)]
-
-        def one(y, carry):
+        for b in range(NY):
+            whole = x_ref[:, b * block : (b + 1) * block]
+            cuts = [whole[:, k * LANES : (k + 1) * LANES] for k in range(NF)]
             for z in range(NZ):
-                to = y * NZ + z
                 for place, f in enumerate(order):
-                    start = y * block + ((z + SHIFT[f]) % NZ) * LANES
-                    out_ref[to, 0, :, pl.ds(place * LANES, LANES)] = take(start, LANES)
-                out_ref[to, 1] = take(COLUMN[z] * block, block)
-            return carry
-
-        lax.fori_loop(0, NY, one, 0)
+                    out_ref[b * NZ + z, 0, :, place * LANES : (place + 1) * LANES] = cuts[
+                        (z + SHIFT[f]) % NZ
+                    ]
+            for y in range(NY):
+                out_ref[y * NZ + HOLDER[b], 1] = whole
 
     for core in range(NC):
         pl.when(core_ref[0] == core)(functools.partial(deal, core))
+
+
+def sums_kernel(core_ref, x_ref, told_ref):
+    plane, _, rows, block = x_ref.shape
+    core = core_ref[0]
+    far = jnp.zeros((rows, LANES), F32)
+    lines = []
+    for part in range(2):
+        pivot = jnp.broadcast_to(x_ref[0, part].astype(F32)[0:1], (rows, block))
+
+        def one(p, carry):
+            total, wide = carry
+            value = x_ref[p, part].astype(F32)
+            return total + value, jnp.maximum(wide, jnp.abs(value - pivot))
+
+        zero = jnp.zeros((rows, block), F32)
+        total, wide = lax.fori_loop(0, plane, one, (zero, zero), unroll=2)
+        total = jnp.sum(total, axis=0, keepdims=True)
+        for k in range(block // LANES):
+            cut = slice(k * LANES, (k + 1) * LANES)
+            far = jnp.maximum(far, wide[:, cut])
+            lines.append(total[:, cut])
+    far = jnp.max(jnp.max(far, axis=1, keepdims=True), axis=0, keepdims=True)
+    dealt = jnp.concatenate(lines[:NF], axis=0)
+    swapped = jnp.concatenate(lines[NX:NF] + lines[:NX], axis=0)
+    plain = jnp.where(core == 0, dealt, swapped)
+    out = jnp.concatenate(
+        [plain] + lines[NF:] + [jnp.broadcast_to(far, (8, LANES))], axis=0
+    )
+    for f in range(NF):
+        told_ref[f] = out
+
+
+def means_kernel(core_ref, told_ref, half_ref, cols_ref, carried_ref, scale_ref, *, rows, held):
+    told = told_ref[...]
+    sums = told[:, : 2 * NF]
+    means = jnp.sum(sums, axis=0) * (1.0 / rows)
+    apart = jnp.max(jnp.abs(sums * (1.0 / held) - means[None]), axis=0)
+
+    def top(value):
+        return jnp.max(jnp.max(value, axis=1, keepdims=True), axis=0, keepdims=True)
+
+    reach = 2.0 * top(jnp.max(told[:, 2 * NF :], axis=0)) + top(apart)
+    power = half_power(reach * reach)
+    mine = jnp.where(core_ref[0] == 0, means[:NX], means[NX:NF])
+    for k in range(NX):
+        half_ref[:, k * LANES : (k + 1) * LANES] = mine[k : k + 1]
+    for k in range(NF):
+        cols_ref[:, k * LANES : (k + 1) * LANES] = means[NF + k : NF + k + 1]
+    up = jnp.exp2(power)
+    carried_ref[...] = jnp.concatenate(
+        (means[NF:], jnp.broadcast_to(up, (8, LANES))), axis=0
+    )
+    scale_ref[...] = in_lane(0, jnp.exp2(-power) * (1.0 / rows), jnp.zeros((1, LANES), F32))
 
 
 def add_all(value):
@@ -63,11 +114,12 @@
     return jnp.where(slot == k, value, row)
 
 
-def block_kernel(place_ref, sum_ref, norms_ref, factor_ref, message_ref):
+def block_kernel(place_ref, sum_ref, norms_ref, carried_ref, message_ref):
     width, block = sum_ref.shape
     lane = lax.broadcasted_iota(jnp.int32, (8, block), 1)
     sub = lax.broadcasted_iota(jnp.int32, (8, block), 0)
-    first, factor = place_ref[0], factor_ref[0]
+    first = place_ref[0]
+    factor = jnp.concatenate([carried_ref[NF : NF + 8, :]] * (block // LANES), axis=1)
     zero = jnp.zeros((8, LANES), F32)
     off, diagonal = zero, zero
     for k in range(width // 8):
@@ -118,7 +170,9 @@
     message_ref[...] = jnp.broadcast_to(row[None], message_ref.shape)
 
 
-def shrink_kernel(place_ref, factor_ref, totals_ref, owned_ref, shrunk_ref, value_ref, *, rows, factors):
+def shrink_kernel(
+    place_ref, carried_ref, totals_ref, owned_ref, shrunk_ref, value_ref, mean_ref, *, rows, factors
+):
     width, block = shrunk_ref.shape
     first = place_ref[0]
     slot = lax.broadcasted_iota(jnp.int32, (1, LANES), 1)
@@ -136,7 +190,8 @@
     beta_value = (pick(sums, 1) / rows - norm_sq) / (factors * rows)
     shrinkage = beta_value / spread
     value_ref[...] = shrinkage
-    keep = (1.0 - shrinkage) * factor_ref[0]
+    mean_ref[...] = carried_ref[:NF, :]
+    keep = (1.0 - shrinkage) * carried_ref[NF : NF + 1, 0:1]
     lift = shrinkage * mu_scale
     lane = lax.broadcasted_iota(jnp.int32, (8, block), 1)
     sub = lax.broadcasted_iota(jnp.int32, (8, block), 0)
@@ -144,6 +199,10 @@
         at = pl.ds(k * 8, 8)
         hit = lane == first + k * 8 + sub
         shrunk_ref[at, :] = keep * owned_ref[at, :] + jnp.where(hit, lift, 0.0)
+
+
+def in_vmem(value):
+    return pltpu.with_memory_space_constraint(value, pltpu.VMEM)
 
 
 def flip(size):
@@ -167,30 +226,37 @@
     exchange = functools.partial(lax.all_to_all, split_axis=0, concat_axis=0, tiled=True)
     shapes = jax.ShapeDtypeStruct
 
+    core = c_idx.reshape(1)
     dealt = pl.pallas_call(
         deal_kernel,
-        out_shape=shapes((plane, 2, row_count, block), BF16),
+        out_shape=pltpu.VMEM((plane, 2, row_count, block), BF16),
         in_specs=[IN_SMEM, IN_VMEM],
         out_specs=IN_VMEM,
         name="deal",
-    )(c_idx.reshape(1), scenarios)
+    )(core, scenarios)
     arrived = exchange(dealt, PLANE)
 
     swapped = lax.ppermute(arrived, "c", flip(NC))
-    values = arrived.astype(F32)
-    sums = jnp.sum(values, axis=(0, 2))
-    wide = jnp.max(jnp.abs(values - values[:1, :, :1]), axis=(0, 2))
-    sums_r = jnp.where(c_idx == 0, sums[0], jnp.roll(sums[0], half))
-    told = jnp.concatenate((sums_r.reshape(NF, width), sums[1].reshape(NF, width)))
-    told = jnp.concatenate((told, jnp.broadcast_to(jnp.max(wide), (8, width))))
-    told = exchange(jnp.broadcast_to(told[None], (NF, *told.shape)), LINE)
-    part = told[:, : 2 * NF] / part_rows
-    means = jnp.sum(told[:, : 2 * NF], axis=0) / total_rows
-    reach = 2.0 * jnp.max(told[:, 2 * NF]) + jnp.max(jnp.abs(part - means))
-    power = half_power(reach * reach)
-    mean_c = means[NF:].reshape(block)
-    mean_r = means[:NF].reshape(2, half)
-    mean_half = jnp.where(c_idx == 0, mean_r[0], mean_r[1])
+    told = pl.pallas_call(
+        sums_kernel,
+        out_shape=pltpu.VMEM((NF, 3 * NF, LANES), F32),
+        in_specs=[IN_SMEM, IN_VMEM],
+        out_specs=IN_VMEM,
+        name="sums",
+    )(core, in_vmem(arrived))
+    told = exchange(told, LINE)
+    mean_half, mean_c, carried, scale = pl.pallas_call(
+        functools.partial(means_kernel, rows=total_rows, held=part_rows),
+        out_shape=(
+            pltpu.VMEM((1, half), F32),
+            pltpu.VMEM((1, block), F32),
+            pltpu.VMEM((2 * NF, LANES), F32),
+            pltpu.VMEM((1, LANES), F32),
+        ),
+        in_specs=[IN_SMEM, IN_VMEM],
+        out_specs=(IN_VMEM,) * 4,
+        name="means",
+    )(core, in_vmem(told))
 
     def centred(rows, mean):
         out = (rows.astype(F32) - mean).astype(BF16)
@@ -200,7 +266,7 @@
     partial = partial + product(
         centred(swapped[:, 0, :, half:], mean_half), centred(swapped[:, 1], mean_c)
     )
-    parcel = (partial * (jnp.exp2(-power) / total_rows)).astype(F16)
+    parcel = (partial * scale[0, 0]).astype(F16)
     pieces = exchange(parcel.reshape(NX, width, block), "x")
     summed = jnp.sum(pieces.astype(F32), axis=0)
 
@@ -215,11 +281,11 @@
     first = jnp.where(y_idx == column, (z_idx + shift) % NZ * width, never)
     message = pl.pallas_call(
         block_kernel,
-        out_shape=shapes((NZ * NF, 2, LANES), F32),
-        in_specs=[IN_SMEM, IN_VMEM, IN_VMEM, IN_SMEM],
+        out_shape=pltpu.VMEM((NZ * NF, 2, LANES), F32),
+        in_specs=[IN_SMEM, IN_VMEM, IN_VMEM, IN_VMEM],
         out_specs=IN_VMEM,
         name="block_stats",
-    )(first.reshape(1), summed, norms, jnp.exp2(power).reshape(1))
+    )(first.reshape(1), in_vmem(summed), in_vmem(norms), in_vmem(carried))
 
     seen = exchange(message, SLAB)
 
@@ -228,28 +294,29 @@
 
     moves = [(z * NF + f, owner(z, f)) for z in range(NZ) for f in range(NF)]
     owned = lax.ppermute(summed.astype(F16), SLAB, moves).astype(F32)
-    carried = jnp.concatenate(
-        (mean_c.reshape(NF, width), jnp.broadcast_to(power, (8, width)))
-    )
     carried = lax.ppermute(carried, SLAB, moves)
     second = pl.pallas_call(
         functools.partial(middle_kernel, width=width),
-        out_shape=shapes((NY, 1, LANES), F32),
+        out_shape=pltpu.VMEM((NY, 1, LANES), F32),
         in_specs=[IN_VMEM],
         out_specs=IN_VMEM,
         name="middle_stats",
-    )(seen)
+    )(in_vmem(seen))
     totals = exchange(second, "y")
 
     first_own = jnp.where(y_idx == f_idx, z_idx * width, never)
-    shrunk, shrinkage = pl.pallas_call(
+    shrunk, shrinkage, col_mean = pl.pallas_call(
         functools.partial(shrink_kernel, rows=total_rows, factors=factors),
-        out_shape=(shapes((width, block), F32), shapes((1, 1), F32)),
-        in_specs=[IN_SMEM, IN_SMEM, IN_VMEM, IN_VMEM],
-        out_specs=(IN_VMEM, IN_VMEM),
+        out_shape=(
+            shapes((width, block), F32),
+            shapes((1, 1), F32),
+            shapes((NF, LANES), F32),
+        ),
+        in_specs=[IN_SMEM, IN_VMEM, IN_VMEM, IN_VMEM],
+        out_specs=(IN_VMEM, IN_VMEM, IN_VMEM),
         name="shrink",
-    )(first_own.reshape(1), jnp.exp2(carried[NF, :1]), totals, owned)
-    return (shrunk, shrinkage.reshape(()), carried[:NF].reshape(block))
+    )(first_own.reshape(1), in_vmem(carried), in_vmem(totals), in_vmem(owned))
+    return (shrunk, shrinkage.reshape(()), col_mean.reshape(block))
 
 
 def solution(mesh):

time: 151 us -> 149 us (0.987)
  blocking collectives: 0 us -> 91.2 us
  waiting for transfers between devices: 67.5 us -> 8.96 us
  starting transfers between devices: 55.4 us -> 33.4 us
  local copies, waits for them, and re-layouts: 4.92 us -> 0.68 us
  other arithmetic: 5.57 us -> 1.34 us
  between operations: 3.65 us -> 1.47 us
    all_to_all x0 -> x3, blocking collectives: none -> 91.2 us  [the longest x1 65.5 us: shrinkage_step(): arrived = exchange(dealt, PLANE)]
    all_to_all x3 -> x0, waiting for transfers between devices: 63.8 us -> none  [the longest x1 48.5 us: shrinkage_step(): arrived = exchange(dealt, PLANE)]
    all_to_all x3 -> x0, starting transfers between devices: 29.4 us -> none  [the longest x1 17.1 us: shrinkage_step(): arrived = exchange(dealt, PLANE)]
    ppermute x1, starting transfers between devices: 2.03 us -> 7.55 us  [shrinkage_step(): carried = lax.ppermute(carried, SLAB, moves)]
    ppermute x1, starting transfers between devices: 1.91 us -> 6.2 us  [shrinkage_step(): swapped = lax.ppermute(arrived, 'c', flip(NC))]
    all_to_all x1, starting transfers between devices: 8.75 us -> 4.9 us  [shrinkage_step(): seen = exchange(message, SLAB)]
    all_to_all x1, waiting for transfers between devices: 3.77 us -> 6.42 us  [shrinkage_step(): totals = exchange(second, 'y')]
    all_to_all x1, waiting for transfers between devices: 0.01 us -> 2.53 us  [shrinkage_step(): seen = exchange(message, SLAB)]
  transfers between devices with their start and end apart: 8 -> 5, of which waited for: 4 -> 2; matrix products, arithmetic and copies ran while one was open for 4% -> 3% of each run, Pallas kernels for 1% -> 3%
where the time goes in v7:
time: 149 us; the launch traced here: 148 us
  blocking collectives  91.2 us (61%)
  starting transfers between devices  33.4 us (22%)
  waiting for transfers between devices  8.96 us (6%)
  Pallas kernels  6.9 us (5%)
  matrix products  4.37 us (3%)
    all_to_all x1, blocking collectives, shrinkage_step(): arrived = exchange(dealt, PLANE)  65.5 us
    all_to_all x1, blocking collectives, shrinkage_step(): pieces = exchange(parcel.reshape(NX, width, block), 'x')  16.5 us
    all_to_all x1, blocking collectives, shrinkage_step(): told = exchange(told, LINE)  9.18 us
    ppermute x1, starting transfers between devices, shrinkage_step(): owned = lax.ppermute(summed.astype(F16), SLAB, moves).astype(F32)  8.21 us
    ppermute x1, starting transfers between devices, shrinkage_step(): carried = lax.ppermute(carried, SLAB, moves)  7.55 us
    all_to_all x1, starting transfers between devices, shrinkage_step(): totals = exchange(second, 'y')  6.51 us
    all_to_all x1, waiting for transfers between devices, shrinkage_step(): totals = exchange(second, 'y')  6.42 us
    ppermute x1, starting transfers between devices, shrinkage_step(): swapped = lax.ppermute(arrived, 'c', flip(NC))  6.2 us
  transfers between devices with their start and end apart: 5, of which 2 were waited for; matrix products, arithmetic and copies ran while one was open for 3% of the time, Pallas kernels for 3%

profile of v7, /device:TPU:1, one launch (start us, length us, event | category | flops | bytes accessed | tf_op | source)
XLA Modules:
  0.0 148.3 jit_solution(15870593836987907414)
XLA Ops:
  0.6 1.1 deal.1
  1.8 65.5 %all_to_all.25.x_ref = bf16[64,2,8,1024]{3,2,1,0:T(8,128)(2,1)} all-to-all(bf16[64,2,8,1024]{3,2,1,0:T(8,128)(2,1)S(1)} %deal.1), channel_id=1, replica_groups=mesh['y'=8,'z'=8,'x'=4,'c'=2] {'y','z'}, dimensions={0} | all-to-all | bytes 4194304 | tf_op jit(solution)/shard_map/all_to_all | solution.py:237
  67.3 6.2 %collective-permute-start.1 = (bf16[64,2,8,1024]{3,2,1,0:T(8,128)(2,1)}, bf16[64,2,8,1024]{3,2,1,0:T(8,128)(2,1)}, u32[]{:S(2)}, u32[]{:S(2)}) collective-permute-start(bf16[64,2,8,1024]{3,2,1,0:T(8,128)(2,1)} %all_to_all.25.x_ref), channel_id=1, source_target_pairs={{0,1},{1,0},{2,3},{3,2},{4,5},{5,4},{6,7},{7,6},{8,9},{9,8},{10,11... | collective-permute-start | bytes 6291464 | tf_op jit(solution)/shard_map/ppermute | solution.py:239
  73.5 2.7 %sums.1 = f32[8,24,128]{2,1,0:T(8,128)S(1)} custom-call(s32[1]{0:T(128)} %bitcast.1.core_ref, bf16[64,2,8,1024]{3,2,1,0:T(8,128)(2,1)} %all_to_all.25.x_ref), custom_call_target="tpu_custom_call" | custom-call | tf_op jit(solution)/shard_map/sums/pallas_call | solution.py:240
  76.2 9.2 %all_to_all.26.told_ref = f32[8,24,128]{2,1,0:T(8,128)S(1)} all-to-all(f32[8,24,128]{2,1,0:T(8,128)S(1)} %sums.1), channel_id=1, replica_groups=mesh['y'=8,'z'=8,'x'=4,'c'=2] {'x','c'}, dimensions={0} | all-to-all | bytes 196608 | tf_op jit(solution)/shard_map/all_to_all | solution.py:247
  85.3 0.1 means.1
  85.5 2.2 %fusion.3 = f32[512,1024,1]{1,0,2:T(8,128)S(1)} fusion(bf16[64,2,8,1024]{3,2,1,0:T(8,128)(2,1)} %all_to_all.25.x_ref, f32[1024]{0:T(1024)S(1)} %bitcast.36, f32[512]{0:T(512)S(1)} %bitcast.39), kind=kOutput, calls=%fused_computation.7 | convolution fusion | flops 539230208 | bytes 3676160 | tf_op jit(solution)/shard_map/dot_general | solution.py:213
  87.6 0.0 collective-permute-done.1
  87.6 2.2 %fusion.1 = f16[512,1024]{1,0:T(8,128)(2,1)S(1)} fusion(f32[512,1024,1]{1,0,2:T(8,128)S(1)} %fusion.3, bf16[64,2,8,1024]{3,2,1,0:T(8,128)(2,1)} %collective-permute-done.1, f32[]{:T(128)S(1)} %bitcast.41, f32[1024]{0:T(1024)S(1)} %bitcast.37, f32[512]{0:T(512)S(1)} %bitcast.40), kind=kOutput, calls=%fused_computation.2 | convolution fusion | flops 540803072 | bytes 4724740 | tf_op jit(solution)/shard_map/dot_general | solution.py:213
  89.9 0.0 copy-start
  89.9 16.5 %all_to_all.27 = f16[4,128,1024]{2,1,0:T(8,128)(2,1)S(1)} all-to-all(f16[4,128,1024]{2,1,0:T(8,128)(2,1)S(1)} %bitcast.42), channel_id=1, replica_groups=mesh['y'=8,'z'=8,'x'=4,'c'=2] {'x'}, dimensions={0} | all-to-all | bytes 2097152 | tf_op jit(solution)/shard_map/all_to_all | solution.py:270
  106.4 0.2 convert_reduce_fusion.sum_ref
  106.7 8.2 %collective-permute-start.2 = (f16[128,1024]{1,0:T(8,128)(2,1)S(1)}, f16[128,1024]{1,0:T(8,128)(2,1)S(1)}, u32[]{:S(2)}, u32[]{:S(2)}) collective-permute-start(f16[128,1024]{1,0:T(8,128)(2,1)S(1)} %convert_element_type.84), channel_id=1, source_target_pairs={{0,0},{1,32},{2,8},{3,56},{4,16},{5,48},{6,24},{7,40},{8,10},{9,42... | collective-permute-start | bytes 786440 | tf_op jit(solution)/shard_map/ppermute | solution.py:296
  114.9 0.0 copy-done
  114.9 0.6 dynamic_slice.6
  116.2 1.0 multiply_reduce_fusion
  117.3 0.1 reshape.43
  117.4 1.0 block_stats.1
  118.3 4.9 %all-to-all-start.3 = ((f32[64,2,128]{2,1,0:T(2,128)}), f32[64,2,128]{2,1,0:T(2,128)S(1)}, u32[]{:S(2)}, u32[]{:S(2)}) async-start(f32[64,2,128]{2,1,0:T(2,128)} %block_stats.1), calls=%async_computation.3 | async-start | bytes 131072 | tf_op jit(solution)/shard_map/all_to_all | solution.py:290
  123.2 7.5 %collective-permute-start = (f32[16,128]{1,0:T(8,128)S(1)}, f32[16,128]{1,0:T(8,128)S(1)}, u32[]{:S(2)}, u32[]{:S(2)}) collective-permute-start(f32[16,128]{1,0:T(8,128)S(1)} %get-tuple-element.10.carried_ref), channel_id=1, source_target_pairs={{0,0},{1,32},{2,8},{3,56},{4,16},{5,48},{6,24},{7,40},{8,10},{9,42... | collective-permute-start | bytes 24584 | tf_op jit(solution)/shard_map/ppermute | solution.py:297
  130.8 2.5 %all-to-all-done.3.seen_ref = f32[64,2,128]{2,1,0:T(2,128)S(1)} async-done(((f32[64,2,128]{2,1,0:T(2,128)}), f32[64,2,128]{2,1,0:T(2,128)S(1)}, u32[]{:S(2)}, u32[]{:S(2)}) %all-to-all-start.3) | async-done | bytes 65568 | tf_op jit(solution)/shard_map/all_to_all | solution.py:290
  133.3 0.9 middle_stats.1
  134.2 6.5 %all-to-all-start.4 = ((f32[8,1,128]{2,1,0:T(1,128)}), f32[8,1,128]{2,1,0:T(1,128)S(1)}, u32[]{:S(2)}, u32[]{:S(2)}) async-start(f32[8,1,128]{2,1,0:T(1,128)} %middle_stats.1), calls=%async_computation.4 | async-start | bytes 8192 | tf_op jit(solution)/shard_map/all_to_all | solution.py:305
  140.7 0.0 collective-permute-done.2
  140.8 0.0 collective-permute-done.carried_ref
  140.8 6.4 %all-to-all-done.4.totals_ref = f32[8,1,128]{2,1,0:T(1,128)S(1)} async-done(((f32[8,1,128]{2,1,0:T(1,128)}), f32[8,1,128]{2,1,0:T(1,128)S(1)}, u32[]{:S(2)}, u32[]{:S(2)}) %all-to-all-start.4) | async-done | bytes 4128 | tf_op jit(solution)/shard_map/all_to_all | solution.py:305
  147.2 1.1 shrink.1
  (3 shorter events, 0.1 us)
Async XLA Ops:
  67.3 20.4 %collective-permute-start.1 = (bf16[64,2,8,1024]{3,2,1,0:T(8,128)(2,1)}, bf16[64,2,8,1024]{3,2,1,0:T(8,128)(2,1)}, u32[]{:S(2)}, u32[]{:S(2)}) collective-permute-start(bf16[64,2,8,1024]{3,2,1,0:T(8,128)(2,1)} %all_to_all.25.x_ref), channel_id=1, source_target_pairs={{0,1},{1,0},{2,3},{3,2},{4,5},{5,4},{6,7},{7,6},{8,9},{9,8},{10,11... | collective-permute-start | bytes 6291464 | tf_op jit(solution)/shard_map/ppermute | solution.py:239
  89.9 25.1 %copy-start = (s32[8]{0:T(128)S(1)}, s32[8]{0:T(128)}, u32[]{:S(2)}) copy-start(s32[8]{0:T(128)} %constant.65.clone) | copy-start | bytes 100
  106.7 34.0 %collective-permute-start.2 = (f16[128,1024]{1,0:T(8,128)(2,1)S(1)}, f16[128,1024]{1,0:T(8,128)(2,1)S(1)}, u32[]{:S(2)}, u32[]{:S(2)}) collective-permute-start(f16[128,1024]{1,0:T(8,128)(2,1)S(1)} %convert_element_type.84), channel_id=1, source_target_pairs={{0,0},{1,32},{2,8},{3,56},{4,16},{5,48},{6,24},{7,40},{8,10},{9,42... | collective-permute-start | bytes 786440 | tf_op jit(solution)/shard_map/ppermute | solution.py:296
  118.3 15.0 %all-to-all-start.3 = ((f32[64,2,128]{2,1,0:T(2,128)}), f32[64,2,128]{2,1,0:T(2,128)S(1)}, u32[]{:S(2)}, u32[]{:S(2)}) async-start(f32[64,2,128]{2,1,0:T(2,128)} %block_stats.1), calls=%async_computation.3 | async-start | bytes 131072 | tf_op jit(solution)/shard_map/all_to_all | solution.py:290
  123.2 17.6 %collective-permute-start = (f32[16,128]{1,0:T(8,128)S(1)}, f32[16,128]{1,0:T(8,128)S(1)}, u32[]{:S(2)}, u32[]{:S(2)}) collective-permute-start(f32[16,128]{1,0:T(8,128)S(1)} %get-tuple-element.10.carried_ref), channel_id=1, source_target_pairs={{0,0},{1,32},{2,8},{3,56},{4,16},{5,48},{6,24},{7,40},{8,10},{9,42... | collective-permute-start | bytes 24584 | tf_op jit(solution)/shard_map/ppermute | solution.py:297
  134.2 13.0 %all-to-all-start.4 = ((f32[8,1,128]{2,1,0:T(1,128)}), f32[8,1,128]{2,1,0:T(1,128)S(1)}, u32[]{:S(2)}, u32[]{:S(2)}) async-start(f32[8,1,128]{2,1,0:T(1,128)} %middle_stats.1), calls=%async_computation.4 | async-start | bytes 8192 | tf_op jit(solution)/shard_map/all_to_all | solution.py:305

commit v8 on v7

--- a/solution.py
+++ b/solution.py
@@ -48,29 +48,22 @@
 
 
 def sums_kernel(core_ref, x_ref, told_ref):
-    plane, _, rows, block = x_ref.shape
-    core = core_ref[0]
-    far = jnp.zeros((rows, LANES), F32)
+    _, _, _, block = x_ref.shape
+    far = jnp.zeros((1, LANES), F32)
     lines = []
     for part in range(2):
-        pivot = jnp.broadcast_to(x_ref[0, part].astype(F32)[0:1], (rows, block))
-
-        def one(p, carry):
-            total, wide = carry
-            value = x_ref[p, part].astype(F32)
-            return total + value, jnp.maximum(wide, jnp.abs(value - pivot))
-
-        zero = jnp.zeros((rows, block), F32)
-        total, wide = lax.fori_loop(0, plane, one, (zero, zero), unroll=2)
-        total = jnp.sum(total, axis=0, keepdims=True)
         for k in range(block // LANES):
-            cut = slice(k * LANES, (k + 1) * LANES)
-            far = jnp.maximum(far, wide[:, cut])
-            lines.append(total[:, cut])
-    far = jnp.max(jnp.max(far, axis=1, keepdims=True), axis=0, keepdims=True)
+            at = slice(k * LANES, (k + 1) * LANES)
+            value = x_ref[:, part, :, at]
+            line = jnp.sum(jnp.sum(value.astype(F32), axis=0), axis=0, keepdims=True)
+            high = jnp.max(jnp.max(value, axis=0).astype(F32), axis=0, keepdims=True)
+            low = jnp.min(jnp.min(value, axis=0).astype(F32), axis=0, keepdims=True)
+            far = jnp.maximum(far, high - low)
+            lines.append(line)
+    far = jnp.max(far, axis=1, keepdims=True)
     dealt = jnp.concatenate(lines[:NF], axis=0)
     swapped = jnp.concatenate(lines[NX:NF] + lines[:NX], axis=0)
-    plain = jnp.where(core == 0, dealt, swapped)
+    plain = jnp.where(core_ref[0] == 0, dealt, swapped)
     out = jnp.concatenate(
         [plain] + lines[NF:] + [jnp.broadcast_to(far, (8, LANES))], axis=0
     )
@@ -87,7 +80,7 @@
     def top(value):
         return jnp.max(jnp.max(value, axis=1, keepdims=True), axis=0, keepdims=True)
 
-    reach = 2.0 * top(jnp.max(told[:, 2 * NF :], axis=0)) + top(apart)
+    reach = top(jnp.max(told[:, 2 * NF :], axis=0)) + top(apart)
     power = half_power(reach * reach)
     mine = jnp.where(core_ref[0] == 0, means[:NX], means[NX:NF])
     for k in range(NX):
@@ -149,7 +142,7 @@
     seen = seen_ref[...]
     slot = lax.broadcasted_iota(jnp.int32, (1, 1, LANES), 2)
     values, flags = seen[:, 0:1, :], seen[:, 1:2, :]
-    norms = jnp.sum(values.reshape(NZ, NF, 1, LANES), axis=0)
+    norms = jnp.sum(values.reshape(NZ, NC, 1, LANES), axis=0)
     norms = jnp.where(slot < OFF, norms, 0.0)
     total = jnp.sum(values, axis=0)
     is_mean = slot == MEANS
@@ -157,7 +150,7 @@
     def lanes(row):
         return jnp.sum(row, axis=1, keepdims=True)
 
-    mean = lanes(jnp.where(is_mean[0], total, 0.0)) / NF
+    mean = lanes(jnp.where(is_mean[0], total, 0.0)) / NC
     apart = jnp.where(is_mean, (values - mean[None]) * flags, 0.0)
     between = lanes(jnp.sum(apart * apart, axis=0))
     second = lanes(jnp.where(slot[0] == SECOND, total, 0.0)) + width * between
@@ -185,7 +178,7 @@
     mu_scale = pick(sums, 0) / (rows * factors)
     apart = totals - mu_scale[None]
     from_mu = pick(jnp.sum(apart * apart, axis=0), 3)
-    spread = (pick(sums, 2) + pick(sums, 4) + block * from_mu) / factors
+    spread = (pick(sums, 2) + pick(sums, 4) + NC * width * from_mu) / factors
     norm_sq = factors * (spread + mu_scale * mu_scale)
     beta_value = (pick(sums, 1) / rows - norm_sq) / (factors * rows)
     shrinkage = beta_value / spread
@@ -281,13 +274,13 @@
     first = jnp.where(y_idx == column, (z_idx + shift) % NZ * width, never)
     message = pl.pallas_call(
         block_kernel,
-        out_shape=pltpu.VMEM((NZ * NF, 2, LANES), F32),
+        out_shape=pltpu.VMEM((NZ * NC, 2, LANES), F32),
         in_specs=[IN_SMEM, IN_VMEM, IN_VMEM, IN_VMEM],
         out_specs=IN_VMEM,
         name="block_stats",
     )(first.reshape(1), in_vmem(summed), in_vmem(norms), in_vmem(carried))
 
-    seen = exchange(message, SLAB)
+    seen = exchange(message, ("z", "c"))
 
     def owner(z, f):
         return ((z + SHIFT[f]) % NZ) * NF + COLUMN[z]
@@ -297,12 +290,12 @@
     carried = lax.ppermute(carried, SLAB, moves)
     second = pl.pallas_call(
         functools.partial(middle_kernel, width=width),
-        out_shape=pltpu.VMEM((NY, 1, LANES), F32),
+        out_shape=pltpu.VMEM((NY * NX, 1, LANES), F32),
         in_specs=[IN_VMEM],
         out_specs=IN_VMEM,
         name="middle_stats",
     )(in_vmem(seen))
-    totals = exchange(second, "y")
+    totals = exchange(second, ("y", "x"))
 
     first_own = jnp.where(y_idx == f_idx, z_idx * width, never)
     shrunk, shrinkage, col_mean = pl.pallas_call(

time: 149 us -> 148 us (level)
  blocking collectives: 91.2 us -> 100 us
  starting transfers between devices: 33.4 us -> 27 us
  waiting for transfers between devices: 8.96 us -> 5.45 us
    all_to_all x0 -> x1, blocking collectives: none -> 8.96 us  [shrinkage_step(): seen = exchange(message, ('z', 'c'))]
    all_to_all x2 -> x1, waiting for transfers between devices: 8.96 us -> 0.01 us  [shrinkage_step(): totals = exchange(second, ('y', 'x'))]
    ppermute x1, waiting for transfers between devices: 0.01 us -> 5.44 us  [shrinkage_step(): carried = lax.ppermute(carried, SLAB, moves)]
    ppermute x1, starting transfers between devices: 7.55 us -> 3.08 us  [shrinkage_step(): carried = lax.ppermute(carried, SLAB, moves)]
    all_to_all x2 -> x1, starting transfers between devices: 11.4 us -> 9.47 us  [shrinkage_step(): totals = exchange(second, ('y', 'x'))]
  transfers between devices with their start and end apart: 5 -> 4, of which waited for: 2 -> 1; matrix products, arithmetic and copies ran while one was open for 3% -> 3% of each run, Pallas kernels for 3% -> 3%
where the time goes in v8:
time: 148 us; the launch traced here: 147 us
  blocking collectives  100 us (68%)
  starting transfers between devices  27 us (18%)
  Pallas kernels  6.07 us (4%)
  waiting for transfers between devices  5.45 us (4%)
  matrix products  4.37 us (3%)
  between operations  1.48 us (1%)
    all_to_all x1, blocking collectives, shrinkage_step(): arrived = exchange(dealt, PLANE)  65.5 us
    all_to_all x1, blocking collectives, shrinkage_step(): pieces = exchange(parcel.reshape(NX, width, block), 'x')  16.5 us
    all_to_all x1, starting transfers between devices, shrinkage_step(): totals = exchange(second, ('y', 'x'))  9.47 us
    all_to_all x1, blocking collectives, shrinkage_step(): told = exchange(told, LINE)  9.18 us
    all_to_all x1, blocking collectives, shrinkage_step(): seen = exchange(message, ('z', 'c'))  8.96 us
    ppermute x1, starting transfers between devices, shrinkage_step(): owned = lax.ppermute(summed.astype(F16), SLAB, moves).astype(F32)  8.21 us
    ppermute x1, starting transfers between devices, shrinkage_step(): swapped = lax.ppermute(arrived, 'c', flip(NC))  6.2 us
    ppermute x1, waiting for transfers between devices, shrinkage_step(): carried = lax.ppermute(carried, SLAB, moves)  5.44 us
  transfers between devices with their start and end apart: 4, of which 1 were waited for; matrix products, arithmetic and copies ran while one was open for 3% of the time, Pallas kernels for 3%

profile of v8, /device:TPU:1, one launch (start us, length us, event | category | flops | bytes accessed | tf_op | source)
XLA Modules:
  0.0 146.5 jit_solution(16895474060003608546)
XLA Ops:
  0.6 1.1 deal.1
  1.8 65.5 %all_to_all.25.x_ref = bf16[64,2,8,1024]{3,2,1,0:T(8,128)(2,1)} all-to-all(bf16[64,2,8,1024]{3,2,1,0:T(8,128)(2,1)S(1)} %deal.1), channel_id=1, replica_groups=mesh['y'=8,'z'=8,'x'=4,'c'=2] {'y','z'}, dimensions={0} | all-to-all | bytes 4194304 | tf_op jit(solution)/shard_map/all_to_all | solution.py:230
  67.3 6.2 %collective-permute-start.1 = (bf16[64,2,8,1024]{3,2,1,0:T(8,128)(2,1)}, bf16[64,2,8,1024]{3,2,1,0:T(8,128)(2,1)}, u32[]{:S(2)}, u32[]{:S(2)}) collective-permute-start(bf16[64,2,8,1024]{3,2,1,0:T(8,128)(2,1)} %all_to_all.25.x_ref), channel_id=1, source_target_pairs={{0,1},{1,0},{2,3},{3,2},{4,5},{5,4},{6,7},{7,6},{8,9},{9,8},{10,11... | collective-permute-start | bytes 6291464 | tf_op jit(solution)/shard_map/ppermute | solution.py:232
  73.5 2.5 %sums.1 = f32[8,24,128]{2,1,0:T(8,128)S(1)} custom-call(s32[1]{0:T(128)} %bitcast.1.core_ref, bf16[64,2,8,1024]{3,2,1,0:T(8,128)(2,1)} %all_to_all.25.x_ref), custom_call_target="tpu_custom_call" | custom-call | tf_op jit(solution)/shard_map/sums/pallas_call | solution.py:233
  76.0 9.2 %all_to_all.26.told_ref = f32[8,24,128]{2,1,0:T(8,128)S(1)} all-to-all(f32[8,24,128]{2,1,0:T(8,128)S(1)} %sums.1), channel_id=1, replica_groups=mesh['y'=8,'z'=8,'x'=4,'c'=2] {'x','c'}, dimensions={0} | all-to-all | bytes 196608 | tf_op jit(solution)/shard_map/all_to_all | solution.py:240
  85.2 0.1 means.1
  85.3 2.2 %fusion.3 = f32[512,1024,1]{1,0,2:T(8,128)S(1)} fusion(bf16[64,2,8,1024]{3,2,1,0:T(8,128)(2,1)} %all_to_all.25.x_ref, f32[1024]{0:T(1024)S(1)} %bitcast.36, f32[512]{0:T(512)S(1)} %bitcast.39), kind=kOutput, calls=%fused_computation.7 | convolution fusion | flops 539230208 | bytes 3676160 | tf_op jit(solution)/shard_map/dot_general | solution.py:206
  87.5 0.0 collective-permute-done.1
  87.5 2.2 %fusion.1 = f16[512,1024]{1,0:T(8,128)(2,1)S(1)} fusion(f32[512,1024,1]{1,0,2:T(8,128)S(1)} %fusion.3, bf16[64,2,8,1024]{3,2,1,0:T(8,128)(2,1)} %collective-permute-done.1, f32[]{:T(128)S(1)} %bitcast.41, f32[1024]{0:T(1024)S(1)} %bitcast.37, f32[512]{0:T(512)S(1)} %bitcast.40), kind=kOutput, calls=%fused_computation.2 | convolution fusion | flops 540803072 | bytes 4724740 | tf_op jit(solution)/shard_map/dot_general | solution.py:206
  89.7 0.0 copy-start
  89.7 16.5 %all_to_all.27 = f16[4,128,1024]{2,1,0:T(8,128)(2,1)S(1)} all-to-all(f16[4,128,1024]{2,1,0:T(8,128)(2,1)S(1)} %bitcast.42), channel_id=1, replica_groups=mesh['y'=8,'z'=8,'x'=4,'c'=2] {'x'}, dimensions={0} | all-to-all | bytes 2097152 | tf_op jit(solution)/shard_map/all_to_all | solution.py:263
  106.2 0.2 convert_reduce_fusion.sum_ref
  106.5 8.2 %collective-permute-start.2 = (f16[128,1024]{1,0:T(8,128)(2,1)S(1)}, f16[128,1024]{1,0:T(8,128)(2,1)S(1)}, u32[]{:S(2)}, u32[]{:S(2)}) collective-permute-start(f16[128,1024]{1,0:T(8,128)(2,1)S(1)} %convert_element_type.84), channel_id=1, source_target_pairs={{0,0},{1,32},{2,8},{3,56},{4,16},{5,48},{6,24},{7,40},{8,10},{9,42... | collective-permute-start | bytes 786440 | tf_op jit(solution)/shard_map/ppermute | solution.py:289
  114.8 0.0 copy-done
  114.8 0.6 dynamic_slice.6
  116.1 1.0 multiply_reduce_fusion
  117.1 0.1 reshape.43
  117.2 0.3 block_stats.1
  117.5 9.0 %all_to_all.28.seen_ref = f32[16,2,128]{2,1,0:T(2,128)S(1)} all-to-all(f32[16,2,128]{2,1,0:T(2,128)S(1)} %block_stats.1), channel_id=1, replica_groups=mesh['y'=8,'z'=8,'x'=4,'c'=2] {'z','c'}, dimensions={0} | all-to-all | bytes 32768 | tf_op jit(solution)/shard_map/all_to_all | solution.py:283
  126.5 0.8 middle_stats.1
  127.3 9.5 %all-to-all-start.4 = ((f32[32,1,128]{2,1,0:T(1,128)}), f32[32,1,128]{2,1,0:T(1,128)S(1)}, u32[]{:S(2)}, u32[]{:S(2)}) async-start(f32[32,1,128]{2,1,0:T(1,128)} %middle_stats.1), calls=%async_computation.4 | async-start | bytes 32768 | tf_op jit(solution)/shard_map/all_to_all | solution.py:298
  136.8 3.1 %collective-permute-start = (f32[16,128]{1,0:T(8,128)S(1)}, f32[16,128]{1,0:T(8,128)S(1)}, u32[]{:S(2)}, u32[]{:S(2)}) collective-permute-start(f32[16,128]{1,0:T(8,128)S(1)} %get-tuple-element.10.carried_ref), channel_id=1, source_target_pairs={{0,0},{1,32},{2,8},{3,56},{4,16},{5,48},{6,24},{7,40},{8,10},{9,42... | collective-permute-start | bytes 24584 | tf_op jit(solution)/shard_map/ppermute | solution.py:290
  139.9 0.0 collective-permute-done.2
  139.9 5.4 %collective-permute-done.carried_ref = f32[16,128]{1,0:T(8,128)S(1)} collective-permute-done((f32[16,128]{1,0:T(8,128)S(1)}, f32[16,128]{1,0:T(8,128)S(1)}, u32[]{:S(2)}, u32[]{:S(2)}) %collective-permute-start) | collective-permute-done | bytes 8224 | tf_op jit(solution)/shard_map/ppermute | solution.py:290
  145.4 0.0 all-to-all-done.4.totals_ref
  145.4 1.2 shrink.1
  (3 shorter events, 0.1 us)
Async XLA Ops:
  67.3 20.2 %collective-permute-start.1 = (bf16[64,2,8,1024]{3,2,1,0:T(8,128)(2,1)}, bf16[64,2,8,1024]{3,2,1,0:T(8,128)(2,1)}, u32[]{:S(2)}, u32[]{:S(2)}) collective-permute-start(bf16[64,2,8,1024]{3,2,1,0:T(8,128)(2,1)} %all_to_all.25.x_ref), channel_id=1, source_target_pairs={{0,1},{1,0},{2,3},{3,2},{4,5},{5,4},{6,7},{7,6},{8,9},{9,8},{10,11... | collective-permute-start | bytes 6291464 | tf_op jit(solution)/shard_map/ppermute | solution.py:232
  89.7 25.1 %copy-start = (s32[8]{0:T(128)S(1)}, s32[8]{0:T(128)}, u32[]{:S(2)}) copy-start(s32[8]{0:T(128)} %constant.65.clone) | copy-start | bytes 100
  106.5 33.3 %collective-permute-start.2 = (f16[128,1024]{1,0:T(8,128)(2,1)S(1)}, f16[128,1024]{1,0:T(8,128)(2,1)S(1)}, u32[]{:S(2)}, u32[]{:S(2)}) collective-permute-start(f16[128,1024]{1,0:T(8,128)(2,1)S(1)} %convert_element_type.84), channel_id=1, source_target_pairs={{0,0},{1,32},{2,8},{3,56},{4,16},{5,48},{6,24},{7,40},{8,10},{9,42... | collective-permute-start | bytes 786440 | tf_op jit(solution)/shard_map/ppermute | solution.py:289
  127.3 18.1 %all-to-all-start.4 = ((f32[32,1,128]{2,1,0:T(1,128)}), f32[32,1,128]{2,1,0:T(1,128)S(1)}, u32[]{:S(2)}, u32[]{:S(2)}) async-start(f32[32,1,128]{2,1,0:T(1,128)} %middle_stats.1), calls=%async_computation.4 | async-start | bytes 32768 | tf_op jit(solution)/shard_map/all_to_all | solution.py:298
  136.8 8.6 %collective-permute-start = (f32[16,128]{1,0:T(8,128)S(1)}, f32[16,128]{1,0:T(8,128)S(1)}, u32[]{:S(2)}, u32[]{:S(2)}) collective-permute-start(f32[16,128]{1,0:T(8,128)S(1)} %get-tuple-element.10.carried_ref), channel_id=1, source_target_pairs={{0,0},{1,32},{2,8},{3,56},{4,16},{5,48},{6,24},{7,40},{8,10},{9,42... | collective-permute-start | bytes 24584 | tf_op jit(solution)/shard_map/ppermute | solution.py:290

commit v9 on v8

--- a/solution.py
+++ b/solution.py
@@ -20,8 +20,7 @@
 NF = NX * NC
 SHIFT = (0, 4, 1, 7, 2, 6, 3, 5)
 COLUMN = tuple(2 * (z % 4) + z // 4 for z in range(NZ))
-HOLDER = tuple(COLUMN.index(block) for block in range(NZ))
-OFF, SECOND, MEANS = 64, 65, 66
+OFF, SECOND, MEAN = range(3)
 F16 = jnp.float16
 IN_VMEM = pl.BlockSpec(memory_space=pltpu.VMEM)
 IN_SMEM = pl.BlockSpec(memory_space=pltpu.SMEM)
@@ -29,38 +28,34 @@
 
 def deal_kernel(core_ref, x_ref, out_ref):
     block = out_ref.shape[3]
+    each = out_ref.shape[0] // NZ
+    step = pl.program_id(0)
 
     def deal(core):
         order = [2 * x + core for x in range(NX)] + [2 * x + 1 - core for x in range(NX)]
-        for b in range(NY):
-            whole = x_ref[:, b * block : (b + 1) * block]
-            cuts = [whole[:, k * LANES : (k + 1) * LANES] for k in range(NF)]
+        for j in range(each):
+            start = pl.multiple_of((step * each + j) * block, block)
+            cuts = [x_ref[:, pl.ds(start + k * LANES, LANES)] for k in range(NF)]
             for z in range(NZ):
                 for place, f in enumerate(order):
-                    out_ref[b * NZ + z, 0, :, place * LANES : (place + 1) * LANES] = cuts[
+                    out_ref[j * NZ + z, 0, :, place * LANES : (place + 1) * LANES] = cuts[
                         (z + SHIFT[f]) % NZ
                     ]
-            for y in range(NY):
-                out_ref[y * NZ + HOLDER[b], 1] = whole
 
     for core in range(NC):
         pl.when(core_ref[0] == core)(functools.partial(deal, core))
-
-
-def sums_kernel(core_ref, x_ref, told_ref):
-    _, _, _, block = x_ref.shape
-    far = jnp.zeros((1, LANES), F32)
-    lines = []
-    for part in range(2):
-        for k in range(block // LANES):
-            at = slice(k * LANES, (k + 1) * LANES)
-            value = x_ref[:, part, :, at]
-            line = jnp.sum(jnp.sum(value.astype(F32), axis=0), axis=0, keepdims=True)
-            high = jnp.max(jnp.max(value, axis=0).astype(F32), axis=0, keepdims=True)
-            low = jnp.min(jnp.min(value, axis=0).astype(F32), axis=0, keepdims=True)
-            far = jnp.maximum(far, high - low)
-            lines.append(line)
-    far = jnp.max(far, axis=1, keepdims=True)
+    for z in range(NZ):
+        whole = x_ref[:, COLUMN[z] * block : (COLUMN[z] + 1) * block]
+        for j in range(each):
+            out_ref[j * NZ + z, 1] = whole
+
+
+def tell_kernel(core_ref, sums_ref, wide_ref, told_ref):
+    far = jnp.max(wide_ref[...], axis=1, keepdims=True)
+    far = 2.0 * jnp.max(far, axis=0, keepdims=True)
+    lines = [
+        sums_ref[part : part + 1, k * LANES : (k + 1) * LANES] for part in range(2) for k in range(NF)
+    ]
     dealt = jnp.concatenate(lines[:NF], axis=0)
     swapped = jnp.concatenate(lines[NX:NF] + lines[:NX], axis=0)
     plain = jnp.where(core_ref[0] == 0, dealt, swapped)
@@ -107,7 +102,7 @@
     return jnp.where(slot == k, value, row)
 
 
-def block_kernel(place_ref, sum_ref, norms_ref, carried_ref, message_ref):
+def block_kernel(place_ref, sum_ref, carried_ref, message_ref):
     width, block = sum_ref.shape
     lane = lax.broadcasted_iota(jnp.int32, (8, block), 1)
     sub = lax.broadcasted_iota(jnp.int32, (8, block), 0)
@@ -129,38 +124,17 @@
     flag = jnp.where(first >= 0, 1.0, 0.0)
     mean = add_all(diagonal) / width
     apart = jnp.where(own, diagonal - mean, 0.0)
-    row = in_lane(OFF, add_all(off), norms_ref[...])
+    row = in_lane(OFF, add_all(off), jnp.zeros((1, LANES), F32))
     row = in_lane(SECOND, add_all(apart * apart) * flag, row)
-    row = in_lane(MEANS, mean * flag, row)
-    flags = in_lane(MEANS, flag, jnp.zeros((1, LANES), F32))
+    row = in_lane(MEAN, mean * flag, row)
+    message_ref[...] = jnp.broadcast_to(row[None], message_ref.shape)
+
+
+def middle_kernel(seen_ref, norms_ref, message_ref):
+    row = jnp.sum(seen_ref[...], axis=0)
     message_ref[...] = jnp.broadcast_to(
-        jnp.concatenate((row, flags), axis=0)[None], message_ref.shape
-    )
-
-
-def middle_kernel(seen_ref, message_ref, *, width):
-    seen = seen_ref[...]
-    slot = lax.broadcasted_iota(jnp.int32, (1, 1, LANES), 2)
-    values, flags = seen[:, 0:1, :], seen[:, 1:2, :]
-    norms = jnp.sum(values.reshape(NZ, NC, 1, LANES), axis=0)
-    norms = jnp.where(slot < OFF, norms, 0.0)
-    total = jnp.sum(values, axis=0)
-    is_mean = slot == MEANS
-
-    def lanes(row):
-        return jnp.sum(row, axis=1, keepdims=True)
-
-    mean = lanes(jnp.where(is_mean[0], total, 0.0)) / NC
-    apart = jnp.where(is_mean, (values - mean[None]) * flags, 0.0)
-    between = lanes(jnp.sum(apart * apart, axis=0))
-    second = lanes(jnp.where(slot[0] == SECOND, total, 0.0)) + width * between
-    row = jnp.zeros((1, LANES), F32)
-    row = in_lane(0, lanes(jnp.sum(norms, axis=0)), row)
-    row = in_lane(1, lanes(jnp.sum(norms * norms, axis=0)), row)
-    row = in_lane(2, lanes(jnp.where(slot[0] == OFF, total, 0.0)), row)
-    row = in_lane(3, mean, row)
-    row = in_lane(4, second, row)
-    message_ref[...] = jnp.broadcast_to(row[None], message_ref.shape)
+        jnp.concatenate((norms_ref[...], row), axis=0)[None], message_ref.shape
+    )
 
 
 def shrink_kernel(
@@ -169,18 +143,22 @@
     width, block = shrunk_ref.shape
     first = place_ref[0]
     slot = lax.broadcasted_iota(jnp.int32, (1, LANES), 1)
-    totals = totals_ref[...]
-    sums = jnp.sum(totals, axis=0)
+    lines = totals_ref.shape[1] - 1
+    norms = jnp.sum(totals_ref[:, :lines].reshape(NZ, NF, lines, LANES), axis=0)
+    trace_total = add_all(jnp.sum(norms, axis=0))
+    fourth_total = add_all(jnp.sum(norms * norms, axis=0))
+    scalars = totals_ref[:, lines:]
+    sums = jnp.sum(scalars, axis=0)
 
     def pick(row, k):
         return jnp.sum(jnp.where(slot == k, row, 0.0), axis=1, keepdims=True)
 
-    mu_scale = pick(sums, 0) / (rows * factors)
-    apart = totals - mu_scale[None]
-    from_mu = pick(jnp.sum(apart * apart, axis=0), 3)
-    spread = (pick(sums, 2) + pick(sums, 4) + NC * width * from_mu) / factors
+    mu_scale = trace_total / (rows * factors)
+    apart = scalars - mu_scale[None]
+    from_mu = pick(jnp.sum(apart * apart, axis=0), MEAN)
+    spread = (pick(sums, OFF) + pick(sums, SECOND) + width * from_mu) / factors
     norm_sq = factors * (spread + mu_scale * mu_scale)
-    beta_value = (pick(sums, 1) / rows - norm_sq) / (factors * rows)
+    beta_value = (fourth_total / rows - norm_sq) / (factors * rows)
     shrinkage = beta_value / spread
     value_ref[...] = shrinkage
     mean_ref[...] = carried_ref[:NF, :]
@@ -220,23 +198,28 @@
     shapes = jax.ShapeDtypeStruct
 
     core = c_idx.reshape(1)
+    steps = 4
     dealt = pl.pallas_call(
         deal_kernel,
-        out_shape=pltpu.VMEM((plane, 2, row_count, block), BF16),
+        grid=(steps,),
+        out_shape=shapes((plane, 2, row_count, block), BF16),
         in_specs=[IN_SMEM, IN_VMEM],
-        out_specs=IN_VMEM,
+        out_specs=pl.BlockSpec((plane // steps, 2, row_count, block), lambda i: (i, 0, 0, 0)),
         name="deal",
     )(core, scenarios)
     arrived = exchange(dealt, PLANE)
 
     swapped = lax.ppermute(arrived, "c", flip(NC))
+    values = arrived.astype(F32)
+    sums = jnp.sum(values, axis=(0, 2))
+    wide = jnp.max(jnp.abs(values - values[:1, :, :1]), axis=(0, 2))
     told = pl.pallas_call(
-        sums_kernel,
-        out_shape=pltpu.VMEM((NF, 3 * NF, LANES), F32),
-        in_specs=[IN_SMEM, IN_VMEM],
+        tell_kernel,
+        out_shape=shapes((NF, 3 * NF, LANES), F32),
+        in_specs=[IN_SMEM, IN_VMEM, IN_VMEM],
         out_specs=IN_VMEM,
-        name="sums",
-    )(core, in_vmem(arrived))
+        name="tell",
+    )(core, in_vmem(sums), in_vmem(wide))
     told = exchange(told, LINE)
     mean_half, mean_c, carried, scale = pl.pallas_call(
         functools.partial(means_kernel, rows=total_rows, held=part_rows),
@@ -263,10 +246,8 @@
     pieces = exchange(parcel.reshape(NX, width, block), "x")
     summed = jnp.sum(pieces.astype(F32), axis=0)
 
-    mine = lax.dynamic_slice_in_dim(arrived, y_idx * NZ, NZ, 0)[:, 1]
-    mine = (mine.astype(F32) - mean_c).astype(BF16).astype(F32)
-    norms = jnp.sum(mine * mine, axis=2).reshape(1, NZ * row_count)
-    norms = jnp.pad(norms, ((0, 0), (0, LANES - NZ * row_count)))
+    mine = (arrived[:, 1].astype(F32) - mean_c).astype(BF16).astype(F32)
+    norms = jnp.sum(mine * mine, axis=2).reshape(part_rows // LANES, LANES)
 
     shift = jnp.array(SHIFT, jnp.int32)[f_idx]
     column = 2 * (z_idx % 4) + z_idx // 4
@@ -274,13 +255,13 @@
     first = jnp.where(y_idx == column, (z_idx + shift) % NZ * width, never)
     message = pl.pallas_call(
         block_kernel,
-        out_shape=pltpu.VMEM((NZ * NC, 2, LANES), F32),
-        in_specs=[IN_SMEM, IN_VMEM, IN_VMEM, IN_VMEM],
+        out_shape=shapes((NY, 1, LANES), F32),
+        in_specs=[IN_SMEM, IN_VMEM, IN_VMEM],
         out_specs=IN_VMEM,
         name="block_stats",
-    )(first.reshape(1), in_vmem(summed), in_vmem(norms), in_vmem(carried))
-
-    seen = exchange(message, ("z", "c"))
+    )(first.reshape(1), in_vmem(summed), in_vmem(carried))
+
+    seen = exchange(message, "y")
 
     def owner(z, f):
         return ((z + SHIFT[f]) % NZ) * NF + COLUMN[z]
@@ -289,13 +270,13 @@
     owned = lax.ppermute(summed.astype(F16), SLAB, moves).astype(F32)
     carried = lax.ppermute(carried, SLAB, moves)
     second = pl.pallas_call(
-        functools.partial(middle_kernel, width=width),
-        out_shape=pltpu.VMEM((NY * NX, 1, LANES), F32),
-        in_specs=[IN_VMEM],
+        middle_kernel,
+        out_shape=shapes((NZ * NF, part_rows // LANES + 1, LANES), F32),
+        in_specs=[IN_VMEM, IN_VMEM],
         out_specs=IN_VMEM,
         name="middle_stats",
-    )(in_vmem(seen))
-    totals = exchange(second, ("y", "x"))
+    )(in_vmem(seen), in_vmem(norms))
+    totals = exchange(second, SLAB)
 
     first_own = jnp.where(y_idx == f_idx, z_idx * width, never)
     shrunk, shrinkage, col_mean = pl.pallas_call(

time: 148 us -> 157 us (1.061)
  the two profiles are of different devices: /device:TPU:1 before, /device:TPU:3 now
where the time goes in v9:
time: 157 us
  blocking collectives  73.8 us (47%)
  starting transfers between devices  38 us (24%)
  waiting for transfers between devices  29.8 us (19%)
  Pallas kernels  6.52 us (4%)
  matrix products  3.98 us (3%)
  other arithmetic  2.46 us (2%)
    all_to_all x1, blocking collectives, shrinkage_step(): arrived = exchange(dealt, PLANE)  65.4 us
    all_to_all x1, waiting for transfers between devices, shrinkage_step(): pieces = exchange(parcel.reshape(NX, width, block), 'x')  12 us
    ppermute x1, waiting for transfers between devices, shrinkage_step(): owned = lax.ppermute(summed.astype(F16), SLAB, moves).astype(F32)  11.6 us
    all_to_all x1, starting transfers between devices, shrinkage_step(): totals = exchange(second, SLAB)  11.1 us
    all_to_all x1, blocking collectives, shrinkage_step(): told = exchange(told, LINE)  8.46 us
    all_to_all x1, starting transfers between devices, shrinkage_step(): seen = exchange(message, 'y')  6.62 us
    all_to_all x1, waiting for transfers between devices, shrinkage_step(): seen = exchange(message, 'y')  6.05 us
    ppermute x1, starting transfers between devices, shrinkage_step(): swapped = lax.ppermute(arrived, 'c', flip(NC))  5.59 us
  transfers between devices with their start and end apart: 6, of which 3 were waited for; matrix products, arithmetic and copies ran while one was open for 2% of the time, Pallas kernels for 1%

profile of v9, /device:TPU:3, one launch (start us, length us, event | category | flops | bytes accessed | tf_op | source)
XLA Modules:
  0.0 156.7 jit_solution(2354477246580034971)
XLA Ops:
  0.6 2.8 %deal.1 = bf16[64,2,8,1024]{3,2,1,0:T(8,128)(2,1)} custom-call(s32[1]{0:T(128)} %bitcast.1.core_ref, bf16[8,8192]{1,0:T(8,128)(2,1)} %x_ref.1), custom_call_target="tpu_custom_call" | custom-call | tf_op jit(solution)/shard_map/deal/pallas_call | solution.py:202
  3.5 65.4 %all_to_all.25 = bf16[64,2,8,1024]{3,2,1,0:T(8,128)(2,1)S(1)} all-to-all(bf16[64,2,8,1024]{3,2,1,0:T(8,128)(2,1)} %deal.1), channel_id=1, replica_groups=mesh['y'=8,'z'=8,'x'=4,'c'=2] {'y','z'}, dimensions={0} | all-to-all | bytes 4194304 | tf_op jit(solution)/shard_map/all_to_all | solution.py:210
  68.9 5.6 %collective-permute-start.1 = (bf16[64,2,8,1024]{3,2,1,0:T(8,128)(2,1)S(1)}, bf16[64,2,8,1024]{3,2,1,0:T(8,128)(2,1)}, u32[]{:S(2)}, u32[]{:S(2)}) collective-permute-start(bf16[64,2,8,1024]{3,2,1,0:T(8,128)(2,1)S(1)} %all_to_all.25), channel_id=1, source_target_pairs={{0,1},{1,0},{2,3},{3,2},{4,5},{5,4},{6,7},{7,6},{8,9},{9,8},{10,11... | collective-permute-start | bytes 6291464 | tf_op jit(solution)/shard_map/ppermute | solution.py:212
  74.5 0.5 abs_reduce_fusion
  75.0 0.7 tell.1
  75.7 8.5 %all_to_all.26.told_ref = f32[8,24,128]{2,1,0:T(8,128)S(1)} all-to-all(f32[8,24,128]{2,1,0:T(8,128)} %tell.1), channel_id=1, replica_groups=mesh['y'=8,'z'=8,'x'=4,'c'=2] {'x','c'}, dimensions={0} | all-to-all | bytes 196608 | tf_op jit(solution)/shard_map/all_to_all | solution.py:223
  84.2 0.1 means.1
  84.3 0.8 fusion.8
  85.1 0.0 collective-permute-done.1
  85.1 3.2 %fusion.4 = f16[512,1024]{1,0:T(8,128)(2,1)} fusion(f32[512,1024,1]{1,0,2:T(8,128)S(1)} %fusion.8, bf16[64,2,8,1024]{3,2,1,0:T(8,128)(2,1)} %collective-permute-done.1, f32[]{:T(128)S(1)} %bitcast.47, f32[1024]{0:T(1024)S(1)} %bitcast.43, f32[512]{0:T(512)S(1)} %bitcast.46), kind=kOutput, calls=%fused_computation.8 | convolution fusion | flops 540803072 | bytes 4724740 | tf_op jit(solution)/shard_map/dot_general | solution.py:184
  88.3 0.0 copy-start
  88.3 5.5 %all-to-all-start.2 = ((f16[4,128,1024]{2,1,0:T(8,128)(2,1)}), f16[4,128,1024]{2,1,0:T(8,128)(2,1)}, u32[]{:S(2)}, u32[]{:S(2)}) async-start(f16[4,128,1024]{2,1,0:T(8,128)(2,1)} %bitcast.13), calls=%async_computation.2 | async-start | bytes 2097152 | tf_op jit(solution)/shard_map/all_to_all | solution.py:246
  93.8 0.0 copy-done
  93.8 0.6 dynamic_slice.3
  95.1 12.0 %all-to-all-done.2 = f16[4,128,1024]{2,1,0:T(8,128)(2,1)} async-done(((f16[4,128,1024]{2,1,0:T(8,128)(2,1)}), f16[4,128,1024]{2,1,0:T(8,128)(2,1)}, u32[]{:S(2)}, u32[]{:S(2)}) %all-to-all-start.2) | async-done | bytes 1048608 | tf_op jit(solution)/shard_map/all_to_all | solution.py:246
  107.1 1.5 convert_reduce_fusion.sum_ref
  108.6 0.9 block_stats.1
  109.5 6.6 %all-to-all-start.3 = ((f32[8,1,128]{2,1,0:T(1,128)}), f32[8,1,128]{2,1,0:T(1,128)S(1)}, u32[]{:S(2)}, u32[]{:S(2)}) async-start(f32[8,1,128]{2,1,0:T(1,128)} %block_stats.1), calls=%async_computation.3 | async-start | bytes 8192 | tf_op jit(solution)/shard_map/all_to_all | solution.py:264
  116.2 0.3 multiply_reduce_fusion
  116.5 0.1 reshape.43.norms_ref
  116.6 6.0 %all-to-all-done.3.seen_ref = f32[8,1,128]{2,1,0:T(1,128)S(1)} async-done(((f32[8,1,128]{2,1,0:T(1,128)}), f32[8,1,128]{2,1,0:T(1,128)S(1)}, u32[]{:S(2)}, u32[]{:S(2)}) %all-to-all-start.3) | async-done | bytes 4128 | tf_op jit(solution)/shard_map/all_to_all | solution.py:264
  122.6 0.7 middle_stats.1
  123.4 11.1 %all-to-all-start.4 = ((f32[64,5,128]{2,1,0:T(8,128)}), f32[64,5,128]{2,1,0:T(8,128)S(1)}, u32[]{:S(2)}, u32[]{:S(2)}) async-start(f32[64,5,128]{2,1,0:T(8,128)} %middle_stats.1), calls=%async_computation.4 | async-start | bytes 524288 | tf_op jit(solution)/shard_map/all_to_all | solution.py:279
  134.5 4.8 %collective-permute-start.2 = (f16[128,1024]{1,0:T(8,128)(2,1)S(1)}, f16[128,1024]{1,0:T(8,128)(2,1)S(1)}, u32[]{:S(2)}, u32[]{:S(2)}) collective-permute-start(f16[128,1024]{1,0:T(8,128)(2,1)S(1)} %convert_element_type.86), channel_id=1, source_target_pairs={{0,0},{1,32},{2,8},{3,56},{4,16},{5,48},{6,24},{7,40},{8,10},{9,42... | collective-permute-start | bytes 786440 | tf_op jit(solution)/shard_map/ppermute | solution.py:270
  139.4 4.3 %collective-permute-start = (f32[16,128]{1,0:T(8,128)S(1)}, f32[16,128]{1,0:T(8,128)S(1)}, u32[]{:S(2)}, u32[]{:S(2)}) collective-permute-start(f32[16,128]{1,0:T(8,128)S(1)} %get-tuple-element.10.carried_ref), channel_id=1, source_target_pairs={{0,0},{1,32},{2,8},{3,56},{4,16},{5,48},{6,24},{7,40},{8,10},{9,42... | collective-permute-start | bytes 24584 | tf_op jit(solution)/shard_map/ppermute | solution.py:271
  143.8 11.6 %collective-permute-done.2 = f16[128,1024]{1,0:T(8,128)(2,1)S(1)} collective-permute-done((f16[128,1024]{1,0:T(8,128)(2,1)S(1)}, f16[128,1024]{1,0:T(8,128)(2,1)S(1)}, u32[]{:S(2)}, u32[]{:S(2)}) %collective-permute-start.2) | collective-permute-done | bytes 262176 | tf_op jit(solution)/shard_map/ppermute | solution.py:270
  155.4 0.0 collective-permute-done.carried_ref
  155.5 0.0 all-to-all-done.4.totals_ref
  155.5 1.2 shrink.1
  (4 shorter events, 0.1 us)
Async XLA Ops:
  68.9 16.2 %collective-permute-start.1 = (bf16[64,2,8,1024]{3,2,1,0:T(8,128)(2,1)S(1)}, bf16[64,2,8,1024]{3,2,1,0:T(8,128)(2,1)}, u32[]{:S(2)}, u32[]{:S(2)}) collective-permute-start(bf16[64,2,8,1024]{3,2,1,0:T(8,128)(2,1)S(1)} %all_to_all.25), channel_id=1, source_target_pairs={{0,1},{1,0},{2,3},{3,2},{4,5},{5,4},{6,7},{7,6},{8,9},{9,8},{10,11... | collective-permute-start | bytes 6291464 | tf_op jit(solution)/shard_map/ppermute | solution.py:212
  88.3 5.5 %copy-start = (s32[8]{0:T(128)S(1)}, s32[8]{0:T(128)}, u32[]{:S(2)}) copy-start(s32[8]{0:T(128)} %constant.64.clone) | copy-start | bytes 100
  88.3 18.8 %all-to-all-start.2 = ((f16[4,128,1024]{2,1,0:T(8,128)(2,1)}), f16[4,128,1024]{2,1,0:T(8,128)(2,1)}, u32[]{:S(2)}, u32[]{:S(2)}) async-start(f16[4,128,1024]{2,1,0:T(8,128)(2,1)} %bitcast.13), calls=%async_computation.2 | async-start | bytes 2097152 | tf_op jit(solution)/shard_map/all_to_all | solution.py:246
  109.5 13.1 %all-to-all-start.3 = ((f32[8,1,128]{2,1,0:T(1,128)}), f32[8,1,128]{2,1,0:T(1,128)S(1)}, u32[]{:S(2)}, u32[]{:S(2)}) async-start(f32[8,1,128]{2,1,0:T(1,128)} %block_stats.1), calls=%async_computation.3 | async-start | bytes 8192 | tf_op jit(solution)/shard_map/all_to_all | solution.py:264
  123.4 32.1 %all-to-all-start.4 = ((f32[64,5,128]{2,1,0:T(8,128)}), f32[64,5,128]{2,1,0:T(8,128)S(1)}, u32[]{:S(2)}, u32[]{:S(2)}) async-start(f32[64,5,128]{2,1,0:T(8,128)} %middle_stats.1), calls=%async_computation.4 | async-start | bytes 524288 | tf_op jit(solution)/shard_map/all_to_all | solution.py:279
  134.5 20.9 %collective-permute-start.2 = (f16[128,1024]{1,0:T(8,128)(2,1)S(1)}, f16[128,1024]{1,0:T(8,128)(2,1)S(1)}, u32[]{:S(2)}, u32[]{:S(2)}) collective-permute-start(f16[128,1024]{1,0:T(8,128)(2,1)S(1)} %convert_element_type.86), channel_id=1, source_target_pairs={{0,0},{1,32},{2,8},{3,56},{4,16},{5,48},{6,24},{7,40},{8,10},{9,42... | collective-permute-start | bytes 786440 | tf_op jit(solution)/shard_map/ppermute | solution.py:270
  139.4 16.1 %collective-permute-start = (f32[16,128]{1,0:T(8,128)S(1)}, f32[16,128]{1,0:T(8,128)S(1)}, u32[]{:S(2)}, u32[]{:S(2)}) collective-permute-start(f32[16,128]{1,0:T(8,128)S(1)} %get-tuple-element.10.carried_ref), channel_id=1, source_target_pairs={{0,0},{1,32},{2,8},{3,56},{4,16},{5,48},{6,24},{7,40},{8,10},{9,42... | collective-permute-start | bytes 24584 | tf_op jit(solution)/shard_map/ppermute | solution.py:271

commit v10 on v7

--- a/solution.py
+++ b/solution.py
@@ -47,30 +47,15 @@
         pl.when(core_ref[0] == core)(functools.partial(deal, core))
 
 
-def sums_kernel(core_ref, x_ref, told_ref):
-    plane, _, rows, block = x_ref.shape
-    core = core_ref[0]
-    far = jnp.zeros((rows, LANES), F32)
-    lines = []
-    for part in range(2):
-        pivot = jnp.broadcast_to(x_ref[0, part].astype(F32)[0:1], (rows, block))
-
-        def one(p, carry):
-            total, wide = carry
-            value = x_ref[p, part].astype(F32)
-            return total + value, jnp.maximum(wide, jnp.abs(value - pivot))
-
-        zero = jnp.zeros((rows, block), F32)
-        total, wide = lax.fori_loop(0, plane, one, (zero, zero), unroll=2)
-        total = jnp.sum(total, axis=0, keepdims=True)
-        for k in range(block // LANES):
-            cut = slice(k * LANES, (k + 1) * LANES)
-            far = jnp.maximum(far, wide[:, cut])
-            lines.append(total[:, cut])
-    far = jnp.max(jnp.max(far, axis=1, keepdims=True), axis=0, keepdims=True)
+def tell_kernel(core_ref, sums_ref, wide_ref, told_ref):
+    far = jnp.max(wide_ref[...], axis=1, keepdims=True)
+    far = 2.0 * jnp.max(far, axis=0, keepdims=True)
+    lines = [
+        sums_ref[part : part + 1, k * LANES : (k + 1) * LANES] for part in range(2) for k in range(NF)
+    ]
     dealt = jnp.concatenate(lines[:NF], axis=0)
     swapped = jnp.concatenate(lines[NX:NF] + lines[:NX], axis=0)
-    plain = jnp.where(core == 0, dealt, swapped)
+    plain = jnp.where(core_ref[0] == 0, dealt, swapped)
     out = jnp.concatenate(
         [plain] + lines[NF:] + [jnp.broadcast_to(far, (8, LANES))], axis=0
     )
@@ -87,7 +72,7 @@
     def top(value):
         return jnp.max(jnp.max(value, axis=1, keepdims=True), axis=0, keepdims=True)
 
-    reach = 2.0 * top(jnp.max(told[:, 2 * NF :], axis=0)) + top(apart)
+    reach = top(jnp.max(told[:, 2 * NF :], axis=0)) + top(apart)
     power = half_power(reach * reach)
     mine = jnp.where(core_ref[0] == 0, means[:NX], means[NX:NF])
     for k in range(NX):
@@ -237,13 +222,16 @@
     arrived = exchange(dealt, PLANE)
 
     swapped = lax.ppermute(arrived, "c", flip(NC))
+    values = arrived.astype(F32)
+    sums = jnp.sum(values, axis=(0, 2))
+    wide = jnp.max(jnp.abs(values - values[:1, :, :1]), axis=(0, 2))
     told = pl.pallas_call(
-        sums_kernel,
-        out_shape=pltpu.VMEM((NF, 3 * NF, LANES), F32),
-        in_specs=[IN_SMEM, IN_VMEM],
+        tell_kernel,
+        out_shape=shapes((NF, 3 * NF, LANES), F32),
+        in_specs=[IN_SMEM, IN_VMEM, IN_VMEM],
         out_specs=IN_VMEM,
-        name="sums",
-    )(core, in_vmem(arrived))
+        name="tell",
+    )(core, in_vmem(sums), in_vmem(wide))
     told = exchange(told, LINE)
     mean_half, mean_c, carried, scale = pl.pallas_call(
         functools.partial(means_kernel, rows=total_rows, held=part_rows),

time: 149 us -> 149 us (level)
  other arithmetic: 1.34 us -> 3.46 us
  Pallas kernels: 6.9 us -> 4.94 us
    reduce_max x0 -> x1, other arithmetic: none -> 2.11 us  [shrinkage_step(): wide = jnp.max(jnp.abs(values - values[:1, :, :1]), axis=(0, 2))]
    pallas_call x1, Pallas kernels: 2.71 us -> 0.74 us  [shrinkage_step(): pl.pallas_call(tell_kernel, out_shape=shapes((NF, 3 * NF, LANES), F32), i...]
  transfers between devices with their start and end apart: 5 -> 5, of which waited for: 2 -> 2; matrix products, arithmetic and copies ran while one was open for 3% -> 4% of each run, Pallas kernels for 3% -> 2%
where the time goes in v10:
time: 149 us; the launch traced here: 148 us
  blocking collectives  91.4 us (61%)
  starting transfers between devices  33.4 us (22%)
  waiting for transfers between devices  8.96 us (6%)
  Pallas kernels  4.94 us (3%)
  other arithmetic  3.46 us (2%)
  matrix products  2.98 us (2%)
    all_to_all x1, blocking collectives, shrinkage_step(): arrived = exchange(dealt, PLANE)  65.5 us
    all_to_all x1, blocking collectives, shrinkage_step(): pieces = exchange(parcel.reshape(NX, width, block), 'x')  16.5 us
    all_to_all x1, blocking collectives, shrinkage_step(): told = exchange(told, LINE)  9.39 us
    ppermute x1, starting transfers between devices, shrinkage_step(): owned = lax.ppermute(summed.astype(F16), SLAB, moves).astype(F32)  8.21 us
    ppermute x1, starting transfers between devices, shrinkage_step(): carried = lax.ppermute(carried, SLAB, moves)  7.55 us
    all_to_all x1, starting transfers between devices, shrinkage_step(): totals = exchange(second, 'y')  6.51 us
    all_to_all x1, waiting for transfers between devices, shrinkage_step(): totals = exchange(second, 'y')  6.42 us
    ppermute x1, starting transfers between devices, shrinkage_step(): swapped = lax.ppermute(arrived, 'c', flip(NC))  6.21 us
  transfers between devices with their start and end apart: 5, of which 2 were waited for; matrix products, arithmetic and copies ran while one was open for 4% of the time, Pallas kernels for 2%

profile of v10, /device:TPU:1, one launch (start us, length us, event | category | flops | bytes accessed | tf_op | source)
XLA Modules:
  0.0 148.1 jit_solution(4885093322218799819)
XLA Ops:
  0.6 1.1 deal.1
  1.8 65.5 %all_to_all.25 = bf16[64,2,8,1024]{3,2,1,0:T(8,128)(2,1)} all-to-all(bf16[64,2,8,1024]{3,2,1,0:T(8,128)(2,1)S(1)} %deal.1), channel_id=1, replica_groups=mesh['y'=8,'z'=8,'x'=4,'c'=2] {'y','z'}, dimensions={0} | all-to-all | bytes 4194304 | tf_op jit(solution)/shard_map/all_to_all | solution.py:222
  67.3 0.8 slice.28
  68.0 6.2 %collective-permute-start.1 = (bf16[64,2,8,1024]{3,2,1,0:T(8,128)(2,1)}, bf16[64,2,8,1024]{3,2,1,0:T(8,128)(2,1)S(1)}, u32[]{:S(2)}, u32[]{:S(2)}) collective-permute-start(bf16[64,2,8,1024]{3,2,1,0:T(8,128)(2,1)} %all_to_all.25), channel_id=1, source_target_pairs={{0,1},{1,0},{2,3},{3,2},{4,5},{5,4},{6,7},{7,6},{8,9},{9,8},{10,11... | collective-permute-start | bytes 6291464 | tf_op jit(solution)/shard_map/ppermute | solution.py:224
  74.2 2.1 %abs_reduce_fusion = (f32[2,1024]{1,0:T(2,128)S(1)}, f32[2,1024]{1,0:T(2,128)S(1)}) fusion(f32[2,1024]{1,0:T(2,128)S(1)} %bitcast.46, bf16[64,2,8,1024]{3,2,1,0:T(8,128)(2,1)} %all_to_all.25), kind=kLoop, calls=%fused_computation | loop fusion | flops 5238784 | bytes 2121728 | tf_op jit(solution)/shard_map/reduce_max | solution.py:227
  76.4 0.7 tell.1
  77.1 9.4 %all_to_all.26.told_ref = f32[8,24,128]{2,1,0:T(8,128)S(1)} all-to-all(f32[8,24,128]{2,1,0:T(8,128)} %tell.1), channel_id=1, replica_groups=mesh['y'=8,'z'=8,'x'=4,'c'=2] {'x','c'}, dimensions={0} | all-to-all | bytes 196608 | tf_op jit(solution)/shard_map/all_to_all | solution.py:235
  86.5 0.1 means.1
  86.6 2.2 %fusion.3 = f32[512,1024,1]{1,0,2:T(8,128)S(1)} fusion(bf16[64,2,8,1024]{3,2,1,0:T(8,128)(2,1)} %all_to_all.25, f32[1024]{0:T(1024)S(1)} %bitcast.39, f32[512]{0:T(512)S(1)} %bitcast.42), kind=kOutput, calls=%fused_computation.9 | convolution fusion | flops 539230208 | bytes 3676160 | tf_op jit(solution)/shard_map/dot_general | solution.py:198
  88.8 0.0 collective-permute-done.1
  88.8 0.8 fusion.1
  89.6 0.0 copy-start
  89.6 16.5 %all_to_all.27 = f16[4,128,1024]{2,1,0:T(8,128)(2,1)S(1)} all-to-all(f16[4,128,1024]{2,1,0:T(8,128)(2,1)S(1)} %bitcast.45), channel_id=1, replica_groups=mesh['y'=8,'z'=8,'x'=4,'c'=2] {'x'}, dimensions={0} | all-to-all | bytes 2097152 | tf_op jit(solution)/shard_map/all_to_all | solution.py:258
  106.2 0.3 convert_reduce_fusion.sum_ref
  106.5 8.2 %collective-permute-start.2 = (f16[128,1024]{1,0:T(8,128)(2,1)S(1)}, f16[128,1024]{1,0:T(8,128)(2,1)S(1)}, u32[]{:S(2)}, u32[]{:S(2)}) collective-permute-start(f16[128,1024]{1,0:T(8,128)(2,1)S(1)} %convert_element_type.88), channel_id=1, source_target_pairs={{0,0},{1,32},{2,8},{3,56},{4,16},{5,48},{6,24},{7,40},{8,10},{9,42... | collective-permute-start | bytes 786440 | tf_op jit(solution)/shard_map/ppermute | solution.py:284
  114.7 0.0 copy-done
  114.7 0.6 dynamic_slice.6
  116.0 1.0 multiply_reduce_fusion
  117.0 0.1 reshape.43
  117.1 1.0 block_stats.1
  118.1 4.9 %all-to-all-start.3 = ((f32[64,2,128]{2,1,0:T(2,128)}), f32[64,2,128]{2,1,0:T(2,128)S(1)}, u32[]{:S(2)}, u32[]{:S(2)}) async-start(f32[64,2,128]{2,1,0:T(2,128)} %block_stats.1), calls=%async_computation.3 | async-start | bytes 131072 | tf_op jit(solution)/shard_map/all_to_all | solution.py:278
  123.0 7.5 %collective-permute-start = (f32[16,128]{1,0:T(8,128)S(1)}, f32[16,128]{1,0:T(8,128)S(1)}, u32[]{:S(2)}, u32[]{:S(2)}) collective-permute-start(f32[16,128]{1,0:T(8,128)S(1)} %get-tuple-element.10.carried_ref), channel_id=1, source_target_pairs={{0,0},{1,32},{2,8},{3,56},{4,16},{5,48},{6,24},{7,40},{8,10},{9,42... | collective-permute-start | bytes 24584 | tf_op jit(solution)/shard_map/ppermute | solution.py:285
  130.6 2.5 %all-to-all-done.3.seen_ref = f32[64,2,128]{2,1,0:T(2,128)S(1)} async-done(((f32[64,2,128]{2,1,0:T(2,128)}), f32[64,2,128]{2,1,0:T(2,128)S(1)}, u32[]{:S(2)}, u32[]{:S(2)}) %all-to-all-start.3) | async-done | bytes 65568 | tf_op jit(solution)/shard_map/all_to_all | solution.py:278
  133.1 0.9 middle_stats.1
  134.0 6.5 %all-to-all-start.4 = ((f32[8,1,128]{2,1,0:T(1,128)}), f32[8,1,128]{2,1,0:T(1,128)S(1)}, u32[]{:S(2)}, u32[]{:S(2)}) async-start(f32[8,1,128]{2,1,0:T(1,128)} %middle_stats.1), calls=%async_computation.4 | async-start | bytes 8192 | tf_op jit(solution)/shard_map/all_to_all | solution.py:293
  140.5 0.0 collective-permute-done.2
  140.6 0.0 collective-permute-done.carried_ref
  140.6 6.4 %all-to-all-done.4.totals_ref = f32[8,1,128]{2,1,0:T(1,128)S(1)} async-done(((f32[8,1,128]{2,1,0:T(1,128)}), f32[8,1,128]{2,1,0:T(1,128)S(1)}, u32[]{:S(2)}, u32[]{:S(2)}) %all-to-all-start.4) | async-done | bytes 4128 | tf_op jit(solution)/shard_map/all_to_all | solution.py:293
  147.0 1.1 shrink.1
  (4 shorter events, 0.1 us)
Async XLA Ops:
  68.0 20.7 %collective-permute-start.1 = (bf16[64,2,8,1024]{3,2,1,0:T(8,128)(2,1)}, bf16[64,2,8,1024]{3,2,1,0:T(8,128)(2,1)S(1)}, u32[]{:S(2)}, u32[]{:S(2)}) collective-permute-start(bf16[64,2,8,1024]{3,2,1,0:T(8,128)(2,1)} %all_to_all.25), channel_id=1, source_target_pairs={{0,1},{1,0},{2,3},{3,2},{4,5},{5,4},{6,7},{7,6},{8,9},{9,8},{10,11... | collective-permute-start | bytes 6291464 | tf_op jit(solution)/shard_map/ppermute | solution.py:224
  89.6 25.1 %copy-start = (s32[8]{0:T(128)S(1)}, s32[8]{0:T(128)}, u32[]{:S(2)}) copy-start(s32[8]{0:T(128)} %constant.67.clone) | copy-start | bytes 100
  106.5 34.0 %collective-permute-start.2 = (f16[128,1024]{1,0:T(8,128)(2,1)S(1)}, f16[128,1024]{1,0:T(8,128)(2,1)S(1)}, u32[]{:S(2)}, u32[]{:S(2)}) collective-permute-start(f16[128,1024]{1,0:T(8,128)(2,1)S(1)} %convert_element_type.88), channel_id=1, source_target_pairs={{0,0},{1,32},{2,8},{3,56},{4,16},{5,48},{6,24},{7,40},{8,10},{9,42... | collective-permute-start | bytes 786440 | tf_op jit(solution)/shard_map/ppermute | solution.py:284
  118.1 15.0 %all-to-all-start.3 = ((f32[64,2,128]{2,1,0:T(2,128)}), f32[64,2,128]{2,1,0:T(2,128)S(1)}, u32[]{:S(2)}, u32[]{:S(2)}) async-start(f32[64,2,128]{2,1,0:T(2,128)} %block_stats.1), calls=%async_computation.3 | async-start | bytes 131072 | tf_op jit(solution)/shard_map/all_to_all | solution.py:278
  123.0 17.6 %collective-permute-start = (f32[16,128]{1,0:T(8,128)S(1)}, f32[16,128]{1,0:T(8,128)S(1)}, u32[]{:S(2)}, u32[]{:S(2)}) collective-permute-start(f32[16,128]{1,0:T(8,128)S(1)} %get-tuple-element.10.carried_ref), channel_id=1, source_target_pairs={{0,0},{1,32},{2,8},{3,56},{4,16},{5,48},{6,24},{7,40},{8,10},{9,42... | collective-permute-start | bytes 24584 | tf_op jit(solution)/shard_map/ppermute | solution.py:285
  134.0 13.0 %all-to-all-start.4 = ((f32[8,1,128]{2,1,0:T(1,128)}), f32[8,1,128]{2,1,0:T(1,128)S(1)}, u32[]{:S(2)}, u32[]{:S(2)}) async-start(f32[8,1,128]{2,1,0:T(1,128)} %middle_stats.1), calls=%async_computation.4 | async-start | bytes 8192 | tf_op jit(solution)/shard_map/all_to_all | solution.py:293

commit v11 on v10

--- a/solution.py
+++ b/solution.py
@@ -20,31 +20,36 @@
 NF = NX * NC
 SHIFT = (0, 4, 1, 7, 2, 6, 3, 5)
 COLUMN = tuple(2 * (z % 4) + z // 4 for z in range(NZ))
-HOLDER = tuple(COLUMN.index(block) for block in range(NZ))
 OFF, SECOND, MEANS = 64, 65, 66
 F16 = jnp.float16
 IN_VMEM = pl.BlockSpec(memory_space=pltpu.VMEM)
 IN_SMEM = pl.BlockSpec(memory_space=pltpu.SMEM)
 
 
-def deal_kernel(core_ref, x_ref, out_ref):
+def deal_kernel(core_ref, x_ref, out_ref, held_ref, sems):
     block = out_ref.shape[3]
 
-    def deal(core):
+    def deal(core, b):
         order = [2 * x + core for x in range(NX)] + [2 * x + 1 - core for x in range(NX)]
-        for b in range(NY):
-            whole = x_ref[:, b * block : (b + 1) * block]
-            cuts = [whole[:, k * LANES : (k + 1) * LANES] for k in range(NF)]
-            for z in range(NZ):
-                for place, f in enumerate(order):
-                    out_ref[b * NZ + z, 0, :, place * LANES : (place + 1) * LANES] = cuts[
-                        (z + SHIFT[f]) % NZ
-                    ]
-            for y in range(NY):
-                out_ref[y * NZ + HOLDER[b], 1] = whole
-
-    for core in range(NC):
-        pl.when(core_ref[0] == core)(functools.partial(deal, core))
+        whole = x_ref[:, b * block : (b + 1) * block]
+        cuts = [whole[:, k * LANES : (k + 1) * LANES] for k in range(NF)]
+        for z in range(NZ):
+            for place, f in enumerate(order):
+                held_ref[b * NZ + z, 0, :, place * LANES : (place + 1) * LANES] = cuts[
+                    (z + SHIFT[f]) % NZ
+                ]
+
+    copies = []
+    for b in range(NY):
+        for core in range(NC):
+            pl.when(core_ref[0] == core)(functools.partial(deal, core, b))
+        for z in range(NZ):
+            held_ref[b * NZ + z, 1] = x_ref[:, COLUMN[z] * block : (COLUMN[z] + 1) * block]
+        chunk = pl.ds(b * NZ, NZ)
+        copies.append(pltpu.make_async_copy(held_ref.at[chunk], out_ref.at[chunk], sems.at[b]))
+        copies[-1].start()
+    for copy in copies:
+        copy.wait()
 
 
 def tell_kernel(core_ref, sums_ref, wide_ref, told_ref):
@@ -212,11 +217,13 @@
     shapes = jax.ShapeDtypeStruct
 
     core = c_idx.reshape(1)
+    packet = (plane, 2, row_count, block)
     dealt = pl.pallas_call(
         deal_kernel,
-        out_shape=pltpu.VMEM((plane, 2, row_count, block), BF16),
+        out_shape=shapes(packet, BF16),
         in_specs=[IN_SMEM, IN_VMEM],
-        out_specs=IN_VMEM,
+        out_specs=pl.BlockSpec(memory_space=pltpu.HBM),
+        scratch_shapes=[pltpu.VMEM(packet, BF16), pltpu.SemaphoreType.DMA((NY,))],
         name="deal",
     )(core, scenarios)
     arrived = exchange(dealt, PLANE)

time: 149 us -> 146 us (0.980)
  other arithmetic: 3.46 us -> 0.98 us
    reduce_max x1, other arithmetic: 2.11 us -> 0.53 us  [shrinkage_step(): wide = jnp.max(jnp.abs(values - values[:1, :, :1]), axis=(0, 2))]
  transfers between devices with their start and end apart: 5 -> 5, of which waited for: 2 -> 2; matrix products, arithmetic and copies ran while one was open for 4% -> 1% of each run, Pallas kernels for 2% -> 2%
where the time goes in v11:
time: 146 us
  blocking collectives  91.5 us (63%)
  starting transfers between devices  33.1 us (23%)
  waiting for transfers between devices  8.96 us (6%)
  Pallas kernels  6.17 us (4%)
  matrix products  3 us (2%)
  between operations  1.48 us (1%)
    all_to_all x1, blocking collectives, shrinkage_step(): arrived = exchange(dealt, PLANE)  65.6 us
    all_to_all x1, blocking collectives, shrinkage_step(): pieces = exchange(parcel.reshape(NX, width, block), 'x')  16.5 us
    all_to_all x1, blocking collectives, shrinkage_step(): told = exchange(told, LINE)  9.39 us
    ppermute x1, starting transfers between devices, shrinkage_step(): owned = lax.ppermute(summed.astype(F16), SLAB, moves).astype(F32)  7.87 us
    ppermute x1, starting transfers between devices, shrinkage_step(): carried = lax.ppermute(carried, SLAB, moves)  7.55 us
    all_to_all x1, starting transfers between devices, shrinkage_step(): totals = exchange(second, 'y')  6.6 us
    all_to_all x1, waiting for transfers between devices, shrinkage_step(): totals = exchange(second, 'y')  6.42 us
    ppermute x1, starting transfers between devices, shrinkage_step(): swapped = lax.ppermute(arrived, 'c', flip(NC))  6.22 us
  transfers between devices with their start and end apart: 5, of which 2 were waited for; matrix products, arithmetic and copies ran while one was open for 1% of the time, Pallas kernels for 2%

profile of v11, /device:TPU:1, one launch (start us, length us, event | category | flops | bytes accessed | tf_op | source)
XLA Modules:
  0.0 145.9 jit_solution(5524044178159640890)
XLA Ops:
  0.6 2.4 %deal.1 = bf16[64,2,8,1024]{3,2,1,0:T(8,128)(2,1)} custom-call(s32[1]{0:T(128)} %bitcast.1.core_ref, bf16[8,8192]{1,0:T(8,128)(2,1)} %x_ref.1), custom_call_target="tpu_custom_call" | custom-call | tf_op jit(solution)/shard_map/deal/pallas_call | solution.py:221
  3.0 65.6 %all_to_all.25 = bf16[64,2,8,1024]{3,2,1,0:T(8,128)(2,1)S(1)} all-to-all(bf16[64,2,8,1024]{3,2,1,0:T(8,128)(2,1)} %deal.1), channel_id=1, replica_groups=mesh['y'=8,'z'=8,'x'=4,'c'=2] {'y','z'}, dimensions={0} | all-to-all | bytes 4194304 | tf_op jit(solution)/shard_map/all_to_all | solution.py:229
  68.6 6.2 %collective-permute-start.1 = (bf16[64,2,8,1024]{3,2,1,0:T(8,128)(2,1)S(1)}, bf16[64,2,8,1024]{3,2,1,0:T(8,128)(2,1)}, u32[]{:S(2)}, u32[]{:S(2)}) collective-permute-start(bf16[64,2,8,1024]{3,2,1,0:T(8,128)(2,1)S(1)} %all_to_all.25), channel_id=1, source_target_pairs={{0,1},{1,0},{2,3},{3,2},{4,5},{5,4},{6,7},{7,6},{8,9},{9,8},{10,11... | collective-permute-start | bytes 6291464 | tf_op jit(solution)/shard_map/ppermute | solution.py:231
  74.8 0.5 abs_reduce_fusion
  75.4 0.7 tell.1
  76.1 9.4 %all_to_all.26.told_ref = f32[8,24,128]{2,1,0:T(8,128)S(1)} all-to-all(f32[8,24,128]{2,1,0:T(8,128)} %tell.1), channel_id=1, replica_groups=mesh['y'=8,'z'=8,'x'=4,'c'=2] {'x','c'}, dimensions={0} | all-to-all | bytes 196608 | tf_op jit(solution)/shard_map/all_to_all | solution.py:242
  85.5 0.1 means.1
  85.6 0.8 fusion.3
  86.4 0.0 collective-permute-done.1
  86.4 2.2 %fusion.1 = f16[512,1024]{1,0:T(8,128)(2,1)S(1)} fusion(f32[512,1024,1]{1,0,2:T(8,128)S(1)} %fusion.3, bf16[64,2,8,1024]{3,2,1,0:T(8,128)(2,1)} %collective-permute-done.1, f32[]{:T(128)S(1)} %bitcast.44, f32[1024]{0:T(1024)S(1)} %bitcast.40, f32[512]{0:T(512)S(1)} %bitcast.43), kind=kOutput, calls=%fused_computation.3 | convolution fusion | flops 540803072 | bytes 4724740 | tf_op jit(solution)/shard_map/dot_general | solution.py:203
  88.6 0.0 copy-start
  88.6 16.5 %all_to_all.27 = f16[4,128,1024]{2,1,0:T(8,128)(2,1)S(1)} all-to-all(f16[4,128,1024]{2,1,0:T(8,128)(2,1)S(1)} %bitcast.45), channel_id=1, replica_groups=mesh['y'=8,'z'=8,'x'=4,'c'=2] {'x'}, dimensions={0} | all-to-all | bytes 2097152 | tf_op jit(solution)/shard_map/all_to_all | solution.py:265
  105.2 0.3 convert_reduce_fusion.sum_ref
  105.5 7.9 %collective-permute-start.2 = (f16[128,1024]{1,0:T(8,128)(2,1)S(1)}, f16[128,1024]{1,0:T(8,128)(2,1)S(1)}, u32[]{:S(2)}, u32[]{:S(2)}) collective-permute-start(f16[128,1024]{1,0:T(8,128)(2,1)S(1)} %convert_element_type.88), channel_id=1, source_target_pairs={{0,0},{1,32},{2,8},{3,56},{4,16},{5,48},{6,24},{7,40},{8,10},{9,42... | collective-permute-start | bytes 786440 | tf_op jit(solution)/shard_map/ppermute | solution.py:291
  113.4 0.0 copy-done
  113.4 0.6 dynamic_slice.6
  114.7 0.1 multiply_reduce_fusion
  114.8 0.1 reshape.43
  114.9 1.0 block_stats.1
  115.9 4.9 %all-to-all-start.3 = ((f32[64,2,128]{2,1,0:T(2,128)}), f32[64,2,128]{2,1,0:T(2,128)S(1)}, u32[]{:S(2)}, u32[]{:S(2)}) async-start(f32[64,2,128]{2,1,0:T(2,128)} %block_stats.1), calls=%async_computation.3 | async-start | bytes 131072 | tf_op jit(solution)/shard_map/all_to_all | solution.py:285
  120.8 7.5 %collective-permute-start = (f32[16,128]{1,0:T(8,128)S(1)}, f32[16,128]{1,0:T(8,128)S(1)}, u32[]{:S(2)}, u32[]{:S(2)}) collective-permute-start(f32[16,128]{1,0:T(8,128)S(1)} %get-tuple-element.10.carried_ref), channel_id=1, source_target_pairs={{0,0},{1,32},{2,8},{3,56},{4,16},{5,48},{6,24},{7,40},{8,10},{9,42... | collective-permute-start | bytes 24584 | tf_op jit(solution)/shard_map/ppermute | solution.py:292
  128.3 2.5 %all-to-all-done.3.seen_ref = f32[64,2,128]{2,1,0:T(2,128)S(1)} async-done(((f32[64,2,128]{2,1,0:T(2,128)}), f32[64,2,128]{2,1,0:T(2,128)S(1)}, u32[]{:S(2)}, u32[]{:S(2)}) %all-to-all-start.3) | async-done | bytes 65568 | tf_op jit(solution)/shard_map/all_to_all | solution.py:285
  130.9 0.9 middle_stats.1
  131.8 6.6 %all-to-all-start.4 = ((f32[8,1,128]{2,1,0:T(1,128)}), f32[8,1,128]{2,1,0:T(1,128)S(1)}, u32[]{:S(2)}, u32[]{:S(2)}) async-start(f32[8,1,128]{2,1,0:T(1,128)} %middle_stats.1), calls=%async_computation.4 | async-start | bytes 8192 | tf_op jit(solution)/shard_map/all_to_all | solution.py:300
  138.4 0.0 collective-permute-done.2
  138.4 0.0 collective-permute-done.carried_ref
  138.4 6.4 %all-to-all-done.4.totals_ref = f32[8,1,128]{2,1,0:T(1,128)S(1)} async-done(((f32[8,1,128]{2,1,0:T(1,128)}), f32[8,1,128]{2,1,0:T(1,128)S(1)}, u32[]{:S(2)}, u32[]{:S(2)}) %all-to-all-start.4) | async-done | bytes 4128 | tf_op jit(solution)/shard_map/all_to_all | solution.py:300
  144.8 1.1 shrink.1
  (5 shorter events, 0.1 us)
Async XLA Ops:
  68.6 17.8 %collective-permute-start.1 = (bf16[64,2,8,1024]{3,2,1,0:T(8,128)(2,1)S(1)}, bf16[64,2,8,1024]{3,2,1,0:T(8,128)(2,1)}, u32[]{:S(2)}, u32[]{:S(2)}) collective-permute-start(bf16[64,2,8,1024]{3,2,1,0:T(8,128)(2,1)S(1)} %all_to_all.25), channel_id=1, source_target_pairs={{0,1},{1,0},{2,3},{3,2},{4,5},{5,4},{6,7},{7,6},{8,9},{9,8},{10,11... | collective-permute-start | bytes 6291464 | tf_op jit(solution)/shard_map/ppermute | solution.py:231
  88.6 24.7 %copy-start = (s32[8]{0:T(128)S(1)}, s32[8]{0:T(128)}, u32[]{:S(2)}) copy-start(s32[8]{0:T(128)} %constant.67.clone) | copy-start | bytes 100
  105.5 32.9 %collective-permute-start.2 = (f16[128,1024]{1,0:T(8,128)(2,1)S(1)}, f16[128,1024]{1,0:T(8,128)(2,1)S(1)}, u32[]{:S(2)}, u32[]{:S(2)}) collective-permute-start(f16[128,1024]{1,0:T(8,128)(2,1)S(1)} %convert_element_type.88), channel_id=1, source_target_pairs={{0,0},{1,32},{2,8},{3,56},{4,16},{5,48},{6,24},{7,40},{8,10},{9,42... | collective-permute-start | bytes 786440 | tf_op jit(solution)/shard_map/ppermute | solution.py:291
  115.9 15.0 %all-to-all-start.3 = ((f32[64,2,128]{2,1,0:T(2,128)}), f32[64,2,128]{2,1,0:T(2,128)S(1)}, u32[]{:S(2)}, u32[]{:S(2)}) async-start(f32[64,2,128]{2,1,0:T(2,128)} %block_stats.1), calls=%async_computation.3 | async-start | bytes 131072 | tf_op jit(solution)/shard_map/all_to_all | solution.py:285
  120.8 17.7 %collective-permute-start = (f32[16,128]{1,0:T(8,128)S(1)}, f32[16,128]{1,0:T(8,128)S(1)}, u32[]{:S(2)}, u32[]{:S(2)}) collective-permute-start(f32[16,128]{1,0:T(8,128)S(1)} %get-tuple-element.10.carried_ref), channel_id=1, source_target_pairs={{0,0},{1,32},{2,8},{3,56},{4,16},{5,48},{6,24},{7,40},{8,10},{9,42... | collective-permute-start | bytes 24584 | tf_op jit(solution)/shard_map/ppermute | solution.py:292
  131.8 13.1 %all-to-all-start.4 = ((f32[8,1,128]{2,1,0:T(1,128)}), f32[8,1,128]{2,1,0:T(1,128)S(1)}, u32[]{:S(2)}, u32[]{:S(2)}) async-start(f32[8,1,128]{2,1,0:T(1,128)} %middle_stats.1), calls=%async_computation.4 | async-start | bytes 8192 | tf_op jit(solution)/shard_map/all_to_all | solution.py:300

commit v12 on v10

--- a/solution.py
+++ b/solution.py
@@ -134,7 +134,7 @@
     seen = seen_ref[...]
     slot = lax.broadcasted_iota(jnp.int32, (1, 1, LANES), 2)
     values, flags = seen[:, 0:1, :], seen[:, 1:2, :]
-    norms = jnp.sum(values.reshape(NZ, NF, 1, LANES), axis=0)
+    norms = jnp.sum(values.reshape(NZ, NX, 1, LANES), axis=0)
     norms = jnp.where(slot < OFF, norms, 0.0)
     total = jnp.sum(values, axis=0)
     is_mean = slot == MEANS
@@ -142,7 +142,7 @@
     def lanes(row):
         return jnp.sum(row, axis=1, keepdims=True)
 
-    mean = lanes(jnp.where(is_mean[0], total, 0.0)) / NF
+    mean = lanes(jnp.where(is_mean[0], total, 0.0)) / NX
     apart = jnp.where(is_mean, (values - mean[None]) * flags, 0.0)
     between = lanes(jnp.sum(apart * apart, axis=0))
     second = lanes(jnp.where(slot[0] == SECOND, total, 0.0)) + width * between
@@ -170,7 +170,7 @@
     mu_scale = pick(sums, 0) / (rows * factors)
     apart = totals - mu_scale[None]
     from_mu = pick(jnp.sum(apart * apart, axis=0), 3)
-    spread = (pick(sums, 2) + pick(sums, 4) + block * from_mu) / factors
+    spread = (pick(sums, 2) + pick(sums, 4) + NX * width * from_mu) / factors
     norm_sq = factors * (spread + mu_scale * mu_scale)
     beta_value = (pick(sums, 1) / rows - norm_sq) / (factors * rows)
     shrinkage = beta_value / spread
@@ -269,13 +269,13 @@
     first = jnp.where(y_idx == column, (z_idx + shift) % NZ * width, never)
     message = pl.pallas_call(
         block_kernel,
-        out_shape=pltpu.VMEM((NZ * NF, 2, LANES), F32),
+        out_shape=pltpu.VMEM((NZ * NX, 2, LANES), F32),
         in_specs=[IN_SMEM, IN_VMEM, IN_VMEM, IN_VMEM],
         out_specs=IN_VMEM,
         name="block_stats",
     )(first.reshape(1), in_vmem(summed), in_vmem(norms), in_vmem(carried))
 
-    seen = exchange(message, SLAB)
+    seen = exchange(message, ("z", "x"))
 
     def owner(z, f):
         return ((z + SHIFT[f]) % NZ) * NF + COLUMN[z]
@@ -285,12 +285,12 @@
     carried = lax.ppermute(carried, SLAB, moves)
     second = pl.pallas_call(
         functools.partial(middle_kernel, width=width),
-        out_shape=pltpu.VMEM((NY, 1, LANES), F32),
+        out_shape=pltpu.VMEM((NY * NC, 1, LANES), F32),
         in_specs=[IN_VMEM],
         out_specs=IN_VMEM,
         name="middle_stats",
     )(in_vmem(seen))
-    totals = exchange(second, "y")
+    totals = exchange(second, ("y", "c"))
 
     first_own = jnp.where(y_idx == f_idx, z_idx * width, never)
     shrunk, shrinkage, col_mean = pl.pallas_call(

time: 149 us -> 150 us (level)
  blocking collectives: 91.4 us -> 103 us
  starting transfers between devices: 33.4 us -> 26.4 us
  waiting for transfers between devices: 8.96 us -> 5.8 us
    all_to_all x0 -> x1, blocking collectives: none -> 11.6 us  [shrinkage_step(): seen = exchange(message, ('z', 'x'))]
    all_to_all x2 -> x1, waiting for transfers between devices: 8.96 us -> 0.01 us  [shrinkage_step(): totals = exchange(second, ('y', 'c'))]
    ppermute x1, waiting for transfers between devices: 0.01 us -> 5.8 us  [shrinkage_step(): carried = lax.ppermute(carried, SLAB, moves)]
    ppermute x1, starting transfers between devices: 7.55 us -> 2.42 us  [shrinkage_step(): carried = lax.ppermute(carried, SLAB, moves)]
    all_to_all x2 -> x1, starting transfers between devices: 11.4 us -> 9.59 us  [shrinkage_step(): totals = exchange(second, ('y', 'c'))]
  transfers between devices with their start and end apart: 5 -> 4, of which waited for: 2 -> 1; matrix products, arithmetic and copies ran while one was open for 4% -> 4% of each run, Pallas kernels for 2% -> 1%
where the time goes in v12:
time: 150 us; the launch traced here: 149 us
  blocking collectives  103 us (69%)
  starting transfers between devices  26.4 us (18%)
  waiting for transfers between devices  5.8 us (4%)
  Pallas kernels  4.27 us (3%)
  other arithmetic  3.46 us (2%)
  matrix products  2.98 us (2%)
    all_to_all x1, blocking collectives, shrinkage_step(): arrived = exchange(dealt, PLANE)  65.5 us
    all_to_all x1, blocking collectives, shrinkage_step(): pieces = exchange(parcel.reshape(NX, width, block), 'x')  16.5 us
    all_to_all x1, blocking collectives, shrinkage_step(): seen = exchange(message, ('z', 'x'))  11.6 us
    all_to_all x1, starting transfers between devices, shrinkage_step(): totals = exchange(second, ('y', 'c'))  9.59 us
    all_to_all x1, blocking collectives, shrinkage_step(): told = exchange(told, LINE)  9.39 us
    ppermute x1, starting transfers between devices, shrinkage_step(): owned = lax.ppermute(summed.astype(F16), SLAB, moves).astype(F32)  8.21 us
    ppermute x1, starting transfers between devices, shrinkage_step(): swapped = lax.ppermute(arrived, 'c', flip(NC))  6.21 us
    ppermute x1, waiting for transfers between devices, shrinkage_step(): carried = lax.ppermute(carried, SLAB, moves)  5.8 us
  transfers between devices with their start and end apart: 4, of which 1 were waited for; matrix products, arithmetic and copies ran while one was open for 4% of the time, Pallas kernels for 1%

profile of v12, /device:TPU:1, one launch (start us, length us, event | category | flops | bytes accessed | tf_op | source)
XLA Modules:
  0.0 148.9 jit_solution(14674256129875230824)
XLA Ops:
  0.6 1.1 deal.1
  1.8 65.5 %all_to_all.25 = bf16[64,2,8,1024]{3,2,1,0:T(8,128)(2,1)} all-to-all(bf16[64,2,8,1024]{3,2,1,0:T(8,128)(2,1)S(1)} %deal.1), channel_id=1, replica_groups=mesh['y'=8,'z'=8,'x'=4,'c'=2] {'y','z'}, dimensions={0} | all-to-all | bytes 4194304 | tf_op jit(solution)/shard_map/all_to_all | solution.py:222
  67.3 0.8 slice.28
  68.0 6.2 %collective-permute-start.1 = (bf16[64,2,8,1024]{3,2,1,0:T(8,128)(2,1)}, bf16[64,2,8,1024]{3,2,1,0:T(8,128)(2,1)S(1)}, u32[]{:S(2)}, u32[]{:S(2)}) collective-permute-start(bf16[64,2,8,1024]{3,2,1,0:T(8,128)(2,1)} %all_to_all.25), channel_id=1, source_target_pairs={{0,1},{1,0},{2,3},{3,2},{4,5},{5,4},{6,7},{7,6},{8,9},{9,8},{10,11... | collective-permute-start | bytes 6291464 | tf_op jit(solution)/shard_map/ppermute | solution.py:224
  74.2 2.1 %abs_reduce_fusion = (f32[2,1024]{1,0:T(2,128)S(1)}, f32[2,1024]{1,0:T(2,128)S(1)}) fusion(f32[2,1024]{1,0:T(2,128)S(1)} %bitcast.46, bf16[64,2,8,1024]{3,2,1,0:T(8,128)(2,1)} %all_to_all.25), kind=kLoop, calls=%fused_computation | loop fusion | flops 5238784 | bytes 2121728 | tf_op jit(solution)/shard_map/reduce_max | solution.py:227
  76.4 0.7 tell.1
  77.1 9.4 %all_to_all.26.told_ref = f32[8,24,128]{2,1,0:T(8,128)S(1)} all-to-all(f32[8,24,128]{2,1,0:T(8,128)} %tell.1), channel_id=1, replica_groups=mesh['y'=8,'z'=8,'x'=4,'c'=2] {'x','c'}, dimensions={0} | all-to-all | bytes 196608 | tf_op jit(solution)/shard_map/all_to_all | solution.py:235
  86.5 0.1 means.1
  86.6 2.2 %fusion.3 = f32[512,1024,1]{1,0,2:T(8,128)S(1)} fusion(bf16[64,2,8,1024]{3,2,1,0:T(8,128)(2,1)} %all_to_all.25, f32[1024]{0:T(1024)S(1)} %bitcast.39, f32[512]{0:T(512)S(1)} %bitcast.42), kind=kOutput, calls=%fused_computation.9 | convolution fusion | flops 539230208 | bytes 3676160 | tf_op jit(solution)/shard_map/dot_general | solution.py:198
  88.8 0.0 collective-permute-done.1
  88.8 0.8 fusion.1
  89.6 0.0 copy-start
  89.6 16.5 %all_to_all.27 = f16[4,128,1024]{2,1,0:T(8,128)(2,1)S(1)} all-to-all(f16[4,128,1024]{2,1,0:T(8,128)(2,1)S(1)} %bitcast.45), channel_id=1, replica_groups=mesh['y'=8,'z'=8,'x'=4,'c'=2] {'x'}, dimensions={0} | all-to-all | bytes 2097152 | tf_op jit(solution)/shard_map/all_to_all | solution.py:258
  106.2 0.3 convert_reduce_fusion.sum_ref
  106.5 8.2 %collective-permute-start.2 = (f16[128,1024]{1,0:T(8,128)(2,1)S(1)}, f16[128,1024]{1,0:T(8,128)(2,1)S(1)}, u32[]{:S(2)}, u32[]{:S(2)}) collective-permute-start(f16[128,1024]{1,0:T(8,128)(2,1)S(1)} %convert_element_type.88), channel_id=1, source_target_pairs={{0,0},{1,32},{2,8},{3,56},{4,16},{5,48},{6,24},{7,40},{8,10},{9,42... | collective-permute-start | bytes 786440 | tf_op jit(solution)/shard_map/ppermute | solution.py:284
  114.7 0.0 copy-done
  114.7 0.6 dynamic_slice.6
  116.0 1.0 multiply_reduce_fusion
  117.0 0.1 reshape.43
  117.1 0.3 block_stats.1
  117.5 11.6 %all_to_all.28.seen_ref = f32[32,2,128]{2,1,0:T(2,128)S(1)} all-to-all(f32[32,2,128]{2,1,0:T(2,128)S(1)} %block_stats.1), channel_id=1, replica_groups=mesh['y'=8,'z'=8,'x'=4,'c'=2] {'z','x'}, dimensions={0} | all-to-all | bytes 65536 | tf_op jit(solution)/shard_map/all_to_all | solution.py:278
  129.1 0.8 middle_stats.1
  129.9 9.6 %all-to-all-start.4 = ((f32[16,1,128]{2,1,0:T(1,128)}), f32[16,1,128]{2,1,0:T(1,128)S(1)}, u32[]{:S(2)}, u32[]{:S(2)}) async-start(f32[16,1,128]{2,1,0:T(1,128)} %middle_stats.1), calls=%async_computation.4 | async-start | bytes 16384 | tf_op jit(solution)/shard_map/all_to_all | solution.py:293
  139.5 2.4 %collective-permute-start = (f32[16,128]{1,0:T(8,128)S(1)}, f32[16,128]{1,0:T(8,128)S(1)}, u32[]{:S(2)}, u32[]{:S(2)}) collective-permute-start(f32[16,128]{1,0:T(8,128)S(1)} %get-tuple-element.10.carried_ref), channel_id=1, source_target_pairs={{0,0},{1,32},{2,8},{3,56},{4,16},{5,48},{6,24},{7,40},{8,10},{9,42... | collective-permute-start | bytes 24584 | tf_op jit(solution)/shard_map/ppermute | solution.py:285
  141.9 0.0 collective-permute-done.2
  142.0 5.8 %collective-permute-done.carried_ref = f32[16,128]{1,0:T(8,128)S(1)} collective-permute-done((f32[16,128]{1,0:T(8,128)S(1)}, f32[16,128]{1,0:T(8,128)S(1)}, u32[]{:S(2)}, u32[]{:S(2)}) %collective-permute-start) | collective-permute-done | bytes 8224 | tf_op jit(solution)/shard_map/ppermute | solution.py:285
  147.8 0.0 all-to-all-done.4.totals_ref
  147.8 1.1 shrink.1
  (4 shorter events, 0.1 us)
Async XLA Ops:
  68.0 20.7 %collective-permute-start.1 = (bf16[64,2,8,1024]{3,2,1,0:T(8,128)(2,1)}, bf16[64,2,8,1024]{3,2,1,0:T(8,128)(2,1)S(1)}, u32[]{:S(2)}, u32[]{:S(2)}) collective-permute-start(bf16[64,2,8,1024]{3,2,1,0:T(8,128)(2,1)} %all_to_all.25), channel_id=1, source_target_pairs={{0,1},{1,0},{2,3},{3,2},{4,5},{5,4},{6,7},{7,6},{8,9},{9,8},{10,11... | collective-permute-start | bytes 6291464 | tf_op jit(solution)/shard_map/ppermute | solution.py:224
  89.6 25.1 %copy-start = (s32[8]{0:T(128)S(1)}, s32[8]{0:T(128)}, u32[]{:S(2)}) copy-start(s32[8]{0:T(128)} %constant.67.clone) | copy-start | bytes 100
  106.5 35.5 %collective-permute-start.2 = (f16[128,1024]{1,0:T(8,128)(2,1)S(1)}, f16[128,1024]{1,0:T(8,128)(2,1)S(1)}, u32[]{:S(2)}, u32[]{:S(2)}) collective-permute-start(f16[128,1024]{1,0:T(8,128)(2,1)S(1)} %convert_element_type.88), channel_id=1, source_target_pairs={{0,0},{1,32},{2,8},{3,56},{4,16},{5,48},{6,24},{7,40},{8,10},{9,42... | collective-permute-start | bytes 786440 | tf_op jit(solution)/shard_map/ppermute | solution.py:284
  129.9 17.9 %all-to-all-start.4 = ((f32[16,1,128]{2,1,0:T(1,128)}), f32[16,1,128]{2,1,0:T(1,128)S(1)}, u32[]{:S(2)}, u32[]{:S(2)}) async-start(f32[16,1,128]{2,1,0:T(1,128)} %middle_stats.1), calls=%async_computation.4 | async-start | bytes 16384 | tf_op jit(solution)/shard_map/all_to_all | solution.py:293
  139.5 8.3 %collective-permute-start = (f32[16,128]{1,0:T(8,128)S(1)}, f32[16,128]{1,0:T(8,128)S(1)}, u32[]{:S(2)}, u32[]{:S(2)}) collective-permute-start(f32[16,128]{1,0:T(8,128)S(1)} %get-tuple-element.10.carried_ref), channel_id=1, source_target_pairs={{0,0},{1,32},{2,8},{3,56},{4,16},{5,48},{6,24},{7,40},{8,10},{9,42... | collective-permute-start | bytes 24584 | tf_op jit(solution)/shard_map/ppermute | solution.py:285

commit v13 on v10

--- a/solution.py
+++ b/solution.py
@@ -47,20 +47,46 @@
         pl.when(core_ref[0] == core)(functools.partial(deal, core))
 
 
-def tell_kernel(core_ref, sums_ref, wide_ref, told_ref):
-    far = jnp.max(wide_ref[...], axis=1, keepdims=True)
-    far = 2.0 * jnp.max(far, axis=0, keepdims=True)
-    lines = [
-        sums_ref[part : part + 1, k * LANES : (k + 1) * LANES] for part in range(2) for k in range(NF)
-    ]
-    dealt = jnp.concatenate(lines[:NF], axis=0)
-    swapped = jnp.concatenate(lines[NX:NF] + lines[:NX], axis=0)
-    plain = jnp.where(core_ref[0] == 0, dealt, swapped)
-    out = jnp.concatenate(
-        [plain] + lines[NF:] + [jnp.broadcast_to(far, (8, LANES))], axis=0
-    )
-    for f in range(NF):
-        told_ref[f] = out
+def sums_kernel(core_ref, x_ref, told_ref, sum_ref, high_ref, low_ref):
+    step, steps = pl.program_id(0), pl.num_programs(0)
+    _, _, _, block = x_ref.shape
+
+    @pl.when(step == 0)
+    def _():
+        sum_ref[...] = jnp.zeros_like(sum_ref)
+        high_ref[...] = x_ref[0].astype(F32)
+        low_ref[...] = x_ref[0].astype(F32)
+
+    for part in range(2):
+        for k in range(block // LANES):
+            at = slice(k * LANES, (k + 1) * LANES)
+            value = x_ref[:, part, :, at]
+            sum_ref[part, :, at] += jnp.sum(value.astype(F32), axis=0)
+            high = jnp.max(value, axis=0).astype(F32)
+            low = jnp.min(value, axis=0).astype(F32)
+            high_ref[part, :, at] = jnp.maximum(high_ref[part, :, at], high)
+            low_ref[part, :, at] = jnp.minimum(low_ref[part, :, at], low)
+
+    @pl.when(step == steps - 1)
+    def _():
+        lines = []
+        far = jnp.zeros((1, LANES), F32)
+        for part in range(2):
+            for k in range(block // LANES):
+                at = slice(k * LANES, (k + 1) * LANES)
+                lines.append(jnp.sum(sum_ref[part, :, at], axis=0, keepdims=True))
+                high = jnp.max(high_ref[part, :, at], axis=0, keepdims=True)
+                low = jnp.min(low_ref[part, :, at], axis=0, keepdims=True)
+                far = jnp.maximum(far, high - low)
+        far = jnp.max(far, axis=1, keepdims=True)
+        dealt = jnp.concatenate(lines[:NF], axis=0)
+        swapped = jnp.concatenate(lines[NX:NF] + lines[:NX], axis=0)
+        plain = jnp.where(core_ref[0] == 0, dealt, swapped)
+        out = jnp.concatenate(
+            [plain] + lines[NF:] + [jnp.broadcast_to(far, (8, LANES))], axis=0
+        )
+        for f in range(NF):
+            told_ref[f] = out
 
 
 def means_kernel(core_ref, told_ref, half_ref, cols_ref, carried_ref, scale_ref, *, rows, held):
@@ -222,16 +248,17 @@
     arrived = exchange(dealt, PLANE)
 
     swapped = lax.ppermute(arrived, "c", flip(NC))
-    values = arrived.astype(F32)
-    sums = jnp.sum(values, axis=(0, 2))
-    wide = jnp.max(jnp.abs(values - values[:1, :, :1]), axis=(0, 2))
+    steps = 4
+    packet = (plane // steps, 2, row_count, block)
     told = pl.pallas_call(
-        tell_kernel,
+        sums_kernel,
+        grid=(steps,),
         out_shape=shapes((NF, 3 * NF, LANES), F32),
-        in_specs=[IN_SMEM, IN_VMEM, IN_VMEM],
-        out_specs=IN_VMEM,
-        name="tell",
-    )(core, in_vmem(sums), in_vmem(wide))
+        in_specs=[IN_SMEM, pl.BlockSpec(packet, lambda i: (i, 0, 0, 0))],
+        out_specs=pl.BlockSpec((NF, 3 * NF, LANES), lambda i: (0, 0, 0)),
+        scratch_shapes=[pltpu.VMEM((2, row_count, block), F32)] * 3,
+        name="sums",
+    )(core, arrived)
     told = exchange(told, LINE)
     mean_half, mean_c, carried, scale = pl.pallas_call(
         functools.partial(means_kernel, rows=total_rows, held=part_rows),

time: 149 us -> 149 us (level)
  Pallas kernels: 4.94 us -> 7.77 us
  other arithmetic: 3.46 us -> 1.35 us
    pallas_call x1, Pallas kernels: 0.74 us -> 3.57 us  [shrinkage_step(): pl.pallas_call(sums_kernel, grid=(steps,), out_shape=shapes((NF, 3 * NF,...]
    reduce_max x1 -> x0, other arithmetic: 2.11 us -> none  [shrinkage_step(): wide = jnp.max(jnp.abs(values - values[:1, :, :1]), axis=(0, 2))]
  transfers between devices with their start and end apart: 5 -> 5, of which waited for: 2 -> 2; matrix products, arithmetic and copies ran while one was open for 4% -> 3% of each run, Pallas kernels for 2% -> 4%
where the time goes in v13:
time: 149 us; the launch traced here: 148 us
  blocking collectives  91.4 us (61%)
  starting transfers between devices  33.4 us (22%)
  waiting for transfers between devices  8.96 us (6%)
  Pallas kernels  7.77 us (5%)
  matrix products  2.98 us (2%)
    all_to_all x1, blocking collectives, shrinkage_step(): arrived = exchange(dealt, PLANE)  65.5 us
    all_to_all x1, blocking collectives, shrinkage_step(): pieces = exchange(parcel.reshape(NX, width, block), 'x')  16.5 us
    all_to_all x1, blocking collectives, shrinkage_step(): told = exchange(told, LINE)  9.39 us
    ppermute x1, starting transfers between devices, shrinkage_step(): owned = lax.ppermute(summed.astype(F16), SLAB, moves).astype(F32)  8.21 us
    ppermute x1, starting transfers between devices, shrinkage_step(): carried = lax.ppermute(carried, SLAB, moves)  7.55 us
    all_to_all x1, starting transfers between devices, shrinkage_step(): totals = exchange(second, 'y')  6.51 us
    all_to_all x1, waiting for transfers between devices, shrinkage_step(): totals = exchange(second, 'y')  6.42 us
    ppermute x1, starting transfers between devices, shrinkage_step(): swapped = lax.ppermute(arrived, 'c', flip(NC))  6.2 us
  transfers between devices with their start and end apart: 5, of which 2 were waited for; matrix products, arithmetic and copies ran while one was open for 3% of the time, Pallas kernels for 4%

profile of v13, /device:TPU:1, one launch (start us, length us, event | category | flops | bytes accessed | tf_op | source)
XLA Modules:
  0.0 148.0 jit_solution(14603158121856603583)
XLA Ops:
  0.6 1.1 deal.1
  1.8 65.5 %all_to_all.25.x_ref = bf16[64,2,8,1024]{3,2,1,0:T(8,128)(2,1)} all-to-all(bf16[64,2,8,1024]{3,2,1,0:T(8,128)(2,1)S(1)} %deal.1), channel_id=1, replica_groups=mesh['y'=8,'z'=8,'x'=4,'c'=2] {'y','z'}, dimensions={0} | all-to-all | bytes 4194304 | tf_op jit(solution)/shard_map/all_to_all | solution.py:248
  67.3 6.2 %collective-permute-start.1 = (bf16[64,2,8,1024]{3,2,1,0:T(8,128)(2,1)}, bf16[64,2,8,1024]{3,2,1,0:T(8,128)(2,1)S(1)}, u32[]{:S(2)}, u32[]{:S(2)}) collective-permute-start(bf16[64,2,8,1024]{3,2,1,0:T(8,128)(2,1)} %all_to_all.25.x_ref), channel_id=1, source_target_pairs={{0,1},{1,0},{2,3},{3,2},{4,5},{5,4},{6,7},{7,6},{8,9},{9,8},{10,11... | collective-permute-start | bytes 6291464 | tf_op jit(solution)/shard_map/ppermute | solution.py:250
  73.5 3.6 %sums.1 = f32[8,24,128]{2,1,0:T(8,128)} custom-call(s32[1]{0:T(128)} %bitcast.1.core_ref, bf16[64,2,8,1024]{3,2,1,0:T(8,128)(2,1)} %all_to_all.25.x_ref), custom_call_target="tpu_custom_call" | custom-call | tf_op jit(solution)/shard_map/sums/pallas_call | solution.py:253
  77.0 9.4 %all_to_all.26.told_ref = f32[8,24,128]{2,1,0:T(8,128)S(1)} all-to-all(f32[8,24,128]{2,1,0:T(8,128)} %sums.1), channel_id=1, replica_groups=mesh['y'=8,'z'=8,'x'=4,'c'=2] {'x','c'}, dimensions={0} | all-to-all | bytes 196608 | tf_op jit(solution)/shard_map/all_to_all | solution.py:262
  86.4 0.1 means.1
  86.5 2.2 %fusion.3 = f32[512,1024,1]{1,0,2:T(8,128)S(1)} fusion(bf16[64,2,8,1024]{3,2,1,0:T(8,128)(2,1)} %all_to_all.25.x_ref, f32[1024]{0:T(1024)S(1)} %bitcast.36, f32[512]{0:T(512)S(1)} %bitcast.39), kind=kOutput, calls=%fused_computation.7 | convolution fusion | flops 539230208 | bytes 3676160 | tf_op jit(solution)/shard_map/dot_general | solution.py:224
  88.7 0.0 collective-permute-done.1
  88.7 0.8 fusion.1
  89.5 0.0 copy-start
  89.6 16.5 %all_to_all.27 = f16[4,128,1024]{2,1,0:T(8,128)(2,1)S(1)} all-to-all(f16[4,128,1024]{2,1,0:T(8,128)(2,1)S(1)} %bitcast.42), channel_id=1, replica_groups=mesh['y'=8,'z'=8,'x'=4,'c'=2] {'x'}, dimensions={0} | all-to-all | bytes 2097152 | tf_op jit(solution)/shard_map/all_to_all | solution.py:285
  106.1 0.3 convert_reduce_fusion.sum_ref
  106.4 8.2 %collective-permute-start.2 = (f16[128,1024]{1,0:T(8,128)(2,1)S(1)}, f16[128,1024]{1,0:T(8,128)(2,1)S(1)}, u32[]{:S(2)}, u32[]{:S(2)}) collective-permute-start(f16[128,1024]{1,0:T(8,128)(2,1)S(1)} %convert_element_type.84), channel_id=1, source_target_pairs={{0,0},{1,32},{2,8},{3,56},{4,16},{5,48},{6,24},{7,40},{8,10},{9,42... | collective-permute-start | bytes 786440 | tf_op jit(solution)/shard_map/ppermute | solution.py:311
  114.6 0.0 copy-done
  114.6 0.6 dynamic_slice.6
  115.9 1.0 multiply_reduce_fusion
  117.0 0.1 reshape.43
  117.1 1.0 block_stats.1
  118.0 4.9 %all-to-all-start.3 = ((f32[64,2,128]{2,1,0:T(2,128)}), f32[64,2,128]{2,1,0:T(2,128)S(1)}, u32[]{:S(2)}, u32[]{:S(2)}) async-start(f32[64,2,128]{2,1,0:T(2,128)} %block_stats.1), calls=%async_computation.3 | async-start | bytes 131072 | tf_op jit(solution)/shard_map/all_to_all | solution.py:305
  122.9 7.5 %collective-permute-start = (f32[16,128]{1,0:T(8,128)S(1)}, f32[16,128]{1,0:T(8,128)S(1)}, u32[]{:S(2)}, u32[]{:S(2)}) collective-permute-start(f32[16,128]{1,0:T(8,128)S(1)} %get-tuple-element.10.carried_ref), channel_id=1, source_target_pairs={{0,0},{1,32},{2,8},{3,56},{4,16},{5,48},{6,24},{7,40},{8,10},{9,42... | collective-permute-start | bytes 24584 | tf_op jit(solution)/shard_map/ppermute | solution.py:312
  130.5 2.5 %all-to-all-done.3.seen_ref = f32[64,2,128]{2,1,0:T(2,128)S(1)} async-done(((f32[64,2,128]{2,1,0:T(2,128)}), f32[64,2,128]{2,1,0:T(2,128)S(1)}, u32[]{:S(2)}, u32[]{:S(2)}) %all-to-all-start.3) | async-done | bytes 65568 | tf_op jit(solution)/shard_map/all_to_all | solution.py:305
  133.0 0.9 middle_stats.1
  133.9 6.5 %all-to-all-start.4 = ((f32[8,1,128]{2,1,0:T(1,128)}), f32[8,1,128]{2,1,0:T(1,128)S(1)}, u32[]{:S(2)}, u32[]{:S(2)}) async-start(f32[8,1,128]{2,1,0:T(1,128)} %middle_stats.1), calls=%async_computation.4 | async-start | bytes 8192 | tf_op jit(solution)/shard_map/all_to_all | solution.py:320
  140.4 0.0 collective-permute-done.2
  140.5 0.0 collective-permute-done.carried_ref
  140.5 6.4 %all-to-all-done.4.totals_ref = f32[8,1,128]{2,1,0:T(1,128)S(1)} async-done(((f32[8,1,128]{2,1,0:T(1,128)}), f32[8,1,128]{2,1,0:T(1,128)S(1)}, u32[]{:S(2)}, u32[]{:S(2)}) %all-to-all-start.4) | async-done | bytes 4128 | tf_op jit(solution)/shard_map/all_to_all | solution.py:320
  146.9 1.1 shrink.1
  (3 shorter events, 0.1 us)
Async XLA Ops:
  67.3 21.4 %collective-permute-start.1 = (bf16[64,2,8,1024]{3,2,1,0:T(8,128)(2,1)}, bf16[64,2,8,1024]{3,2,1,0:T(8,128)(2,1)S(1)}, u32[]{:S(2)}, u32[]{:S(2)}) collective-permute-start(bf16[64,2,8,1024]{3,2,1,0:T(8,128)(2,1)} %all_to_all.25.x_ref), channel_id=1, source_target_pairs={{0,1},{1,0},{2,3},{3,2},{4,5},{5,4},{6,7},{7,6},{8,9},{9,8},{10,11... | collective-permute-start | bytes 6291464 | tf_op jit(solution)/shard_map/ppermute | solution.py:250
  89.5 25.1 %copy-start = (s32[8]{0:T(128)S(1)}, s32[8]{0:T(128)}, u32[]{:S(2)}) copy-start(s32[8]{0:T(128)} %constant.65.clone) | copy-start | bytes 100
  106.4 34.0 %collective-permute-start.2 = (f16[128,1024]{1,0:T(8,128)(2,1)S(1)}, f16[128,1024]{1,0:T(8,128)(2,1)S(1)}, u32[]{:S(2)}, u32[]{:S(2)}) collective-permute-start(f16[128,1024]{1,0:T(8,128)(2,1)S(1)} %convert_element_type.84), channel_id=1, source_target_pairs={{0,0},{1,32},{2,8},{3,56},{4,16},{5,48},{6,24},{7,40},{8,10},{9,42... | collective-permute-start | bytes 786440 | tf_op jit(solution)/shard_map/ppermute | solution.py:311
  118.0 15.0 %all-to-all-start.3 = ((f32[64,2,128]{2,1,0:T(2,128)}), f32[64,2,128]{2,1,0:T(2,128)S(1)}, u32[]{:S(2)}, u32[]{:S(2)}) async-start(f32[64,2,128]{2,1,0:T(2,128)} %block_stats.1), calls=%async_computation.3 | async-start | bytes 131072 | tf_op jit(solution)/shard_map/all_to_all | solution.py:305
  122.9 17.6 %collective-permute-start = (f32[16,128]{1,0:T(8,128)S(1)}, f32[16,128]{1,0:T(8,128)S(1)}, u32[]{:S(2)}, u32[]{:S(2)}) collective-permute-start(f32[16,128]{1,0:T(8,128)S(1)} %get-tuple-element.10.carried_ref), channel_id=1, source_target_pairs={{0,0},{1,32},{2,8},{3,56},{4,16},{5,48},{6,24},{7,40},{8,10},{9,42... | collective-permute-start | bytes 24584 | tf_op jit(solution)/shard_map/ppermute | solution.py:312
  133.9 13.0 %all-to-all-start.4 = ((f32[8,1,128]{2,1,0:T(1,128)}), f32[8,1,128]{2,1,0:T(1,128)S(1)}, u32[]{:S(2)}, u32[]{:S(2)}) async-start(f32[8,1,128]{2,1,0:T(1,128)} %middle_stats.1), calls=%async_computation.4 | async-start | bytes 8192 | tf_op jit(solution)/shard_map/all_to_all | solution.py:320
